TPU v7x, 32 devices: a whole 2x2x4 slice. The times are simulated.
32 devices in a mesh: dp: 8 (over y, x, core), mp: 4 (over z).
Axes of the slice: x: 2, y: 2, z: 4, core: 2. Of those that a mesh axis runs over, the one named last changes fastest.
Arguments:
- tokens: bfloat16 [8192, 2048], P('dp'), may hold values from -6 to 6
- doc_lengths: int32 [8, 8], P('dp'), may hold values from 1 to 512, 1024 in all within a row
- slot_live: int32 [36], P('mp'), may hold values from 0 to 1, as said below
- attn_gain: bfloat16 [2048], replicated, may hold values from 0.5 to 1.5
- w_query: bfloat16 [2048, 1536], P(None, 'mp'), may hold values from -0.125 to 0.125
- w_keyval: bfloat16 [2048, 768], replicated, may hold values from -0.125 to 0.125
- q_gain: bfloat16 [64], replicated, may hold values from 0.099609375 to 1.8984375
- k_gain: bfloat16 [64], replicated, may hold values from 0.099609375 to 1.8984375
- w_out: bfloat16 [1536, 2048], P('mp'), may hold values from -0.625 to 0.625
- ffn_gain: bfloat16 [2048], replicated, may hold values from 0.5 to 1.5
- w_gate: bfloat16 [2048, 4608], P(None, 'mp'), may hold values from -0.125 to 0.125
- w_up: bfloat16 [2048, 4608], P(None, 'mp'), may hold values from -0.125 to 0.125
- w_down: bfloat16 [4608, 2048], P('mp'), may hold values from -0.09375 to 0.09375
- out_grad: bfloat16 [8192, 2048], P('dp'), may hold values from -6 to 6
Outputs:
- block_out: bfloat16 [8192, 2048], P(('dp', 'mp'))
- grad_tokens: float32 [8192, 2048], P(('dp', 'mp'))
- grad_attn_gain: float32 [2048], replicated
- grad_query: float32 [2048, 1536], P('dp', 'mp')
- grad_keyval: float32 [2048, 768], P(('dp', 'mp'))
- grad_q_gain: float32 [64], replicated
- grad_k_gain: float32 [64], replicated
- grad_out_proj: float32 [1536, 2048], P('mp', 'dp')
- grad_ffn_gain: float32 [2048], replicated
- grad_gate: float32 [2048, 4608], P('dp', 'mp')
- grad_up: float32 [2048, 4608], P('dp', 'mp')
- grad_down: float32 [4608, 2048], P('mp', 'dp')
Inputs may be any that keep to these rules, and one draw needn't show every extreme that they name: `doc_lengths`: each row's 8 lengths sum to 1024, and one of them is 512. `slot_live`: the 9 slots of each index of mp hold 34 // 4 or 34 // 4 + 1 live ones, 34 live in all; which slots and which indices hold more varies.
All inputs are finite; a program needn't handle non-finite values.
Results may differ from a plain program's by a relative error of at most 0.018.
Values may be sent and summed in bfloat16 or wider, within the bound.
A program may use at most 192 MiB of HBM per device.

v0:
```python
import math

import jax
import jax.numpy as jnp
from jax import lax
from jax.sharding import PartitionSpec as P

EPSILON = 1e-06
MASKED = -1000000000.0
ROPE_BASE = 10000.0
HIGHEST_PREC = lax.Precision.HIGHEST
CONTRACT_LAST = (((1,), (1,)), ((), ()))
CONTRACT_FIRST = (((0,), (0,)), ((), ()))


def normalize(raw_in):
    return raw_in * lax.rsqrt(jnp.mean(raw_in * raw_in, axis=-1, keepdims=True) + EPSILON)


def norm_back(grad_normed, raw_in, gain_vec):
    factor = lax.rsqrt(jnp.mean(raw_in * raw_in, axis=-1, keepdims=True) + EPSILON)
    unit_rows = raw_in * factor
    scaled = grad_normed * gain_vec
    grad_raw = factor * (scaled - unit_rows * jnp.mean(scaled * unit_rows, axis=-1, keepdims=True))
    return (grad_raw, jnp.sum(grad_normed * unit_rows, axis=tuple(range(raw_in.ndim - 1))))


def rotate(values, cosine_tab, sine_tab, sign):
    half_size = values.shape[-1] // 2
    first_half = values[..., :half_size]
    second_half = values[..., half_size:]
    return jnp.concatenate(
        [
            first_half * cosine_tab - sign * second_half * sine_tab,
            second_half * cosine_tab + sign * first_half * sine_tab,
        ],
        axis=-1,
    )


def doc_layout(lengths, row_count):
    doc_ends = jnp.cumsum(lengths)
    token_index = jnp.arange(row_count, dtype=jnp.int32)
    past_end = (token_index[:, None] >= doc_ends[None, :]).astype(jnp.int32)
    doc_id = jnp.sum(past_end, axis=1)
    doc_pos = token_index - jnp.sum(past_end * lengths[None, :], axis=1)
    return (doc_id, doc_pos, token_index)


def rope_table(doc_pos, head_size):
    rope_freq = jnp.exp(
        jnp.arange(head_size // 2, dtype=jnp.float32) * (-2.0 * math.log(ROPE_BASE) / head_size)
    )
    rope_angle = doc_pos.astype(jnp.float32)[:, None] * rope_freq[None, :]
    return (jnp.cos(rope_angle)[:, None, :], jnp.sin(rope_angle)[:, None, :])


def shards(
    tokens,
    doc_lengths,
    slot_live,
    attn_gain,
    w_query,
    w_keyval,
    q_gain,
    k_gain,
    w_out,
    ffn_gain,
    w_gate,
    w_up,
    w_down,
    out_grad,
):
    row_count, model_width = tokens.shape
    head_size = q_gain.shape[0]
    heads_dev = w_query.shape[1] // head_size
    heads_all = heads_dev * lax.axis_size("mp")
    kv_heads = w_keyval.shape[1] // (2 * head_size)
    group_size = heads_all // kv_heads
    kv_window = min(kv_heads, (heads_dev + group_size - 2) // group_size + 1)
    tile_cols = w_gate.shape[1] // slot_live.shape[0]
    shard_rows = row_count // lax.axis_size("mp")
    block_rows = min(512, row_count)
    score_scale = head_size ** (-0.5)
    head_span = heads_dev * head_size
    mp_index = lax.axis_index("mp")
    row_first = mp_index * shard_rows
    q_first = mp_index * heads_dev
    kv_first = jnp.minimum(q_first // group_size, kv_heads - kv_window)
    kv_owner = (q_first + jnp.arange(heads_dev, dtype=jnp.int32)) // group_size - kv_first
    head_pick = (kv_owner[:, None] == jnp.arange(kv_window, dtype=jnp.int32)[None, :]).astype(
        jnp.float32
    )
    key_cols = lax.dynamic_slice_in_dim(w_keyval, kv_first * head_size, kv_window * head_size, 1)
    value_cols = lax.dynamic_slice_in_dim(
        w_keyval, (kv_heads + kv_first) * head_size, kv_window * head_size, 1
    )

    def spread(window_cols):
        return (
            jnp.einsum(
                "dwe,hw->dhe",
                window_cols.reshape(model_width, kv_window, head_size),
                head_pick.astype(jnp.bfloat16),
                preferred_element_type=jnp.float32,
            )
            .astype(jnp.bfloat16)
            .reshape(model_width, head_span)
        )

    def fold_heads(per_head):
        return jnp.einsum(
            "dhe,hw->dwe",
            per_head.reshape(model_width, heads_dev, head_size),
            head_pick,
            precision=HIGHEST_PREC,
        ).reshape(model_width, kv_window * head_size)

    doc_id, doc_pos, token_index = doc_layout(doc_lengths[0], row_count)
    cosine_tab, sine_tab = rope_table(doc_pos, head_size)
    x_float = tokens.astype(jnp.float32)
    x_rows = lax.dynamic_slice_in_dim(x_float, row_first, shard_rows, 0)
    gain_one = attn_gain.astype(jnp.float32)
    gain_two = ffn_gain.astype(jnp.float32)
    q_gain_f = q_gain.astype(jnp.float32)
    k_gain_f = k_gain.astype(jnp.float32)
    xn_one = (normalize(x_float) * gain_one).astype(jnp.bfloat16)
    q_raw = jnp.dot(xn_one, w_query, preferred_element_type=jnp.float32).reshape(
        row_count, heads_dev, head_size
    )
    kv_raw = jnp.dot(
        xn_one, jnp.concatenate([key_cols, value_cols], axis=1), preferred_element_type=jnp.float32
    ).reshape(row_count, 2, kv_window, head_size)
    k_raw = jnp.einsum("twe,hw->the", kv_raw[:, 0], head_pick, precision=HIGHEST_PREC)
    v_raw = jnp.einsum("twe,hw->the", kv_raw[:, 1], head_pick, precision=HIGHEST_PREC)
    q_rot = rotate(normalize(q_raw) * q_gain_f, cosine_tab, sine_tab, 1.0).astype(jnp.bfloat16)
    k_rot = rotate(normalize(k_raw) * k_gain_f, cosine_tab, sine_tab, 1.0).astype(jnp.bfloat16)
    v_low = v_raw.astype(jnp.bfloat16)

    def block_scores(row_start, key_stop):
        scores = (
            jnp.einsum(
                "qhe,khe->hqk",
                q_rot[row_start : row_start + block_rows],
                k_rot[:key_stop],
                preferred_element_type=jnp.float32,
            )
            * score_scale
        )
        allowed = (doc_id[row_start : row_start + block_rows, None] == doc_id[None, :key_stop]) & (
            token_index[None, :key_stop] <= token_index[row_start : row_start + block_rows, None]
        )
        return jnp.where(allowed[None], scores, MASKED)

    block_outs = []
    block_lse = []
    for row_start in range(0, row_count, block_rows):
        key_stop = row_start + block_rows
        scores = block_scores(row_start, key_stop)
        row_max = jnp.max(scores, axis=-1, keepdims=True)
        shifted = jnp.exp(scores - row_max)
        row_total = jnp.sum(shifted, axis=-1, keepdims=True)
        attn_probs = (shifted / row_total).astype(jnp.bfloat16)
        block_outs.append(
            jnp.einsum(
                "hqk,khe->qhe", attn_probs, v_low[:key_stop], preferred_element_type=jnp.float32
            )
        )
        block_lse.append(row_max + jnp.log(row_total))
    attended = (
        jnp.concatenate(block_outs, axis=0).reshape(row_count, head_span).astype(jnp.bfloat16)
    )
    attn_part = jnp.dot(attended, w_out, preferred_element_type=jnp.float32)
    hidden_full = x_float + lax.psum(attn_part, "mp")
    hidden_rows = lax.dynamic_slice_in_dim(hidden_full, row_first, shard_rows, 0)
    xn_two = (normalize(hidden_full) * gain_two).astype(jnp.bfloat16)
    live_cols = jnp.repeat(slot_live.astype(jnp.float32), tile_cols)
    gate_act = jnp.dot(xn_two, w_gate, preferred_element_type=jnp.float32)
    up_act = jnp.dot(xn_two, w_up, preferred_element_type=jnp.float32)
    gate_sigmoid = jax.nn.sigmoid(gate_act)
    gate_silu = gate_act * gate_sigmoid
    ffn_hidden = (gate_silu * up_act * live_cols).astype(jnp.bfloat16)
    ffn_part = jnp.dot(ffn_hidden, w_down, preferred_element_type=jnp.float32)
    out_rows = hidden_rows + lax.psum_scatter(
        ffn_part.astype(jnp.bfloat16), "mp", scatter_dimension=0, tiled=True
    ).astype(jnp.float32)
    block_out = out_rows.astype(jnp.bfloat16)
    d_hidden = (
        lax.dot_general(out_grad, w_down, CONTRACT_LAST, preferred_element_type=jnp.float32)
        * live_cols
    )
    grad_down = lax.dot_general(
        ffn_hidden, out_grad, CONTRACT_FIRST, preferred_element_type=jnp.float32
    )
    d_gate = (d_hidden * up_act * gate_sigmoid * (1.0 + gate_act * (1.0 - gate_sigmoid))).astype(
        jnp.bfloat16
    )
    d_up = (d_hidden * gate_silu).astype(jnp.bfloat16)
    grad_gate = lax.dot_general(xn_two, d_gate, CONTRACT_FIRST, preferred_element_type=jnp.float32)
    grad_up = lax.dot_general(xn_two, d_up, CONTRACT_FIRST, preferred_element_type=jnp.float32)
    dn_two_part = lax.dot_general(
        d_gate, w_gate, CONTRACT_LAST, preferred_element_type=jnp.float32
    ) + lax.dot_general(d_up, w_up, CONTRACT_LAST, preferred_element_type=jnp.float32)
    dn_two = lax.psum(dn_two_part, "mp")
    back_two, _ = norm_back(dn_two, hidden_full, gain_two)
    dh_full = out_grad.astype(jnp.float32) + back_two
    dh_rows = lax.dynamic_slice_in_dim(dh_full, row_first, shard_rows, 0)
    grad_gain_two = jnp.sum(
        lax.dynamic_slice_in_dim(dn_two, row_first, shard_rows, 0) * normalize(hidden_rows), axis=0
    )
    dh_low = dh_full.astype(jnp.bfloat16)
    grad_out_proj = lax.dot_general(
        attended, dh_low, CONTRACT_FIRST, preferred_element_type=jnp.float32
    )
    d_att = lax.dot_general(dh_low, w_out, CONTRACT_LAST, preferred_element_type=jnp.float32)
    d_att = d_att.astype(jnp.bfloat16).reshape(row_count, heads_dev, head_size)
    dq_blocks = []
    d_keys = jnp.zeros((row_count, heads_dev, head_size), jnp.float32)
    d_values = jnp.zeros((row_count, heads_dev, head_size), jnp.float32)
    for block_index, row_start in enumerate(range(0, row_count, block_rows)):
        key_stop = row_start + block_rows
        scores = block_scores(row_start, key_stop)
        attn_probs = jnp.exp(scores - block_lse[block_index])
        probs_low = attn_probs.astype(jnp.bfloat16)
        att_rows = d_att[row_start:key_stop]
        d_probs = jnp.einsum(
            "qhe,khe->hqk", att_rows, v_low[:key_stop], preferred_element_type=jnp.float32
        )
        d_scores = (
            attn_probs * (d_probs - jnp.sum(d_probs * attn_probs, axis=-1, keepdims=True))
        ).astype(jnp.bfloat16)
        dq_blocks.append(
            jnp.einsum(
                "hqk,khe->qhe", d_scores, k_rot[:key_stop], preferred_element_type=jnp.float32
            )
            * score_scale
        )
        d_keys = d_keys.at[:key_stop].add(
            jnp.einsum(
                "hqk,qhe->khe",
                d_scores,
                q_rot[row_start:key_stop],
                preferred_element_type=jnp.float32,
            )
            * score_scale
        )
        d_values = d_values.at[:key_stop].add(
            jnp.einsum("hqk,qhe->khe", probs_low, att_rows, preferred_element_type=jnp.float32)
        )
    d_queries = jnp.concatenate(dq_blocks, axis=0)
    dq_raw, grad_q_gain = norm_back(rotate(d_queries, cosine_tab, sine_tab, -1.0), q_raw, q_gain_f)
    dk_raw, grad_k_gain = norm_back(rotate(d_keys, cosine_tab, sine_tab, -1.0), k_raw, k_gain_f)
    d_proj = jnp.concatenate(
        [
            dq_raw.reshape(row_count, head_span),
            dk_raw.reshape(row_count, head_span),
            d_values.reshape(row_count, head_span),
        ],
        axis=1,
    ).astype(jnp.bfloat16)
    w_proj = jnp.concatenate([w_query, spread(key_cols), spread(value_cols)], axis=1)
    dn_one_part = lax.dot_general(d_proj, w_proj, CONTRACT_LAST, preferred_element_type=jnp.float32)
    grad_proj = lax.dot_general(xn_one, d_proj, CONTRACT_FIRST, preferred_element_type=jnp.float32)
    grad_query = grad_proj[:, :head_span]
    grad_keyval = jnp.zeros((model_width, 2 * kv_heads * head_size), jnp.float32)
    grad_keyval = lax.dynamic_update_slice_in_dim(
        grad_keyval, fold_heads(grad_proj[:, head_span : 2 * head_span]), kv_first * head_size, 1
    )
    grad_keyval = lax.dynamic_update_slice_in_dim(
        grad_keyval, fold_heads(grad_proj[:, 2 * head_span :]), (kv_heads + kv_first) * head_size, 1
    )
    dn_one_rows = lax.psum_scatter(
        dn_one_part.astype(jnp.bfloat16), "mp", scatter_dimension=0, tiled=True
    ).astype(jnp.float32)
    back_one, grad_gain_one = norm_back(dn_one_rows, x_rows, gain_one)
    grad_tokens = dh_rows + back_one
    grad_query, grad_out_proj, grad_gate, grad_up, grad_down = (
        lax.psum_scatter(
            grad_query.astype(jnp.bfloat16), "dp", scatter_dimension=0, tiled=True
        ).astype(jnp.float32),
        lax.psum_scatter(
            grad_out_proj.astype(jnp.bfloat16), "dp", scatter_dimension=1, tiled=True
        ).astype(jnp.float32),
        lax.psum_scatter(
            grad_gate.astype(jnp.bfloat16), "dp", scatter_dimension=0, tiled=True
        ).astype(jnp.float32),
        lax.psum_scatter(
            grad_up.astype(jnp.bfloat16), "dp", scatter_dimension=0, tiled=True
        ).astype(jnp.float32),
        lax.psum_scatter(
            grad_down.astype(jnp.bfloat16), "dp", scatter_dimension=1, tiled=True
        ).astype(jnp.float32),
    )
    grad_keyval = lax.psum_scatter(grad_keyval, ("dp", "mp"), scatter_dimension=0, tiled=True)
    grad_gain_one, grad_gain_two, grad_q_gain, grad_k_gain = lax.psum(
        (grad_gain_one, grad_gain_two, grad_q_gain, grad_k_gain), ("dp", "mp")
    )
    return (
        block_out,
        grad_tokens,
        grad_gain_one,
        grad_query,
        grad_keyval,
        grad_q_gain,
        grad_k_gain,
        grad_out_proj,
        grad_gain_two,
        grad_gate,
        grad_up,
        grad_down,
    )


def solution(mesh):
    return jax.shard_map(
        shards,
        mesh=mesh,
        in_specs=(
            P("dp", None),
            P("dp", None),
            P("mp"),
            P(),
            P(None, "mp"),
            P(),
            P(),
            P(),
            P("mp", None),
            P(),
            P(None, "mp"),
            P(None, "mp"),
            P("mp", None),
            P("dp", None),
        ),
        out_specs=(
            P(("dp", "mp"), None),
            P(("dp", "mp"), None),
            P(),
            P("dp", "mp"),
            P(("dp", "mp"), None),
            P(),
            P(),
            P("mp", "dp"),
            P(),
            P("dp", "mp"),
            P("dp", "mp"),
            P("mp", "dp"),
        ),
        check_vma=False,
    )
```

profile of v0, /device:TPU:0, one launch (start us, length us, event | category | flops | bytes accessed | tf_op | source)
XLA Modules:
  0.0 1244.2 jit_solution(17080760547115743847)
XLA Ops:
  8.2 3.3 multiply_reduce_fusion.3
  11.6 3.5 fusion.103
  15.3 4.5 constant_dynamic-slice_fusion.1
  24.7 4.5 fusion.45
  34.5 2.9 fusion.58
  43.5 3.0 fusion
  48.0 3.6 fusion.68
  56.8 5.6 fusion.110
  63.2 292.8 %all-reduce.6.cloned.1.call-done = f32[1024,2048]{1,0:T(8,128)} async-done(((f32[1024,2048]{1,0:T(8,128)}), f32[1024,2048]{1,0:T(8,128)}) %all-reduce.6.cloned.1.call-update) | async-done | bytes 8388624 | tf_op jit(solution)/shard_map/psum | solution.py:174
  356.0 5.7 multiply_reduce_fusion.2
  364.9 11.4 fusion.111
  376.4 7.3 fusion.112
  383.7 12.7 %multiply_convert_fusion.4 = (bf16[1024,1152]{1,0:T(8,128)(2,1)S(1)}, bf16[1024,1152]{1,0:T(8,128)(2,1)}, bf16[1024,1152]{1,0:T(8,128)(2,1)}) fusion(f32[1024,1152]{1,0:T(8,128)} %fusion.111, f32[1024,1152]{1,0:T(8,128)} %fusion.112, f32[1152]{0:T(1024)S(1)} %broadcast_bitcast_fusion, bf16[1024,2048]{1,0:T(8,128)(2,1)S(1)} %copy-done.27, ...), kind=kOutput, calls=%fused_computation.36 | convolution fusion | flops 4851892224 | bytes 25432576 | tf_op jit(solution)/shard_map/dot_general | solution.py:189
  396.5 8.1 fusion.113
  404.6 8.5 convolution_add_fusion
  413.3 9.6 convolution_convert_fusion.2
  422.9 9.6 convolution_convert_fusion.1
  432.6 9.2 convolution_convert_fusion
  442.5 9.5 convolution_convert_fusion.3
  452.1 251.1 %all-reduce.8.cloned.1.call-done = f32[1024,2048]{1,0:T(8,128)} async-done(((f32[1024,2048]{1,0:T(8,128)}), f32[1024,2048]{1,0:T(8,128)}) %all-reduce.8.cloned.1.call-update) | async-done | bytes 8388624 | tf_op jit(solution)/shard_map/psum | solution.py:204
  703.2 6.9 multiply_reduce_fusion.1
  713.0 8.3 multiply_add_fusion
  721.3 5.3 fusion.55
  727.4 4.7 multiply_reduce_fusion.4
  732.1 4.8 multiply_convert_fusion.3
  739.6 2.9 fusion.62
  742.6 6.3 multiply_reduce_fusion
  748.9 6.9 multiply_convert_fusion
  768.8 5.3 fusion.73
  774.2 3.7 copy-done.14
  779.3 6.4 convolution_convert_fusion.6
  792.5 7.4 fusion.19
  800.1 5.2 fusion.104
  805.3 3.7 fusion.26
  811.8 5.7 fusion.29
  820.2 3.0 broadcast_in_dim.37
  823.2 11.5 dynamic_update_slice.6
  834.7 11.0 dynamic_update_slice.7
  845.8 6.5 convert_element_type.145
  860.3 13.2 %reduce-scatter.23.cloned.1.call-done = bf16[1152,256]{1,0:T(8,128)(2,1)} async-done(((bf16[1152,2048]{1,0:T(8,128)(2,1)}), bf16[1152,256]{1,0:T(8,128)(2,1)}) %reduce-scatter.23.cloned.1.call-update) | async-done | bytes 589840 | tf_op jit(solution)/shard_map/reduce_scatter | solution.py:290
  875.8 76.7 %reduce-scatter.9.cloned.1.call-done = bf16[256,2048]{1,0:T(8,128)(2,1)} async-done(((bf16[1024,2048]{1,0:T(8,128)(2,1)}), bf16[256,2048]{1,0:T(8,128)(2,1)}) %reduce-scatter.9.cloned.1.call-update) | async-done | bytes 1048592 | tf_op jit(solution)/shard_map/reduce_scatter | solution.py:184
  952.5 4.0 multiply_reduce_fusion.5
  956.6 38.2 %reduce-scatter.13.cloned.1.call-done = bf16[256,384]{0,1:T(8,128)(2,1)} async-done(((bf16[2048,384]{0,1:T(8,128)(2,1)}), bf16[256,384]{0,1:T(8,128)(2,1)}) %reduce-scatter.13.cloned.1.call-update) | async-done | bytes 196624 | tf_op jit(solution)/shard_map/reduce_scatter | solution.py:278
  996.5 39.9 %reduce-scatter.17.cloned.1.call-done = bf16[384,256]{1,0:T(8,128)(2,1)} async-done(((bf16[384,2048]{1,0:T(8,128)(2,1)}), bf16[384,256]{1,0:T(8,128)(2,1)}) %reduce-scatter.17.cloned.1.call-update) | async-done | bytes 196624 | tf_op jit(solution)/shard_map/reduce_scatter | solution.py:281
  1038.1 77.4 %reduce-scatter.11.cloned.1.call-done = bf16[256,2048]{1,0:T(8,128)(2,1)} async-done(((bf16[1024,2048]{1,0:T(8,128)(2,1)}), bf16[256,2048]{1,0:T(8,128)(2,1)}) %reduce-scatter.11.cloned.1.call-update) | async-done | bytes 1048592 | tf_op jit(solution)/shard_map/reduce_scatter | solution.py:272
  1118.2 41.1 %all-reduce.2 = (f32[2048]{0:T(1024)}, f32[64]{0:T(128)}, f32[64]{0:T(128)}, f32[2048]{0:T(1024)}) all-reduce(f32[2048]{0:T(1024)S(1)} %get-tuple-element.124, f32[64]{0:T(128)S(1)} %reduce_sum.217, f32[64]{0:T(128)S(1)} %get-tuple-element.126, f32[2048]{0:T(1024)S(1)} %get-tuple-element.141), channel_id=1, replica_groups=mesh['dp'=8,'mp'=4] {'dp','mp'}, use_global_device_ids=true, to_apply=%region_23.24 | all-reduce | flops 4224 | bytes 33792 | tf_op jit(solution)/shard_map/psum | solution.py:295
  1159.3 4.6 fusion.38
  1163.9 73.2 %reduce-scatter.15.cloned.1.call-done = f32[64,768]{1,0:T(8,128)} async-done(((f32[2048,768]{1,0:T(8,128)}), f32[64,768]{1,0:T(8,128)}) %reduce-scatter.15.cloned.1.call-update) | async-done | bytes 196624 | tf_op jit(solution)/shard_map/reduce_scatter | solution.py:294
  (265 shorter events, 78.3 us)
Async XLA Ops:
  7.2 49.6 %copy-start = (bf16[384,2048]{1,0:T(8,128)(2,1)S(1)}, bf16[384,2048]{1,0:T(8,128)(2,1)}, u32[]{:S(2)}) copy-start(bf16[384,2048]{1,0:T(8,128)(2,1)} %param.34) | copy-start | bytes 4718596
  7.2 348.8 %all-reduce.6.cloned.1.call-start = ((), (), s32[]{:S(2)}) async-start(), calls=%async_computation.8 | async-start | bytes 16777216 | tf_op jit(solution)/shard_map/psum | solution.py:174
  7.3 27.2 %copy-start.54 = (s32[6]{0:T(128)}, s32[6]{0:T(128)S(1)}, u32[]{:S(2)}) copy-start(s32[6]{0:T(128)S(1)} %fusion.88) | copy-start | bytes 76
  8.2 16.5 %copy-start.52 = (f32[2048]{0:T(1024)}, f32[2048]{0:T(1024)S(1)}, u32[]{:S(2)}) copy-start(f32[2048]{0:T(1024)S(1)} %convert_element_type.146) | copy-start | bytes 24580
  11.5 13.2 %copy-start.59 = (f32[1024]{0:T(1024)}, f32[1024]{0:T(1024)S(1)}, u32[]{:S(2)}) copy-start(f32[1024]{0:T(1024)S(1)} %add_rsqrt_fusion.3) | copy-start | bytes 12292
  11.6 27.6 %copy-start.61 = (f32[64]{0:T(128)}, f32[64]{0:T(128)S(1)}, u32[]{:S(2)}) copy-start(f32[64]{0:T(128)S(1)} %convert_element_type.151) | copy-start | bytes 772
  15.1 24.2 %copy-start.10 = (f32[1024,384]{0,1:T(8,128)}, f32[1024,384]{0,1:T(8,128)S(1)}, u32[]{:S(2)}) copy-start(f32[1024,384]{0,1:T(8,128)S(1)} %fusion.103) | copy-start | bytes 4718596
  15.3 23.9 %copy-start.45 = (f32[1024,6]{0,1:T(8,128)}, f32[1024,6]{0,1:T(8,128)S(1)}, u32[]{:S(2)}) copy-start(f32[1024,6]{0,1:T(8,128)S(1)} %add_rsqrt_fusion.1) | copy-start | bytes 73732
  15.3 23.9 %copy-start.56 = (f32[64]{0:T(128)}, f32[64]{0:T(128)S(1)}, u32[]{:S(2)}) copy-start(f32[64]{0:T(128)S(1)} %convert_element_type.153) | copy-start | bytes 772
  34.1 6.3 copy-start.47
  37.4 9.1 copy-start.23
  37.4 16.6 %copy-start.36 = (bf16[512,6,64]{0,1,2:T(8,128)(2,1)}, bf16[512,6,64]{0,1,2:T(8,128)(2,1)S(1)}, u32[]{:S(2)}) copy-start(bf16[512,6,64]{0,1,2:T(8,128)(2,1)S(1)} %slice.197) | copy-start | bytes 1179652
  41.0 10.9 copy-start.15
  41.0 10.9 copy-start.17
  41.0 10.9 copy-start.19
  41.0 10.9 copy-start.21
  62.5 640.7 %all-reduce.8.cloned.1.call-start = ((), (), s32[]{:S(2)}) async-start(), calls=%async_computation.10 | async-start | bytes 16777216 | tf_op jit(solution)/shard_map/psum | solution.py:204
  361.7 14.6 %slice-start.7 = ((s8[4718592]{0:T(1024)(128)(4,1)}), s8[524288]{0:T(1024)(128)(4,1)S(1)}, s32[]{:S(2)}) async-start(s8[4718592]{0:T(1024)(128)(4,1)} %bitcast.161), calls=%async_computation.25 | async-start | bytes 1048576
  364.9 11.4 copy-start.29
  364.9 11.4 slice-start.8
  376.3 7.4 copy-start.27
  376.4 20.1 %slice-start.5 = ((s8[4718592]{0:T(1024)(128)(4,1)}), s8[4194304]{0:T(1024)(128)(4,1)S(1)}, s32[]{:S(2)}) async-start(s8[4718592]{0:T(1024)(128)(4,1)} %bitcast.159), calls=%async_computation.23 | async-start | bytes 8388608
  376.4 28.3 %slice-start.9 = ((s8[4718592]{0:T(1024)(128)(4,1)}), s8[4194304]{0:T(1024)(128)(4,1)S(1)}, s32[]{:S(2)}) async-start(s8[4718592]{0:T(1024)(128)(4,1)} %bitcast.163), calls=%async_computation.27 | async-start | bytes 8388608
  383.7 12.7 %slice-start.6 = ((s8[4718592]{0:T(1024)(128)(4,1)}), s8[524288]{0:T(1024)(128)(4,1)S(1)}, s32[]{:S(2)}) async-start(s8[4718592]{0:T(1024)(128)(4,1)} %bitcast.159), calls=%async_computation.24 | async-start | bytes 1048576
  383.7 20.9 %slice-start.10 = ((s8[4718592]{0:T(1024)(128)(4,1)}), s8[524288]{0:T(1024)(128)(4,1)S(1)}, s32[]{:S(2)}) async-start(s8[4718592]{0:T(1024)(128)(4,1)} %bitcast.163), calls=%async_computation.28 | async-start | bytes 1048576
  396.5 8.2 copy-start.68
  413.2 442.8 %reduce-scatter.19.cloned.1.call-start = ((), (), s32[]{:S(2)}) async-start(), calls=%async_computation.15 | async-start | bytes 5308416 | tf_op jit(solution)/shard_map/reduce_scatter | solution.py:284
  422.9 435.3 %reduce-scatter.21.cloned.1.call-start = ((), (), s32[]{:S(2)}) async-start(), calls=%async_computation.16 | async-start | bytes 5308416 | tf_op jit(solution)/shard_map/reduce_scatter | solution.py:287
  432.5 441.0 %reduce-scatter.23.cloned.1.call-start = ((), (), s32[]{:S(2)}) async-start(), calls=%async_computation.17 | async-start | bytes 5308416 | tf_op jit(solution)/shard_map/reduce_scatter | solution.py:290
  441.8 510.8 %reduce-scatter.9.cloned.1.call-start = ((), (), s32[]{:S(2)}) async-start(), calls=%async_computation.9 | async-start | bytes 5242880 | tf_op jit(solution)/shard_map/reduce_scatter | solution.py:184
  442.5 284.9 %copy-start.50 = (f32[6,512]{1,0:T(8,128)}, f32[6,512]{1,0:T(8,128)S(1)}, u32[]{:S(2)}) copy-start(f32[6,512]{1,0:T(8,128)S(1)} %log_add_fusion.1) | copy-start | bytes 36868
  452.0 542.7 %reduce-scatter.13.cloned.1.call-start = ((), (), s32[]{:S(2)}) async-start(), calls=%async_computation.12 | async-start | bytes 1769472 | tf_op jit(solution)/shard_map/reduce_scatter | solution.py:278
  703.2 8.5 copy-start.7
  703.2 9.9 copy-start.28
  710.1 17.3 %slice-start.3 = ((s8[6291456]{0:T(1024)(128)(4,1)}), s8[4194304]{0:T(1024)(128)(4,1)S(1)}, s32[]{:S(2)}) async-start(s8[6291456]{0:T(1024)(128)(4,1)} %bitcast.132), calls=%async_computation.21 | async-start | bytes 8388608
  713.0 14.3 %slice-start.4 = ((s8[6291456]{0:T(1024)(128)(4,1)}), s8[2097152]{0:T(1024)(128)(4,1)S(1)}, s32[]{:S(2)}) async-start(s8[6291456]{0:T(1024)(128)(4,1)} %bitcast.132), calls=%async_computation.22 | async-start | bytes 4194304
  721.3 6.1 copy-start.37
  732.1 10.4 slice-start
  732.1 10.4 slice-start.1
  736.9 5.6 slice-start.2
  736.9 5.6 copy-start.24
  736.9 5.6 copy-start.32
  748.9 6.9 copy-start.18
  748.9 6.9 copy-start.35
  761.8 7.0 copy-start.43
  779.3 257.2 %reduce-scatter.17.cloned.1.call-start = ((), (), s32[]{:S(2)}) async-start(), calls=%async_computation.14 | async-start | bytes 1769472 | tf_op jit(solution)/shard_map/reduce_scatter | solution.py:281
  785.7 329.8 %reduce-scatter.11.cloned.1.call-start = ((), (), s32[]{:S(2)}) async-start(), calls=%async_computation.11 | async-start | bytes 5242880 | tf_op jit(solution)/shard_map/reduce_scatter | solution.py:272
  799.9 437.2 %reduce-scatter.15.cloned.1.call-start = ((), (), s32[]{:S(2)}) async-start(), calls=%async_computation.13 | async-start | bytes 6488064 | tf_op jit(solution)/shard_map/reduce_scatter | solution.py:294
  (42 other events, 104.5 us)
Sparse Core Ops, SparseCore 0:
  62.6 293.3 all-reduce.5
  413.3 289.8 all-reduce.7
  706.6 52.7 reduce-scatter.18
  762.7 53.7 reduce-scatter.20
  819.9 53.6 reduce-scatter.22
  875.7 76.7 reduce-scatter.8
  955.8 38.8 reduce-scatter.12
  998.0 38.3 reduce-scatter.16
  1038.7 76.7 reduce-scatter.10
  1121.6 115.4 reduce-scatter.14
where the time goes:
time: 1250 us; the launch traced here: 1240 us
  waiting for transfers between devices  863 us (69%)
  matrix products  172 us (14%)
  other arithmetic  80.4 us (6%)
  local copies, waits for them, and re-layouts  71.4 us (6%)
  blocking collectives  41.1 us (3%)
  between operations  15.7 us (1%)
    psum x1, waiting for transfers between devices, shards(): hidden_full = x_float + lax.psum(attn_part, 'mp')  293 us
    psum x1, waiting for transfers between devices, shards(): dn_two = lax.psum(dn_two_part, 'mp')  251 us
    reduce_scatter x1, waiting for transfers between devices, shards(): lax.psum_scatter(dn_one_part.astype(jnp.bfloat16), 'mp', scatter_dimensio...  77.4 us
    reduce_scatter x1, waiting for transfers between devices, shards(): lax.psum_scatter(ffn_part.astype(jnp.bfloat16), 'mp', scatter_dimension=0...  76.7 us
    reduce_scatter x1, waiting for transfers between devices, shards(): lax.psum_scatter(grad_keyval, ('dp', 'mp'), scatter_dimension=0, tiled=True)  73.2 us
    psum x1, blocking collectives, shards(): lax.psum((grad_gain_one, grad_gain_two, grad_q_gain, grad_k_gain), ('dp',...  41.1 us
    reduce_scatter x1, waiting for transfers between devices, shards(): lax.psum_scatter(grad_out_proj.astype(jnp.bfloat16), 'dp', scatter_dimens...  39.9 us
    reduce_scatter x1, waiting for transfers between devices, shards(): lax.psum_scatter(grad_query.astype(jnp.bfloat16), 'dp', scatter_dimension...  38.2 us
  transfers between devices with their start and end apart: 10, of which 8 were waited for; matrix products, arithmetic and copies ran while one was open for 16% of the time, Pallas kernels for 0%

commit v1 on v0

--- a/solution.py
+++ b/solution.py
@@ -171,9 +171,12 @@
         jnp.concatenate(block_outs, axis=0).reshape(row_count, head_span).astype(jnp.bfloat16)
     )
     attn_part = jnp.dot(attended, w_out, preferred_element_type=jnp.float32)
-    hidden_full = x_float + lax.psum(attn_part, "mp")
-    hidden_rows = lax.dynamic_slice_in_dim(hidden_full, row_first, shard_rows, 0)
-    xn_two = (normalize(hidden_full) * gain_two).astype(jnp.bfloat16)
+    hidden_rows = x_rows + lax.psum_scatter(
+        attn_part.astype(jnp.bfloat16), "mp", scatter_dimension=0, tiled=True
+    ).astype(jnp.float32)
+    xn_two = lax.all_gather(
+        (normalize(hidden_rows) * gain_two).astype(jnp.bfloat16), "mp", axis=0, tiled=True
+    )
     live_cols = jnp.repeat(slot_live.astype(jnp.float32), tile_cols)
     gate_act = jnp.dot(xn_two, w_gate, preferred_element_type=jnp.float32)
     up_act = jnp.dot(xn_two, w_up, preferred_element_type=jnp.float32)
@@ -201,14 +204,13 @@
     dn_two_part = lax.dot_general(
         d_gate, w_gate, CONTRACT_LAST, preferred_element_type=jnp.float32
     ) + lax.dot_general(d_up, w_up, CONTRACT_LAST, preferred_element_type=jnp.float32)
-    dn_two = lax.psum(dn_two_part, "mp")
-    back_two, _ = norm_back(dn_two, hidden_full, gain_two)
-    dh_full = out_grad.astype(jnp.float32) + back_two
-    dh_rows = lax.dynamic_slice_in_dim(dh_full, row_first, shard_rows, 0)
-    grad_gain_two = jnp.sum(
-        lax.dynamic_slice_in_dim(dn_two, row_first, shard_rows, 0) * normalize(hidden_rows), axis=0
-    )
-    dh_low = dh_full.astype(jnp.bfloat16)
+    dn_two_rows = lax.psum_scatter(
+        dn_two_part.astype(jnp.bfloat16), "mp", scatter_dimension=0, tiled=True
+    ).astype(jnp.float32)
+    back_two, grad_gain_two = norm_back(dn_two_rows, hidden_rows, gain_two)
+    g_rows = lax.dynamic_slice_in_dim(out_grad, row_first, shard_rows, 0)
+    dh_rows = g_rows.astype(jnp.float32) + back_two
+    dh_low = lax.all_gather(dh_rows.astype(jnp.bfloat16), "mp", axis=0, tiled=True)
     grad_out_proj = lax.dot_general(
         attended, dh_low, CONTRACT_FIRST, preferred_element_type=jnp.float32
     )
@@ -262,12 +264,24 @@
     dn_one_part = lax.dot_general(d_proj, w_proj, CONTRACT_LAST, preferred_element_type=jnp.float32)
     grad_proj = lax.dot_general(xn_one, d_proj, CONTRACT_FIRST, preferred_element_type=jnp.float32)
     grad_query = grad_proj[:, :head_span]
-    grad_keyval = jnp.zeros((model_width, 2 * kv_heads * head_size), jnp.float32)
+    keyval_window = jnp.concatenate(
+        [
+            fold_heads(grad_proj[:, head_span : 2 * head_span]),
+            fold_heads(grad_proj[:, 2 * head_span :]),
+        ],
+        axis=1,
+    ).astype(jnp.bfloat16)
+    keyval_rows = lax.psum_scatter(keyval_window, "dp", scatter_dimension=0, tiled=True)
+    window_span = kv_window * head_size
+    grad_keyval = jnp.zeros((keyval_rows.shape[0], 2 * kv_heads * head_size), jnp.bfloat16)
     grad_keyval = lax.dynamic_update_slice_in_dim(
-        grad_keyval, fold_heads(grad_proj[:, head_span : 2 * head_span]), kv_first * head_size, 1
+        grad_keyval, keyval_rows[:, :window_span], kv_first * head_size, 1
     )
     grad_keyval = lax.dynamic_update_slice_in_dim(
-        grad_keyval, fold_heads(grad_proj[:, 2 * head_span :]), (kv_heads + kv_first) * head_size, 1
+        grad_keyval, keyval_rows[:, window_span:], (kv_heads + kv_first) * head_size, 1
+    )
+    grad_keyval = lax.psum_scatter(grad_keyval, "mp", scatter_dimension=0, tiled=True).astype(
+        jnp.float32
     )
     dn_one_rows = lax.psum_scatter(
         dn_one_part.astype(jnp.bfloat16), "mp", scatter_dimension=0, tiled=True
@@ -291,7 +305,6 @@
             grad_down.astype(jnp.bfloat16), "dp", scatter_dimension=1, tiled=True
         ).astype(jnp.float32),
     )
-    grad_keyval = lax.psum_scatter(grad_keyval, ("dp", "mp"), scatter_dimension=0, tiled=True)
     grad_gain_one, grad_gain_two, grad_q_gain, grad_k_gain = lax.psum(
         (grad_gain_one, grad_gain_two, grad_q_gain, grad_k_gain), ("dp", "mp")
     )

time: 1250 us -> 997 us (0.80)
  waiting for transfers between devices: 863 us -> 651 us
  local copies, waits for them, and re-layouts: 71.4 us -> 39.3 us
  other arithmetic: 80.4 us -> 67.6 us
    psum x2 -> x0, waiting for transfers between devices: 544 us -> none  [the longest x1 293 us: shards(): hidden_full = x_float + lax.psum(attn_part, 'mp')]
    all_gather x0 -> x2, waiting for transfers between devices: none -> 162 us  [the longest x1 81.2 us: shards(): lax.all_gather((normalize(hidden_rows) * gain_two).astype(jnp.bfloat16),...]
    reduce_scatter x1 -> x4, waiting for transfers between devices: 73.2 us -> 170 us  [the longest x1 75.4 us: shards(): lax.psum_scatter(dn_two_part.astype(jnp.bfloat16), 'mp', scatter_dimensio...]
    reduce_scatter x1, waiting for transfers between devices: 0.01 us -> 55.1 us  [shards(): lax.psum_scatter(grad_up.astype(jnp.bfloat16), 'dp', scatter_dimension=0,...]
    reduce_scatter x1, waiting for transfers between devices: 0.02 us -> 55.1 us  [shards(): lax.psum_scatter(grad_gate.astype(jnp.bfloat16), 'dp', scatter_dimension=...]
    reduce_scatter x1, waiting for transfers between devices: 76.7 us -> 32.2 us  [shards(): lax.psum_scatter(ffn_part.astype(jnp.bfloat16), 'mp', scatter_dimension=0...]
    dynamic_update_slice x2, local copies, waits for them, and re-layouts: 22.5 us -> 3.38 us  [the longest x1 1.79 us: shards(): lax.dynamic_update_slice_in_dim(grad_keyval, keyval_rows[:, :window_span]...]
    unnamed x164 -> x168, local copies, waits for them, and re-layouts: 25.4 us -> 20.5 us
  transfers between devices with their start and end apart: 10 -> 13, of which waited for: 8 -> 12; matrix products, arithmetic and copies ran while one was open for 16% -> 9% of each run, Pallas kernels for 0% -> 0%
where the time goes in v1:
time: 997 us; the launch traced here: 992 us
  waiting for transfers between devices  651 us (65%)
  matrix products  172 us (17%)
  other arithmetic  67.6 us (7%)
  blocking collectives  45.8 us (5%)
  local copies, waits for them, and re-layouts  39.3 us (4%)
  between operations  15.4 us (2%)
    all_gather x1, waiting for transfers between devices, shards(): lax.all_gather((normalize(hidden_rows) * gain_two).astype(jnp.bfloat16),...  81.2 us
    all_gather x1, waiting for transfers between devices, shards(): lax.all_gather(dh_rows.astype(jnp.bfloat16), 'mp', axis=0, tiled=True)  80.6 us
    reduce_scatter x1, waiting for transfers between devices, shards(): lax.psum_scatter(dn_one_part.astype(jnp.bfloat16), 'mp', scatter_dimensio...  75.6 us
    reduce_scatter x1, waiting for transfers between devices, shards(): lax.psum_scatter(dn_two_part.astype(jnp.bfloat16), 'mp', scatter_dimensio...  75.4 us
    reduce_scatter x1, waiting for transfers between devices, shards(): lax.psum_scatter(attn_part.astype(jnp.bfloat16), 'mp', scatter_dimension=...  73 us
    reduce_scatter x1, waiting for transfers between devices, shards(): lax.psum_scatter(grad_gate.astype(jnp.bfloat16), 'dp', scatter_dimension=...  55.1 us
    reduce_scatter x1, waiting for transfers between devices, shards(): lax.psum_scatter(grad_up.astype(jnp.bfloat16), 'dp', scatter_dimension=0,...  55.1 us
    psum x1, blocking collectives, shards(): lax.psum((grad_gain_one, grad_gain_two, grad_q_gain, grad_k_gain), ('dp',...  45.8 us
  transfers between devices with their start and end apart: 13, of which 12 were waited for; matrix products, arithmetic and copies ran while one was open for 9% of the time, Pallas kernels for 0%

profile of v1, /device:TPU:0, one launch (start us, length us, event | category | flops | bytes accessed | tf_op | source)
XLA Modules:
  0.0 991.8 jit_solution(625020342008226701)
XLA Ops:
  9.6 3.2 multiply_reduce_fusion.1
  13.0 3.5 fusion.110
  16.8 4.6 constant_dynamic-slice_fusion.1
  26.0 4.5 fusion.54
  40.2 3.0 fusion.116
  43.2 2.8 fusion
  47.8 3.6 fusion.74
  54.4 4.4 convolution_convert_fusion.3
  59.0 6.5 convert_element_type.161
  65.5 73.0 %reduce-scatter.12.cloned.1.call-done = bf16[256,2048]{1,0:T(8,128)(2,1)} async-done(((bf16[1024,2048]{1,0:T(8,128)(2,1)}), bf16[256,2048]{1,0:T(8,128)(2,1)}) %reduce-scatter.12.cloned.1.call-update) | async-done | bytes 1048592 | tf_op jit(solution)/shard_map/reduce_scatter | solution.py:174
  138.4 3.0 multiply_reduce_fusion.4
  144.1 81.2 %all-gather.3.cloned.1.call-done = bf16[1024,2048]{1,0:T(8,128)(2,1)} async-done(((bf16[256,2048]{1,0:T(8,128)(2,1)}), bf16[1024,2048]{1,0:T(8,128)(2,1)}) %all-gather.3.cloned.1.call-update) | async-done | bytes 4194320 | tf_op jit(solution)/shard_map/all_gather | solution.py:177
  225.3 10.5 %fusion.119 = f32[1024,1152]{1,0:T(8,128)} fusion(bf16[1024,2048]{1,0:T(8,128)(2,1)} %all-gather.3.cloned.1.call-done, bf16[2048,1152]{1,0:T(8,128)(2,1)} %param.37), kind=kOutput, calls=%fused_computation.206 | convolution fusion | flops 4831838208 | bytes 13631488 | tf_op jit(solution)/shard_map/dot_general | solution.py:182
  235.8 9.7 fusion.118
  245.5 13.1 %multiply_convert_fusion.3 = (bf16[1024,1152]{1,0:T(8,128)(2,1)}, bf16[1024,1152]{1,0:T(8,128)(2,1)}, bf16[1024,1152]{1,0:T(8,128)(2,1)}) fusion(f32[1024,1152]{1,0:T(8,128)} %fusion.118, f32[1024,1152]{1,0:T(8,128)} %fusion.119, f32[1152]{0:T(1024)S(1)} %broadcast_bitcast_fusion, bf16[1024,2048]{1,0:T(8,128)(2,1)S(1)} %copy-done.34, ...), kind=kOutput, calls=%fused_computation.32 | convolution fusion | flops 4851892224 | bytes 25432576 | tf_op jit(solution)/shard_map/dot_general | solution.py:192
  258.6 7.4 fusion.120
  266.1 7.6 add_convert_fusion
  273.8 75.4 %reduce-scatter.16.cloned.1.call-done = bf16[256,2048]{1,0:T(8,128)(2,1)} async-done(((bf16[1024,2048]{1,0:T(8,128)(2,1)}), bf16[256,2048]{1,0:T(8,128)(2,1)}) %reduce-scatter.16.cloned.1.call-update) | async-done | bytes 1048592 | tf_op jit(solution)/shard_map/reduce_scatter | solution.py:207
  349.2 3.4 fusion.50
  352.7 2.9 fusion.109
  356.4 80.6 %all-gather.5.cloned.1.call-done = bf16[1024,2048]{1,0:T(8,128)(2,1)} async-done(((bf16[256,2048]{1,0:T(8,128)(2,1)}), bf16[1024,2048]{1,0:T(8,128)(2,1)}) %all-gather.5.cloned.1.call-update) | async-done | bytes 4194320 | tf_op jit(solution)/shard_map/all_gather | solution.py:213
  437.0 4.0 convolution_convert_fusion.9
  441.1 4.9 fusion.65
  446.0 7.5 multiply_reduce_fusion.2
  453.6 4.8 multiply_convert_fusion.2
  461.1 6.3 multiply_reduce_fusion
  469.8 6.7 multiply_convert_fusion
  487.2 5.3 fusion.79
  493.3 2.8 copy-done.14
  496.2 4.0 fusion.41
  500.7 3.8 fusion.38
  506.5 9.1 convolution_convert_fusion
  515.6 10.1 %convolution_convert_fusion.2 = bf16[2048,1152]{1,0:T(8,128)(2,1)} fusion(bf16[1024,2048]{1,0:T(8,128)(2,1)} %all-gather.3.cloned.1.call-done, bf16[1024,1152]{1,0:T(8,128)(2,1)} %get-tuple-element.141), kind=kOutput, calls=%fused_computation.13 | convolution fusion | flops 4834197504 | bytes 11272192 | tf_op jit(solution)/shard_map/dot_general | solution.py:202
  525.8 9.6 convolution_convert_fusion.1
  536.5 5.3 convolution_convert_fusion.7
  541.9 3.5 slice.261
  557.8 9.7 fusion.19
  567.6 10.3 %convolution_convert_fusion.4 = bf16[1024,2048]{1,0:T(8,128)(2,1)} fusion(bf16[1024,1152]{1,0:T(8,128)(2,1)} %get-tuple-element.142, bf16[1152,2048]{1,0:T(8,128)(2,1)} %param.38), kind=kOutput, calls=%fused_computation.43 | convolution fusion | flops 4833935360 | bytes 11272192 | tf_op jit(solution)/shard_map/dot_general | solution.py:186
  578.5 21.9 %reduce-scatter.32.cloned.1.call-done = bf16[1152,256]{1,0:T(8,128)(2,1)} async-done(((bf16[1152,2048]{1,0:T(8,128)(2,1)}), bf16[1152,256]{1,0:T(8,128)(2,1)}) %reduce-scatter.32.cloned.1.call-update) | async-done | bytes 589840 | tf_op jit(solution)/shard_map/reduce_scatter | solution.py:304
  602.6 55.1 %reduce-scatter.28.cloned.1.call-done = bf16[256,1152]{1,0:T(8,128)(2,1)} async-done(((bf16[2048,1152]{1,0:T(8,128)(2,1)}), bf16[256,1152]{1,0:T(8,128)(2,1)}) %reduce-scatter.28.cloned.1.call-update) | async-done | bytes 589840 | tf_op jit(solution)/shard_map/reduce_scatter | solution.py:298
  659.8 55.1 %reduce-scatter.30.cloned.1.call-done = bf16[256,1152]{1,0:T(8,128)(2,1)} async-done(((bf16[2048,1152]{1,0:T(8,128)(2,1)}), bf16[256,1152]{1,0:T(8,128)(2,1)}) %reduce-scatter.30.cloned.1.call-update) | async-done | bytes 589840 | tf_op jit(solution)/shard_map/reduce_scatter | solution.py:301
  717.2 39.4 %reduce-scatter.26.cloned.1.call-done = bf16[384,256]{1,0:T(8,128)(2,1)} async-done(((bf16[384,2048]{1,0:T(8,128)(2,1)}), bf16[384,256]{1,0:T(8,128)(2,1)}) %reduce-scatter.26.cloned.1.call-update) | async-done | bytes 196624 | tf_op jit(solution)/shard_map/reduce_scatter | solution.py:295
  758.3 39.8 %reduce-scatter.20.cloned.1.call-done = bf16[256,384]{0,1:T(8,128)(2,1)} async-done(((bf16[2048,384]{0,1:T(8,128)(2,1)}), bf16[256,384]{0,1:T(8,128)(2,1)}) %reduce-scatter.20.cloned.1.call-update) | async-done | bytes 196624 | tf_op jit(solution)/shard_map/reduce_scatter | solution.py:292
  799.9 21.3 %reduce-scatter.24.cloned.1.call-done = bf16[64,768]{1,0:T(8,128)(2,1)} async-done(((bf16[256,768]{1,0:T(8,128)(2,1)}), bf16[64,768]{1,0:T(8,128)(2,1)}) %reduce-scatter.24.cloned.1.call-update) | async-done | bytes 98320 | tf_op jit(solution)/shard_map/reduce_scatter | solution.py:283
  822.8 75.6 %reduce-scatter.18.cloned.1.call-done = bf16[256,2048]{1,0:T(8,128)(2,1)} async-done(((bf16[1024,2048]{1,0:T(8,128)(2,1)}), bf16[256,2048]{1,0:T(8,128)(2,1)}) %reduce-scatter.18.cloned.1.call-update) | async-done | bytes 1048592 | tf_op jit(solution)/shard_map/reduce_scatter | solution.py:286
  901.2 45.8 %all-reduce.2 = (f32[2048]{0:T(1024)}, f32[64]{0:T(128)}, f32[64]{0:T(128)}, f32[2048]{0:T(1024)}) all-reduce(f32[2048]{0:T(1024)S(1)} %get-tuple-element.124, f32[64]{0:T(128)S(1)} %reduce_sum.208, f32[64]{0:T(128)S(1)} %copy-done.67, f32[2048]{0:T(1024)S(1)} %copy-done.48), channel_id=1, replica_groups=mesh['dp'=8,'mp'=4] {'dp','mp'}, use_global_device_ids=true, to_apply=%region_23.24 | all-reduce | flops 4224 | bytes 33792 | tf_op jit(solution)/shard_map/psum | solution.py:308
  946.9 32.2 %reduce-scatter.14.cloned.1.call-done = bf16[256,2048]{1,0:T(8,128)(2,1)} async-done(((bf16[1024,2048]{1,0:T(8,128)(2,1)}), bf16[256,2048]{1,0:T(8,128)(2,1)}) %reduce-scatter.14.cloned.1.call-update) | async-done | bytes 1048592 | tf_op jit(solution)/shard_map/reduce_scatter | solution.py:187
  979.1 6.0 fusion.46
  (277 shorter events, 72.7 us)
Async XLA Ops:
  7.2 47.3 %copy-start = (bf16[384,2048]{1,0:T(8,128)(2,1)S(1)}, bf16[384,2048]{1,0:T(8,128)(2,1)}, u32[]{:S(2)}) copy-start(bf16[384,2048]{1,0:T(8,128)(2,1)} %param.34) | copy-start | bytes 4718596
  7.2 131.2 %reduce-scatter.12.cloned.1.call-start = ((), (), s32[]{:S(2)}) async-start(), calls=%async_computation.11 | async-start | bytes 5242880 | tf_op jit(solution)/shard_map/reduce_scatter | solution.py:174
  7.3 25.2 %copy-start.52 = (s32[6]{0:T(128)}, s32[6]{0:T(128)S(1)}, u32[]{:S(2)}) copy-start(s32[6]{0:T(128)S(1)} %fusion.94) | copy-start | bytes 76
  8.1 29.0 %copy-start.58 = (f32[64]{0:T(128)}, f32[64]{0:T(128)S(1)}, u32[]{:S(2)}) copy-start(f32[64]{0:T(128)S(1)} %convert_element_type.169) | copy-start | bytes 772
  8.7 28.4 %copy-start.65 = (f32[64]{0:T(128)}, f32[64]{0:T(128)S(1)}, u32[]{:S(2)}) copy-start(f32[64]{0:T(128)S(1)} %convert_element_type.167) | copy-start | bytes 772
  12.8 13.2 %copy-start.63 = (f32[1024]{0:T(1024)}, f32[1024]{0:T(1024)S(1)}, u32[]{:S(2)}) copy-start(f32[1024]{0:T(1024)S(1)} %add_rsqrt_fusion.2) | copy-start | bytes 12292
  13.0 13.0 %copy-start.46 = (f32[2048]{0:T(1024)}, f32[2048]{0:T(1024)S(1)}, u32[]{:S(2)}) copy-start(f32[2048]{0:T(1024)S(1)} %convert_element_type.162) | copy-start | bytes 24580
  16.5 20.6 %copy-start.8 = (f32[1024,384]{0,1:T(8,128)}, f32[1024,384]{0,1:T(8,128)S(1)}, u32[]{:S(2)}) copy-start(f32[1024,384]{0,1:T(8,128)S(1)} %fusion.110) | copy-start | bytes 4718596
  16.8 20.4 %copy-start.40 = (f32[1024,6]{0,1:T(8,128)}, f32[1024,6]{0,1:T(8,128)S(1)}, u32[]{:S(2)}) copy-start(f32[1024,6]{0,1:T(8,128)S(1)} %add_rsqrt_fusion.1) | copy-start | bytes 73732
  32.4 13.7 %copy-start.23 = (bf16[1024,6,64]{0,1,2:T(8,128)(2,1)}, bf16[1024,6,64]{0,1,2:T(8,128)(2,1)S(1)}, u32[]{:S(2)}) copy-start(bf16[1024,6,64]{0,1,2:T(8,128)(2,1)S(1)} %fusion.64) | copy-start | bytes 2359300
  32.4 19.8 %copy-start.28 = (bf16[512,6,64]{0,1,2:T(8,128)(2,1)}, bf16[512,6,64]{0,1,2:T(8,128)(2,1)S(1)}, u32[]{:S(2)}) copy-start(bf16[512,6,64]{0,1,2:T(8,128)(2,1)S(1)} %slice.205) | copy-start | bytes 1179652
  40.2 12.0 %copy-start.3 = (f32[6,512,512]{1,2,0:T(8,128)}, f32[6,512,512]{1,2,0:T(8,128)S(1)}, u32[]{:S(2)}) copy-start(f32[6,512,512]{1,2,0:T(8,128)S(1)} %get-tuple-element.178) | copy-start | bytes 18874372
  58.9 6.5 copy-start.62
  58.9 166.4 %all-gather.3.cloned.1.call-start = ((), (), s32[]{:S(2)}) async-start(), calls=%async_computation.12 | async-start | bytes 5242880 | tf_op jit(solution)/shard_map/all_gather | solution.py:177
  141.4 211.2 %copy-start.49 = (f32[256]{0:T(256)}, f32[256]{0:T(256)S(1)}, u32[]{:S(2)}) copy-start(f32[256]{0:T(256)S(1)} %add_rsqrt_fusion.4) | copy-start | bytes 3076
  143.9 205.3 %reduce-scatter.16.cloned.1.call-start = ((), (), s32[]{:S(2)}) async-start(), calls=%async_computation.14 | async-start | bytes 5242880 | tf_op jit(solution)/shard_map/reduce_scatter | solution.py:207
  225.3 10.5 %copy-start.70 = (bf16[1024,2048]{1,0:T(8,128)(2,1)S(1)}, bf16[1024,2048]{1,0:T(8,128)(2,1)}, u32[]{:S(2)}) copy-start(bf16[1024,2048]{1,0:T(8,128)(2,1)} %all-gather.3.cloned.1.call-done) | copy-start | bytes 12582916
  235.8 9.7 copy-start.34
  235.8 22.8 %slice-start.6 = ((s8[4718592]{0:T(1024)(128)(4,1)}), s8[4194304]{0:T(1024)(128)(4,1)S(1)}, s32[]{:S(2)}) async-start(s8[4718592]{0:T(1024)(128)(4,1)} %bitcast.161), calls=%async_computation.30 | async-start | bytes 8388608
  235.8 30.3 %slice-start.8 = ((s8[4718592]{0:T(1024)(128)(4,1)}), s8[4194304]{0:T(1024)(128)(4,1)S(1)}, s32[]{:S(2)}) async-start(s8[4718592]{0:T(1024)(128)(4,1)} %bitcast.163), calls=%async_computation.32 | async-start | bytes 8388608
  245.5 13.1 %slice-start.7 = ((s8[4718592]{0:T(1024)(128)(4,1)}), s8[524288]{0:T(1024)(128)(4,1)S(1)}, s32[]{:S(2)}) async-start(s8[4718592]{0:T(1024)(128)(4,1)} %bitcast.161), calls=%async_computation.31 | async-start | bytes 1048576
  245.5 20.6 %slice-start.9 = ((s8[4718592]{0:T(1024)(128)(4,1)}), s8[524288]{0:T(1024)(128)(4,1)S(1)}, s32[]{:S(2)}) async-start(s8[4718592]{0:T(1024)(128)(4,1)} %bitcast.163), calls=%async_computation.33 | async-start | bytes 1048576
  258.6 7.5 copy-start.72
  273.8 163.2 %all-gather.5.cloned.1.call-start = ((), (), s32[]{:S(2)}) async-start(), calls=%async_computation.15 | async-start | bytes 5242880 | tf_op jit(solution)/shard_map/all_gather | solution.py:213
  355.6 195.4 %reduce-scatter.22.cloned.1.call-start = ((), (), s32[]{:S(2)}) async-start(), calls=%async_computation.18 | async-start | bytes 1769472 | tf_op jit(solution)/shard_map/reduce_scatter | solution.py:274
  356.4 89.6 %copy-start.45 = (f32[6,512]{1,0:T(8,128)}, f32[6,512]{1,0:T(8,128)S(1)}, u32[]{:S(2)}) copy-start(f32[6,512]{1,0:T(8,128)S(1)} %log_add_fusion.1) | copy-start | bytes 36868
  441.1 12.4 %slice-start.3 = ((s8[6291456]{0:T(1024)(128)(4,1)}), s8[4194304]{0:T(1024)(128)(4,1)S(1)}, s32[]{:S(2)}) async-start(s8[6291456]{0:T(1024)(128)(4,1)} %bitcast.134), calls=%async_computation.27 | async-start | bytes 8388608
  446.0 7.5 slice-start.4
  453.6 5.9 copy-start.22
  453.6 6.6 slice-start
  453.6 6.6 slice-start.1
  461.1 6.3 copy-start.27
  469.8 16.5 %copy-start.35 = (bf16[1024,6,64]{0,2,1:T(8,128)(2,1)}, bf16[1024,6,64]{0,2,1:T(8,128)(2,1)S(1)}, u32[]{:S(2)}) copy-start(bf16[1024,6,64]{0,2,1:T(8,128)(2,1)S(1)} %fusion.58) | copy-start | bytes 2359300
  506.4 94.0 %reduce-scatter.32.cloned.1.call-start = ((), (), s32[]{:S(2)}) async-start(), calls=%async_computation.23 | async-start | bytes 5308416 | tf_op jit(solution)/shard_map/reduce_scatter | solution.py:304
  515.6 142.1 %reduce-scatter.28.cloned.1.call-start = ((), (), s32[]{:S(2)}) async-start(), calls=%async_computation.21 | async-start | bytes 5308416 | tf_op jit(solution)/shard_map/reduce_scatter | solution.py:298
  525.8 189.1 %reduce-scatter.30.cloned.1.call-start = ((), (), s32[]{:S(2)}) async-start(), calls=%async_computation.22 | async-start | bytes 5308416 | tf_op jit(solution)/shard_map/reduce_scatter | solution.py:301
  535.4 221.2 %reduce-scatter.26.cloned.1.call-start = ((), (), s32[]{:S(2)}) async-start(), calls=%async_computation.20 | async-start | bytes 1769472 | tf_op jit(solution)/shard_map/reduce_scatter | solution.py:295
  541.8 256.3 %reduce-scatter.20.cloned.1.call-start = ((), (), s32[]{:S(2)}) async-start(), calls=%async_computation.17 | async-start | bytes 1769472 | tf_op jit(solution)/shard_map/reduce_scatter | solution.py:292
  545.4 275.8 %reduce-scatter.24.cloned.1.call-start = ((), (), s32[]{:S(2)}) async-start(), calls=%async_computation.19 | async-start | bytes 491520 | tf_op jit(solution)/shard_map/reduce_scatter | solution.py:283
  557.8 340.7 %reduce-scatter.18.cloned.1.call-start = ((), (), s32[]{:S(2)}) async-start(), calls=%async_computation.16 | async-start | bytes 5242880 | tf_op jit(solution)/shard_map/reduce_scatter | solution.py:286
  567.5 411.6 %reduce-scatter.14.cloned.1.call-start = ((), (), s32[]{:S(2)}) async-start(), calls=%async_computation.13 | async-start | bytes 5242880 | tf_op jit(solution)/shard_map/reduce_scatter | solution.py:187
  577.9 139.2 %copy-start.56 = (f32[384]{0:T(512)S(1)}, f32[384]{0:T(512)}, u32[]{:S(2)}) copy-start(f32[384]{0:T(512)} %get-tuple-element.144) | copy-start | bytes 4612
  659.8 241.3 %copy-start.48 = (f32[2048]{0:T(1024)S(1)}, f32[2048]{0:T(1024)}, u32[]{:S(2)}) copy-start(f32[2048]{0:T(1024)} %get-tuple-element.128) | copy-start | bytes 24580
  659.8 241.3 %copy-start.67 = (f32[64]{0:T(128)S(1)}, f32[64]{0:T(128)}, u32[]{:S(2)}) copy-start(f32[64]{0:T(128)} %get-tuple-element.126) | copy-start | bytes 772
  659.8 319.3 %copy-start.13 = (bf16[256,2048]{1,0:T(8,128)(2,1)S(1)}, bf16[256,2048]{1,0:T(8,128)(2,1)}, u32[]{:S(2)}) copy-start(bf16[256,2048]{1,0:T(8,128)(2,1)} %reduce-scatter.16.cloned.1.call-done) | copy-start | bytes 3145732
  659.8 319.3 %copy-start.50 = (f32[256]{0:T(256)S(1)}, f32[256]{0:T(256)}, u32[]{:S(2)}) copy-start(f32[256]{0:T(256)} %copy-done.49) | copy-start | bytes 3076
  659.8 319.3 %copy-start.55 = (f32[256]{0:T(256)S(1)}, f32[256]{0:T(256)}, u32[]{:S(2)}) copy-start(f32[256]{0:T(256)} %copy-done.54) | copy-start | bytes 3076
  946.9 38.2 %copy-start.1 = (bf16[384,2048]{1,0:T(8,128)(2,1)S(1)}, bf16[384,2048]{1,0:T(8,128)(2,1)}, u32[]{:S(2)}) copy-start(bf16[384,2048]{1,0:T(8,128)(2,1)} %param.34) | copy-start | bytes 4718596
  (48 other events, 119.5 us)
Sparse Core Ops, SparseCore 0:
  59.0 79.3 reduce-scatter.11
  144.1 81.2 all-gather.2
  273.9 75.2 reduce-scatter.15
  355.7 81.2 all-gather.4
  506.5 36.8 reduce-scatter.21
  546.7 53.6 reduce-scatter.31
  603.8 53.7 reduce-scatter.27
  661.1 53.7 reduce-scatter.29
  718.2 38.3 reduce-scatter.25
  759.7 38.3 reduce-scatter.19
  800.4 20.7 reduce-scatter.23
  823.4 75.0 reduce-scatter.17
  900.8 78.3 reduce-scatter.13

commit v2 on v1

--- a/solution.py
+++ b/solution.py
@@ -1,16 +1,265 @@
+import functools
 import math
 
 import jax
 import jax.numpy as jnp
 from jax import lax
+from jax.experimental import pallas as pl
+from jax.experimental.pallas import tpu as pltpu
 from jax.sharding import PartitionSpec as P
 
 EPSILON = 1e-06
 MASKED = -1000000000.0
 ROPE_BASE = 10000.0
 HIGHEST_PREC = lax.Precision.HIGHEST
+MESH_ID = pl.DeviceIdType.MESH
+KERNEL_VMEM = 60 * 1024 * 1024
 CONTRACT_LAST = (((1,), (1,)), ((), ()))
 CONTRACT_FIRST = (((0,), (0,)), ((), ()))
+
+
+def exchange_kernel(size, data_ref, out_ref, send_sem, recv_sem, local_sem):
+    here = lax.axis_index("mp")
+    barrier = pltpu.get_barrier_semaphore()
+    for step in range(1, size):
+        pl.semaphore_signal(
+            barrier, inc=1, device_id={"mp": (here + step) % size}, device_id_type=MESH_ID
+        )
+    pl.semaphore_wait(barrier, size - 1)
+    copies = []
+    for step in range(1, size):
+        there = (here + step) % size
+        copy = pltpu.make_async_remote_copy(
+            src_ref=data_ref.at[there],
+            dst_ref=out_ref.at[here],
+            send_sem=send_sem.at[step],
+            recv_sem=recv_sem.at[step],
+            device_id={"mp": there},
+            device_id_type=MESH_ID,
+        )
+        copy.start()
+        copies.append(copy)
+    own = pltpu.make_async_copy(data_ref.at[here], out_ref.at[here], local_sem)
+    own.start()
+    own.wait()
+    for copy in copies:
+        copy.wait()
+
+
+def exchange(data, collective_id):
+    size = data.shape[0]
+    return pl.pallas_call(
+        functools.partial(exchange_kernel, size),
+        out_shape=jax.ShapeDtypeStruct(data.shape, data.dtype),
+        in_specs=[pl.BlockSpec(memory_space=pltpu.VMEM)],
+        out_specs=pl.BlockSpec(memory_space=pltpu.VMEM),
+        scratch_shapes=[
+            pltpu.SemaphoreType.DMA((size,)),
+            pltpu.SemaphoreType.DMA((size,)),
+            pltpu.SemaphoreType.DMA,
+        ],
+        compiler_params=pltpu.CompilerParams(collective_id=collective_id, has_side_effects=True),
+        cost_estimate=pl.CostEstimate(flops=0, bytes_accessed=data.size * 32, transcendentals=0),
+        name=f"exchange_{collective_id}",
+    )(data)
+
+
+def sum_kernel(mp_size, dp_size, data_ref, out_ref, first, second, total, sems):
+    mp_here = lax.axis_index("mp")
+    dp_here = lax.axis_index("dp")
+    barrier = pltpu.get_barrier_semaphore()
+    for step in range(1, mp_size):
+        pl.semaphore_signal(
+            barrier, inc=1, device_id={"mp": (mp_here + step) % mp_size}, device_id_type=MESH_ID
+        )
+    for step in range(1, dp_size):
+        pl.semaphore_signal(
+            barrier, inc=1, device_id={"dp": (dp_here + step) % dp_size}, device_id_type=MESH_ID
+        )
+    pl.semaphore_wait(barrier, mp_size + dp_size - 2)
+    copies = []
+    for step in range(1, mp_size):
+        copy = pltpu.make_async_remote_copy(
+            src_ref=data_ref,
+            dst_ref=first.at[step],
+            send_sem=sems.at[0, step],
+            recv_sem=sems.at[1, step],
+            device_id={"mp": (mp_here + step) % mp_size},
+            device_id_type=MESH_ID,
+        )
+        copy.start()
+        copies.append(copy)
+    value = data_ref[...]
+    for step in range(1, mp_size):
+        copies[step - 1].wait()
+        value = value + first[step]
+    total[...] = value
+    copies = []
+    for step in range(1, dp_size):
+        copy = pltpu.make_async_remote_copy(
+            src_ref=total,
+            dst_ref=second.at[step],
+            send_sem=sems.at[2, step],
+            recv_sem=sems.at[3, step],
+            device_id={"dp": (dp_here + step) % dp_size},
+            device_id_type=MESH_ID,
+        )
+        copy.start()
+        copies.append(copy)
+    second[0] = value
+    for copy in copies:
+        copy.wait()
+    value = jnp.zeros_like(value)
+    for source in range(dp_size):
+        value = value + second[(dp_here - source + dp_size) % dp_size]
+    out_ref[...] = value
+
+
+def sum_everywhere(data, collective_id):
+    mp_size = lax.axis_size("mp")
+    dp_size = lax.axis_size("dp")
+    return pl.pallas_call(
+        functools.partial(sum_kernel, mp_size, dp_size),
+        out_shape=jax.ShapeDtypeStruct(data.shape, data.dtype),
+        in_specs=[pl.BlockSpec(memory_space=pltpu.VMEM)],
+        out_specs=pl.BlockSpec(memory_space=pltpu.VMEM),
+        scratch_shapes=[
+            pltpu.VMEM((mp_size,) + data.shape, data.dtype),
+            pltpu.VMEM((dp_size,) + data.shape, data.dtype),
+            pltpu.VMEM(data.shape, data.dtype),
+            pltpu.SemaphoreType.DMA((4, max(mp_size, dp_size))),
+        ],
+        compiler_params=pltpu.CompilerParams(collective_id=collective_id, has_side_effects=True),
+        name=f"sum_everywhere_{collective_id}",
+    )(data)
+
+
+def reduce_kernel(size, splits, count, *refs):
+    data_refs, out_refs = refs[:count], refs[count : 2 * count]
+    recv_refs, sums_refs = refs[2 * count : 3 * count], refs[3 * count : 4 * count]
+    send_sem, recv_sem = refs[4 * count :]
+    here = lax.axis_index("dp")
+    masks = [1 << index for index in range(size.bit_length() - 1)]
+    bit_of = {mask: (here // mask) % 2 for mask in masks}
+
+    def relative(offset):
+        place = here
+        for mask in masks:
+            if offset & mask:
+                place = place + mask - 2 * mask * bit_of[mask]
+        return place
+
+    barrier = pltpu.get_barrier_semaphore()
+    for mask in masks:
+        pl.semaphore_signal(
+            barrier, inc=1, device_id={"dp": relative(mask)}, device_id_type=MESH_ID
+        )
+    pl.semaphore_wait(barrier, len(masks))
+
+    items = []
+    for split in range(splits):
+        for index in range(count):
+            turn = (len(items)) % max(1, len(masks) - 1)
+            order = masks[:1] + masks[1 + turn :] + masks[1 : 1 + turn]
+            rows = data_refs[index].shape[1] // splits
+            items.append((index, split * rows, rows, order))
+    copies = {}
+
+    def start(item, stage, source_of):
+        index, first_row, rows, order = items[item]
+        mask = order[stage]
+        for offset in range(size):
+            if offset & mask and not any(offset & done for done in order[:stage]):
+                source = source_of(offset)
+                copy = pltpu.make_async_remote_copy(
+                    src_ref=source,
+                    dst_ref=recv_refs[index].at[offset - 1, pl.ds(first_row, rows)],
+                    send_sem=send_sem.at[item, offset],
+                    recv_sem=recv_sem.at[item, offset],
+                    device_id={"dp": relative(mask)},
+                    device_id_type=MESH_ID,
+                )
+                copy.start()
+                copies[(item, offset)] = copy
+
+    def received(item, stage):
+        index, first_row, rows, order = items[item]
+        return [
+            offset
+            for offset in range(size)
+            if offset & order[stage] and not any(offset & done for done in order[:stage])
+        ]
+
+    def add_up(item, stage, offset, store):
+        index, first_row, rows, order = items[item]
+        place = relative(offset)
+        step = 16
+
+        def body(turn, carry):
+            at = pl.ds(pl.multiple_of(first_row + turn * step, step), step)
+            value = data_refs[index][place, at, :].astype(jnp.float32)
+            for done in order[:stage]:
+                value = value + recv_refs[index][(offset | done) - 1, at, :].astype(jnp.float32)
+            store(index, at, value)
+            return carry
+
+        lax.fori_loop(0, rows // step, body, 0)
+
+    for item in range(len(items)):
+        index, first_row, rows, order = items[item]
+        start(
+            item,
+            0,
+            lambda offset: data_refs[index].at[relative(offset), pl.ds(first_row, rows)],
+        )
+    for stage in range(1, len(masks)):
+        for item in range(len(items)):
+            index, first_row, rows, order = items[item]
+            for offset in received(item, stage - 1):
+                copies[(item, offset)].wait_recv()
+            for offset in received(item, stage):
+
+                def store(index, at, value, offset=offset):
+                    sums_refs[index][offset // 2 - 1, at, :] = value.astype(jnp.bfloat16)
+
+                add_up(item, stage, offset, store)
+            start(
+                item,
+                stage,
+                lambda offset: sums_refs[index].at[offset // 2 - 1, pl.ds(first_row, rows)],
+            )
+    for item in range(len(items)):
+        for offset in received(item, len(masks) - 1):
+            copies[(item, offset)].wait_recv()
+
+        def store_out(index, at, value):
+            out_refs[index][at, :] = value
+
+        add_up(item, len(masks), 0, store_out)
+    for copy in copies.values():
+        copy.wait_send()
+
+
+def reduce_rows(arrays, size, collective_id, splits=2):
+    rows = arrays[0].shape[0] // size
+    widths = [array.shape[1] for array in arrays]
+    count = len(arrays)
+    items = count * splits
+    total = sum(array.size for array in arrays)
+    return pl.pallas_call(
+        functools.partial(reduce_kernel, size, splits, count),
+        out_shape=[jax.ShapeDtypeStruct((rows, width), jnp.float32) for width in widths],
+        in_specs=[pl.BlockSpec(memory_space=pltpu.VMEM)] * count,
+        out_specs=[pl.BlockSpec(memory_space=pltpu.VMEM)] * count,
+        scratch_shapes=[pltpu.VMEM((size - 1, rows, width), jnp.bfloat16) for width in widths]
+        + [pltpu.VMEM((size // 2 - 1, rows, width), jnp.bfloat16) for width in widths]
+        + [pltpu.SemaphoreType.DMA((items, size)), pltpu.SemaphoreType.DMA((items, size))],
+        compiler_params=pltpu.CompilerParams(
+            collective_id=collective_id, has_side_effects=True, vmem_limit_bytes=KERNEL_VMEM
+        ),
+        cost_estimate=pl.CostEstimate(flops=0, bytes_accessed=total * 12, transcendentals=0),
+        name=f"reduce_rows_{collective_id}",
+    )(*[array.reshape(size, rows, array.shape[1]) for array in arrays])
 
 
 def normalize(raw_in):
@@ -77,7 +326,15 @@
     heads_all = heads_dev * lax.axis_size("mp")
     kv_heads = w_keyval.shape[1] // (2 * head_size)
     group_size = heads_all // kv_heads
-    kv_window = min(kv_heads, (heads_dev + group_size - 2) // group_size + 1)
+    mp_size = lax.axis_size("mp")
+    dp_size = lax.axis_size("dp")
+    kv_window = max(
+        ((index + 1) * heads_dev - 1) // group_size - (index * heads_dev) // group_size + 1
+        for index in range(mp_size)
+    )
+    window_firsts = [
+        min(index * heads_dev // group_size, kv_heads - kv_window) for index in range(mp_size)
+    ]
     tile_cols = w_gate.shape[1] // slot_live.shape[0]
     shard_rows = row_count // lax.axis_size("mp")
     block_rows = min(512, row_count)
@@ -96,26 +353,36 @@
         w_keyval, (kv_heads + kv_first) * head_size, kv_window * head_size, 1
     )
 
-    def spread(window_cols):
-        return (
-            jnp.einsum(
-                "dwe,hw->dhe",
-                window_cols.reshape(model_width, kv_window, head_size),
-                head_pick.astype(jnp.bfloat16),
-                preferred_element_type=jnp.float32,
-            )
-            .astype(jnp.bfloat16)
-            .reshape(model_width, head_span)
-        )
-
     def fold_heads(per_head):
         return jnp.einsum(
-            "dhe,hw->dwe",
-            per_head.reshape(model_width, heads_dev, head_size),
-            head_pick,
-            precision=HIGHEST_PREC,
-        ).reshape(model_width, kv_window * head_size)
-
+            "the,hw->twe",
+            per_head.astype(jnp.bfloat16),
+            head_pick.astype(jnp.bfloat16),
+            preferred_element_type=jnp.float32,
+        ).reshape(row_count, kv_window * head_size)
+
+    def unfold_windows(per_source):
+        sums = [None] * kv_heads
+        for index, first in enumerate(window_firsts):
+            for place in range(kv_window):
+                part = per_source[index][:, place * head_size : (place + 1) * head_size].astype(
+                    jnp.float32
+                )
+                head = first + place
+                sums[head] = part if sums[head] is None else sums[head] + part
+        return jnp.concatenate(sums, axis=1)
+
+    dp_index = lax.axis_index("dp")
+    out_piece = lax.dynamic_slice_in_dim(
+        w_out, dp_index * (head_span // dp_size), head_span // dp_size, 0
+    )
+    query_piece = lax.dynamic_slice_in_dim(
+        w_query, dp_index * (model_width // dp_size), model_width // dp_size, 0
+    )
+    w_out_full = lax.all_gather(out_piece, ("mp", "dp"), axis=0, tiled=True)
+    w_query_full = lax.all_gather(query_piece, ("mp", "dp"), axis=0, tiled=True).reshape(
+        mp_size, model_width, head_span
+    )
     doc_id, doc_pos, token_index = doc_layout(doc_lengths[0], row_count)
     cosine_tab, sine_tab = rope_table(doc_pos, head_size)
     x_float = tokens.astype(jnp.float32)
@@ -170,10 +437,9 @@
     attended = (
         jnp.concatenate(block_outs, axis=0).reshape(row_count, head_span).astype(jnp.bfloat16)
     )
-    attn_part = jnp.dot(attended, w_out, preferred_element_type=jnp.float32)
-    hidden_rows = x_rows + lax.psum_scatter(
-        attn_part.astype(jnp.bfloat16), "mp", scatter_dimension=0, tiled=True
-    ).astype(jnp.float32)
+    att_rows_all = exchange(attended.reshape(mp_size, shard_rows, head_span), 1)
+    att_rows_cat = jnp.concatenate([att_rows_all[i] for i in range(mp_size)], axis=1)
+    hidden_rows = x_rows + jnp.dot(att_rows_cat, w_out_full, preferred_element_type=jnp.float32)
     xn_two = lax.all_gather(
         (normalize(hidden_rows) * gain_two).astype(jnp.bfloat16), "mp", axis=0, tiled=True
     )
@@ -193,14 +459,22 @@
         * live_cols
     )
     grad_down = lax.dot_general(
-        ffn_hidden, out_grad, CONTRACT_FIRST, preferred_element_type=jnp.float32
-    )
+        out_grad, ffn_hidden, CONTRACT_FIRST, preferred_element_type=jnp.float32
+    ).astype(jnp.bfloat16)
     d_gate = (d_hidden * up_act * gate_sigmoid * (1.0 + gate_act * (1.0 - gate_sigmoid))).astype(
         jnp.bfloat16
     )
     d_up = (d_hidden * gate_silu).astype(jnp.bfloat16)
-    grad_gate = lax.dot_general(xn_two, d_gate, CONTRACT_FIRST, preferred_element_type=jnp.float32)
-    grad_up = lax.dot_general(xn_two, d_up, CONTRACT_FIRST, preferred_element_type=jnp.float32)
+    grad_gate = lax.dot_general(
+        xn_two, d_gate, CONTRACT_FIRST, preferred_element_type=jnp.float32
+    ).astype(jnp.bfloat16)
+    grad_up = lax.dot_general(
+        xn_two, d_up, CONTRACT_FIRST, preferred_element_type=jnp.float32
+    ).astype(jnp.bfloat16)
+    grad_gate, grad_up, grad_down = reduce_rows(
+        (grad_gate, grad_up, grad_down), dp_size, 2
+    )
+    grad_down = grad_down.T
     dn_two_part = lax.dot_general(
         d_gate, w_gate, CONTRACT_LAST, preferred_element_type=jnp.float32
     ) + lax.dot_general(d_up, w_up, CONTRACT_LAST, preferred_element_type=jnp.float32)
@@ -212,10 +486,15 @@
     dh_rows = g_rows.astype(jnp.float32) + back_two
     dh_low = lax.all_gather(dh_rows.astype(jnp.bfloat16), "mp", axis=0, tiled=True)
     grad_out_proj = lax.dot_general(
-        attended, dh_low, CONTRACT_FIRST, preferred_element_type=jnp.float32
-    )
-    d_att = lax.dot_general(dh_low, w_out, CONTRACT_LAST, preferred_element_type=jnp.float32)
-    d_att = d_att.astype(jnp.bfloat16).reshape(row_count, heads_dev, head_size)
+        dh_low, attended, CONTRACT_FIRST, preferred_element_type=jnp.float32
+    ).astype(jnp.bfloat16)
+    d_att_rows = lax.dot_general(
+        dh_rows.astype(jnp.bfloat16), w_out_full, CONTRACT_LAST, preferred_element_type=jnp.float32
+    ).astype(jnp.bfloat16)
+    d_att_blocks = jnp.stack(
+        [d_att_rows[:, i * head_span : (i + 1) * head_span] for i in range(mp_size)]
+    )
+    d_att = exchange(d_att_blocks, 3).reshape(row_count, heads_dev, head_size)
     dq_blocks = []
     d_keys = jnp.zeros((row_count, heads_dev, head_size), jnp.float32)
     d_values = jnp.zeros((row_count, heads_dev, head_size), jnp.float32)
@@ -252,61 +531,60 @@
     d_queries = jnp.concatenate(dq_blocks, axis=0)
     dq_raw, grad_q_gain = norm_back(rotate(d_queries, cosine_tab, sine_tab, -1.0), q_raw, q_gain_f)
     dk_raw, grad_k_gain = norm_back(rotate(d_keys, cosine_tab, sine_tab, -1.0), k_raw, k_gain_f)
-    d_proj = jnp.concatenate(
+    dq_low = dq_raw.reshape(row_count, head_span).astype(jnp.bfloat16)
+    d_window = jnp.concatenate([fold_heads(dk_raw), fold_heads(d_values)], axis=1).astype(
+        jnp.bfloat16
+    )
+    window_span = kv_window * head_size
+    d_proj = jnp.concatenate([dq_low, d_window], axis=1)
+    d_proj_all = exchange(d_proj.reshape(mp_size, shard_rows, head_span + 2 * window_span), 4)
+    d_keyval_rows = jnp.concatenate(
         [
-            dq_raw.reshape(row_count, head_span),
-            dk_raw.reshape(row_count, head_span),
-            d_values.reshape(row_count, head_span),
+            unfold_windows(d_proj_all[:, :, head_span : head_span + window_span]),
+            unfold_windows(d_proj_all[:, :, head_span + window_span :]),
         ],
         axis=1,
     ).astype(jnp.bfloat16)
-    w_proj = jnp.concatenate([w_query, spread(key_cols), spread(value_cols)], axis=1)
-    dn_one_part = lax.dot_general(d_proj, w_proj, CONTRACT_LAST, preferred_element_type=jnp.float32)
-    grad_proj = lax.dot_general(xn_one, d_proj, CONTRACT_FIRST, preferred_element_type=jnp.float32)
-    grad_query = grad_proj[:, :head_span]
-    keyval_window = jnp.concatenate(
+    dn_one_rows = lax.dot_general(
+        d_keyval_rows, w_keyval, CONTRACT_LAST, preferred_element_type=jnp.float32
+    )
+    for index in range(mp_size):
+        dn_one_rows = dn_one_rows + lax.dot_general(
+            d_proj_all[index, :, :head_span],
+            w_query_full[index],
+            CONTRACT_LAST,
+            preferred_element_type=jnp.float32,
+        )
+    back_one, grad_gain_one = norm_back(dn_one_rows, x_rows, gain_one)
+    grad_tokens = dh_rows + back_one
+    grad_query = lax.dot_general(
+        xn_one, dq_low, CONTRACT_FIRST, preferred_element_type=jnp.float32
+    ).astype(jnp.bfloat16)
+    grad_window = lax.dot_general(
+        xn_one, d_window, CONTRACT_FIRST, preferred_element_type=jnp.float32
+    ).astype(jnp.bfloat16)
+    grad_out_proj, grad_query, grad_window = reduce_rows(
+        (grad_out_proj, grad_query, grad_window), dp_size, 5
+    )
+    grad_out_proj = grad_out_proj.T
+    window_rows = exchange(
+        grad_window.astype(jnp.bfloat16).reshape(mp_size, -1, 2 * window_span), 6
+    )
+    grad_keyval = jnp.concatenate(
         [
-            fold_heads(grad_proj[:, head_span : 2 * head_span]),
-            fold_heads(grad_proj[:, 2 * head_span :]),
+            unfold_windows(window_rows[:, :, :window_span]),
+            unfold_windows(window_rows[:, :, window_span:]),
         ],
         axis=1,
-    ).astype(jnp.bfloat16)
-    keyval_rows = lax.psum_scatter(keyval_window, "dp", scatter_dimension=0, tiled=True)
-    window_span = kv_window * head_size
-    grad_keyval = jnp.zeros((keyval_rows.shape[0], 2 * kv_heads * head_size), jnp.bfloat16)
-    grad_keyval = lax.dynamic_update_slice_in_dim(
-        grad_keyval, keyval_rows[:, :window_span], kv_first * head_size, 1
-    )
-    grad_keyval = lax.dynamic_update_slice_in_dim(
-        grad_keyval, keyval_rows[:, window_span:], (kv_heads + kv_first) * head_size, 1
-    )
-    grad_keyval = lax.psum_scatter(grad_keyval, "mp", scatter_dimension=0, tiled=True).astype(
-        jnp.float32
-    )
-    dn_one_rows = lax.psum_scatter(
-        dn_one_part.astype(jnp.bfloat16), "mp", scatter_dimension=0, tiled=True
-    ).astype(jnp.float32)
-    back_one, grad_gain_one = norm_back(dn_one_rows, x_rows, gain_one)
-    grad_tokens = dh_rows + back_one
-    grad_query, grad_out_proj, grad_gate, grad_up, grad_down = (
-        lax.psum_scatter(
-            grad_query.astype(jnp.bfloat16), "dp", scatter_dimension=0, tiled=True
-        ).astype(jnp.float32),
-        lax.psum_scatter(
-            grad_out_proj.astype(jnp.bfloat16), "dp", scatter_dimension=1, tiled=True
-        ).astype(jnp.float32),
-        lax.psum_scatter(
-            grad_gate.astype(jnp.bfloat16), "dp", scatter_dimension=0, tiled=True
-        ).astype(jnp.float32),
-        lax.psum_scatter(
-            grad_up.astype(jnp.bfloat16), "dp", scatter_dimension=0, tiled=True
-        ).astype(jnp.float32),
-        lax.psum_scatter(
-            grad_down.astype(jnp.bfloat16), "dp", scatter_dimension=1, tiled=True
-        ).astype(jnp.float32),
-    )
-    grad_gain_one, grad_gain_two, grad_q_gain, grad_k_gain = lax.psum(
-        (grad_gain_one, grad_gain_two, grad_q_gain, grad_k_gain), ("dp", "mp")
+    )
+    gain_sizes = (model_width, model_width, head_size, head_size)
+    gains = jnp.concatenate([grad_gain_one, grad_gain_two, grad_q_gain, grad_k_gain])
+    gain_rows = 8 * pl.cdiv(gains.shape[0], 1024)
+    gains = jnp.pad(gains, (0, gain_rows * 128 - gains.shape[0])).reshape(gain_rows, 128)
+    gains = sum_everywhere(gains, 7).reshape(-1)
+    bounds = [sum(gain_sizes[:i]) for i in range(5)]
+    grad_gain_one, grad_gain_two, grad_q_gain, grad_k_gain = (
+        gains[bounds[i] : bounds[i + 1]] for i in range(4)
     )
     return (
         block_out,

time: 997 us -> 635 us (0.64)
  waiting for transfers between devices: 651 us -> 114 us
  Pallas kernels: 0 us -> 215 us
  blocking collectives: 45.8 us -> 0 us
  local copies, waits for them, and re-layouts: 39.3 us -> 49.5 us
    reduce_scatter x9 -> x0, waiting for transfers between devices: 381 us -> none  [the longest x1 75.6 us: shards(): lax.psum_scatter(dn_one_part.astype(jnp.bfloat16), 'mp', scatter_dimensio...]
    pallas_call x0 -> x7, Pallas kernels: none -> 215 us  [the longest x2 103 us: reduce_rows(): pl.pallas_call(functools.partial(reduce_kernel, size, splits, count), out...]
    reduce_scatter x1, waiting for transfers between devices: 75.4 us -> 0.02 us  [shards(): lax.psum_scatter(dn_two_part.astype(jnp.bfloat16), 'mp', scatter_dimensio...]
    all_gather x1, waiting for transfers between devices: 80.6 us -> 22.4 us  [shards(): lax.all_gather(dh_rows.astype(jnp.bfloat16), 'mp', axis=0, tiled=True)]
    psum x1 -> x0, blocking collectives: 45.8 us -> none  [shards(): lax.psum((grad_gain_one, grad_gain_two, grad_q_gain, grad_k_gain), ('dp',...]
    reduce_scatter x1, waiting for transfers between devices: 32.2 us -> 0.01 us  [shards(): lax.psum_scatter(ffn_part.astype(jnp.bfloat16), 'mp', scatter_dimension=0...]
    all_gather x0 -> x2, waiting for transfers between devices: none -> 10.7 us  [the longest x1 10.7 us: shards(): w_out_full = lax.all_gather(out_piece, ('mp', 'dp'), axis=0, tiled=True)]
    unnamed x168 -> x189, local copies, waits for them, and re-layouts: 20.5 us -> 12.2 us
  transfers between devices with their start and end apart: 13 -> 6, of which waited for: 12 -> 3; matrix products, arithmetic and copies ran while one was open for 9% -> 33% of each run, Pallas kernels for 0% -> 29%
where the time goes in v2:
time: 635 us; the launch traced here: 625 us
  Pallas kernels  215 us (34%)
  matrix products  170 us (27%)
  waiting for transfers between devices  114 us (18%)
  other arithmetic  60.5 us (10%)
  local copies, waits for them, and re-layouts  49.5 us (8%)
  between operations  15.9 us (3%)
    pallas_call x2, Pallas kernels, reduce_rows(): pl.pallas_call(functools.partial(reduce_kernel, size, splits, count), out...  103 us
    pallas_call x4, Pallas kernels, exchange(): pl.pallas_call(functools.partial(exchange_kernel, size), out_shape=jax.Sh...  92.9 us
    all_gather x1, waiting for transfers between devices, shards(): lax.all_gather((normalize(hidden_rows) * gain_two).astype(jnp.bfloat16),...  80.7 us
    all_gather x1, waiting for transfers between devices, shards(): lax.all_gather(dh_rows.astype(jnp.bfloat16), 'mp', axis=0, tiled=True)  22.4 us
    pallas_call x1, Pallas kernels, sum_everywhere(): pl.pallas_call(functools.partial(sum_kernel, mp_size, dp_size), out_shape...  19 us
    dot_general x2, matrix products, shards(): jnp.einsum('qhe,khe->hqk', att_rows, v_low[:key_stop], preferred_element_...  13.6 us
    dot_general x1, matrix products, shards(): lax.dot_general(out_grad, w_down, CONTRACT_LAST, preferred_element_type=j...  12.7 us
  transfers between devices with their start and end apart: 6, of which 3 were waited for; matrix products, arithmetic and copies ran while one was open for 33% of the time, Pallas kernels for 29%

profile of v2, /device:TPU:0, one launch (start us, length us, event | category | flops | bytes accessed | tf_op | source)
XLA Modules:
  0.0 625.4 jit_solution(8851764521829239549)
XLA Ops:
  9.1 6.5 %convert_element_type.229 = f32[1024,2048]{1,0:T(8,128)} convert(bf16[1024,2048]{1,0:T(8,128)(2,1)} %param.26) | non-fusion elementwise | flops 2097152 | bytes 12582912 | tf_op jit(solution)/shard_map/convert_element_type | solution.py:388
  15.6 3.2 multiply_reduce_fusion.1
  19.0 3.6 fusion.93
  24.9 2.2 constant_dynamic-slice_fusion.3
  27.1 3.8 fusion.41
  41.7 2.4 fusion.98
  44.1 2.9 fusion
  48.7 3.6 fusion.37
  54.5 30.6 %exchange_1.1 = bf16[4,256,384]{2,1,0:T(8,128)(2,1)} custom-call(bf16[4,256,384]{2,1,0:T(8,128)(2,1)} %copy.152.data_ref), custom_call_target="tpu_custom_call" | custom-call | bytes 12582912 | tf_op jit(solution)/shard_map/exchange_1/pallas_call | solution.py:51
  86.4 10.7 %all-gather.5.cloned.1.call-done = bf16[1536,2048]{1,0:T(8,128)(2,1)} async-done(((bf16[48,2048]{1,0:T(8,128)(2,1)}), bf16[1536,2048]{1,0:T(8,128)(2,1)}) %all-gather.5.cloned.1.call-update) | async-done | bytes 6291472 | tf_op jit(solution)/shard_map/all_gather | solution.py:382
  97.1 5.3 multiply_reduce_fusion.6
  105.5 80.7 %all-gather.7.cloned.1.call-done = bf16[1024,2048]{1,0:T(8,128)(2,1)} async-done(((bf16[256,2048]{1,0:T(8,128)(2,1)}), bf16[1024,2048]{1,0:T(8,128)(2,1)}) %all-gather.7.cloned.1.call-update) | async-done | bytes 4194320 | tf_op jit(solution)/shard_map/all_gather | solution.py:443
  186.2 10.3 %fusion.100 = f32[1024,1152]{1,0:T(8,128)} fusion(bf16[1024,2048]{1,0:T(8,128)(2,1)} %all-gather.7.cloned.1.call-done, bf16[2048,1152]{1,0:T(8,128)(2,1)} %param.36), kind=kOutput, calls=%fused_computation.248 | convolution fusion | flops 4831838208 | bytes 13631488 | tf_op jit(solution)/shard_map/dot_general | solution.py:447
  196.5 9.7 %fusion.101 = f32[1024,1152]{1,0:T(8,128)} fusion(bf16[1024,2048]{1,0:T(8,128)(2,1)S(1)} %copy-done.76, bf16[2048,1152]{1,0:T(8,128)(2,1)} %param.37), kind=kOutput, calls=%fused_computation.249 | convolution fusion | flops 4831838208 | bytes 13631488 | tf_op jit(solution)/shard_map/dot_general | solution.py:448
  206.2 12.7 %multiply_convert_fusion.3 = (bf16[1024,1152]{1,0:T(8,128)(2,1)}, bf16[1024,1152]{1,0:T(8,128)(2,1)S(1)}, bf16[1024,1152]{1,0:T(8,128)(2,1)}) fusion(f32[1024,1152]{1,0:T(8,128)} %fusion.100, f32[1024,1152]{1,0:T(8,128)} %fusion.101, f32[1152]{0:T(1024)S(1)} %broadcast_bitcast_fusion, bf16[1024,2048]{1,0:T(8,128)(2,1)S(1)} %copy-done.42, ...), kind=kOutput, calls=%fused_computation.27 | convolution fusion | flops 4851892224 | bytes 25432576 | tf_op jit(solution)/shard_map/dot_general | solution.py:458
  219.0 5.6 fusion.102
  224.6 7.3 %add_convert_fusion = bf16[1024,2048]{1,0:T(8,128)(2,1)} fusion(f32[1024,2048]{1,0:T(8,128)S(1)} %fusion.102, bf16[1024,1152]{1,0:T(8,128)(2,1)S(1)} %copy-done.81, bf16[2048,1152]{1,0:T(8,128)(2,1)S(1)} %bitcast.226), kind=kOutput, calls=%fused_computation.8 | convolution fusion | flops 4836032512 | bytes 19660800 | tf_op jit(solution)/shard_map/dot_general | solution.py:480
  238.0 9.2 %fusion.2 = bf16[2048,1152]{0,1:T(8,128)(2,1)} fusion(bf16[1024,1152]{1,0:T(8,128)(2,1)} %get-tuple-element.146, bf16[1024,2048]{1,0:T(8,128)(2,1)} %param.39), kind=kOutput, calls=%fused_computation.14 | convolution fusion | flops 4834197504 | bytes 11272192 | tf_op jit(solution)/shard_map/dot_general | solution.py:461
  247.2 6.7 %copy.173 = bf16[2048,1152]{1,0:T(8,128)(2,1)} copy(bf16[2048,1152]{0,1:T(8,128)(2,1)} %fusion.2) | data formatting | bytes 9437184 | tf_op jit(solution)/shard_map/convert_element_type | solution.py:463
  253.9 9.7 %convolution_convert_fusion.2 = bf16[2048,1152]{1,0:T(8,128)(2,1)} fusion(bf16[1024,2048]{1,0:T(8,128)(2,1)} %all-gather.7.cloned.1.call-done, bf16[1024,1152]{1,0:T(8,128)(2,1)} %copy-done.80), kind=kOutput, calls=%fused_computation.13 | convolution fusion | flops 4834197504 | bytes 11272192 | tf_op jit(solution)/shard_map/dot_general | solution.py:468
  263.6 7.3 %convolution_convert_fusion.1 = bf16[2048,1152]{1,0:T(8,128)(2,1)} fusion(bf16[1024,2048]{1,0:T(8,128)(2,1)S(1)} %copy-done.77, bf16[1024,1152]{1,0:T(8,128)(2,1)S(1)} %copy-done.82), kind=kOutput, calls=%fused_computation.12 | convolution fusion | flops 4834197504 | bytes 11272192 | tf_op jit(solution)/shard_map/dot_general | solution.py:471
  271.0 75.9 %reduce_rows_2.1 = (f32[256,1152]{1,0:T(8,128)}, f32[256,1152]{1,0:T(8,128)}, f32[256,1152]{1,0:T(8,128)}) custom-call(bf16[8,256,1152]{2,1,0:T(8,128)(2,1)} %bitcast.202, bf16[8,256,1152]{2,1,0:T(8,128)(2,1)} %bitcast.203, bf16[8,256,1152]{2,1,0:T(8,128)(2,1)} %bitcast.198), custom_call_target="tpu_custom_call" | custom-call | bytes 84934656 | tf_op jit(solution)/shard_map/reduce_rows_2/pallas_call | solution.py:249
  346.9 2.7 copy.175
  349.6 9.5 %convolution_convert_fusion.3 = bf16[1024,2048]{1,0:T(8,128)(2,1)} fusion(bf16[1024,1152]{1,0:T(8,128)(2,1)} %get-tuple-element.146, bf16[1152,2048]{1,0:T(8,128)(2,1)} %param.38), kind=kOutput, calls=%fused_computation.32 | convolution fusion | flops 4833935360 | bytes 11272192 | tf_op jit(solution)/shard_map/dot_general | solution.py:452
  359.4 3.4 fusion.19
  362.8 2.6 fusion.92
  365.4 5.0 convolution_convert_fusion.7
  371.5 22.2 %exchange_3.1 = bf16[4,256,384]{2,1,0:T(8,128)(2,1)} custom-call(bf16[4,256,384]{2,1,0:T(8,128)(2,1)} %pad_maximum_fusion.5.data_ref), custom_call_target="tpu_custom_call" | custom-call | bytes 12582912 | tf_op jit(solution)/shard_map/exchange_3/pallas_call | solution.py:51
  396.7 4.8 fusion.31
  401.5 6.0 fusion.25
  410.1 7.3 %multiply_reduce_fusion.2 = (f32[6,512]{1,0:T(8,128)S(1)}, f32[6,512,512]{1,2,0:T(8,128)}) fusion(f32[6,512,512]{1,2,0:T(8,128)} %copy-done.3, f32[6,512]{1,0:T(8,128)S(1)} %log_add_fusion.1, bf16[512,6,64]{0,2,1:T(8,128)(2,1)S(1)} %slice.434, bf16[512,6,64]{0,1,2:T(8,128)(2,1)S(1)} %copy-done.38), kind=kOutput, calls=%fused_computation.18 | convolution fusion | flops 206042112 | bytes 13393920 | tf_op jit(solution)/shard_map/qhe,khe->hqk/dot_general | solution.py:507
  417.4 4.8 multiply_convert_fusion.2
  425.0 6.4 %multiply_reduce_fusion = (f32[6,512]{1,0:T(8,128)S(1)}, f32[6,512,1024]{2,1,0:T(8,128)}) fusion(f32[6,512,1024]{2,1,0:T(8,128)S(1)} %bitcast.192, f32[6,512]{1,0:T(8,128)S(1)} %log_add_fusion, bf16[512,6,64]{0,2,1:T(8,128)(2,1)S(1)} %copy-done.31, bf16[1024,6,64]{0,1,2:T(8,128)(2,1)S(1)} %copy-done.27), kind=kOutput, calls=%fused_computation.1 | convolution fusion | flops 412087296 | bytes 26370048 | tf_op jit(solution)/shard_map/qhe,khe->hqk/dot_general | solution.py:507
  431.4 6.8 %multiply_convert_fusion = bf16[6,512,1024]{2,1,0:T(8,128)(2,1)S(1)} fusion(f32[6,512,1024]{2,1,0:T(8,128)} %get-tuple-element.211, f32[6,512,1024]{2,1,0:T(8,128)S(1)} %bitcast.192, f32[6,512]{1,0:T(8,128)S(1)} %get-tuple-element.210, f32[6,512]{1,0:T(8,128)S(1)} %log_add_fusion), kind=kLoop, calls=%fused_computation | loop fusion | flops 12582912 | bytes 31481856 | tf_op jit(solution)/shard_map/convert_element_type | solution.py:512
  454.4 2.8 multiply_reduce_fusion.8
  458.6 32.5 %exchange_4.1 = bf16[4,256,640]{2,1,0:T(8,128)(2,1)} custom-call(bf16[4,256,640]{2,1,0:T(8,128)(2,1)} %pad_maximum_fusion.2.data_ref), custom_call_target="tpu_custom_call" | custom-call | bytes 20971520 | tf_op jit(solution)/shard_map/exchange_4/pallas_call | solution.py:51
  493.7 4.5 fusion.103
  498.2 3.0 convolution_add_fusion.3
  504.2 3.9 multiply_reduce_fusion.3
  508.8 19.0 %sum_everywhere_7.1 = f32[40,128]{1,0:T(8,128)} custom-call(f32[40,128]{1,0:T(8,128)} %pad_bitcast_fusion.data_ref), custom_call_target="tpu_custom_call" | custom-call | tf_op jit(solution)/shard_map/sum_everywhere_7/pallas_call | solution.py:121
  530.6 4.9 convolution_convert_fusion.6
  535.5 3.9 convolution_convert_fusion.4
  539.5 6.3 %multiply_add_fusion = (f32[256,2048]{1,0:T(8,128)}, bf16[256,2048]{1,0:T(8,128)(2,1)}) fusion(f32[256,2048]{1,0:T(8,128)} %get-tuple-element.214, f32[1024,2048]{1,0:T(8,128)} %convert_element_type.229, s32[]{:T(128)S(6)} %select_n.40, f32[256]{0:T(256)S(1)} %broadcast_multiply_fusion.3, f32[2048]{0:T(1024)S(1)} %copy-done.54, f32[256]{0:T(256)S(1)} %copy-done.59, ...), kind=kLoop, calls=%fused_computation.54 | loop fusion | flops 8912896 | bytes 12603396 | tf_op jit(solution)/shard_map/add | solution.py:559
  545.8 22.4 %all-gather.11.cloned.1.call-done = bf16[1024,2048]{1,0:T(8,128)(2,1)} async-done(((bf16[256,2048]{1,0:T(8,128)(2,1)}), bf16[1024,2048]{1,0:T(8,128)(2,1)}) %all-gather.11.cloned.1.call-update) | async-done | bytes 4194320 | tf_op jit(solution)/shard_map/all_gather | solution.py:487
  568.2 5.8 convolution_convert_fusion.5
  574.0 26.7 %reduce_rows_5.1 = (f32[256,384]{1,0:T(8,128)}, f32[256,384]{1,0:T(8,128)}, f32[256,256]{1,0:T(8,128)}) custom-call(bf16[8,256,384]{2,1,0:T(8,128)(2,1)} %bitcast.207, bf16[8,256,384]{2,1,0:T(8,128)(2,1)} %bitcast.206, bf16[8,256,256]{2,1,0:T(8,128)(2,1)} %bitcast.210), custom_call_target="tpu_custom_call" | custom-call | bytes 25165824 | tf_op jit(solution)/shard_map/reduce_rows_5/pallas_call | solution.py:249
  602.4 7.7 %exchange_6.1 = bf16[4,64,256]{2,1,0:T(8,128)(2,1)} custom-call(bf16[4,64,256]{2,1,0:T(8,128)(2,1)} %bitcast.215), custom_call_target="tpu_custom_call" | custom-call | bytes 2097152 | tf_op jit(solution)/shard_map/exchange_6/pallas_call | solution.py:51
  615.0 2.4 copy.215
  (321 shorter events, 72.5 us)
Async XLA Ops:
  7.2 11.7 %copy-start = (bf16[2048,384]{1,0:T(8,128)(2,1)S(1)}, bf16[2048,384]{1,0:T(8,128)(2,1)}, u32[]{:S(2)}) copy-start(bf16[2048,384]{1,0:T(8,128)(2,1)} %param.30) | copy-start | bytes 4718596
  7.2 89.9 %all-gather.5.cloned.1.call-start = ((), (), s32[]{:S(2)}) async-start(), calls=%async_computation.2 | async-start | bytes 6488064 | tf_op jit(solution)/shard_map/all_gather | solution.py:382
  9.0 177.2 %all-gather.7.cloned.1.call-start = ((), (), s32[]{:S(2)}) async-start(), calls=%async_computation.3 | async-start | bytes 5242880 | tf_op jit(solution)/shard_map/all_gather | solution.py:443
  9.1 6.5 %copy-start.68 = (bf16[2048]{0:T(1024)(128)(2,1)S(1)}, bf16[2048]{0:T(1024)(128)(2,1)}, u32[]{:S(2)}) copy-start(bf16[2048]{0:T(1024)(128)(2,1)} %param.29) | copy-start | bytes 12292
  15.6 11.5 %copy-start.53 = (f32[2048]{0:T(1024)}, f32[2048]{0:T(1024)S(1)}, u32[]{:S(2)}) copy-start(f32[2048]{0:T(1024)S(1)} %convert_element_type.230) | copy-start | bytes 24580
  19.0 8.1 %copy-start.70 = (f32[1024]{0:T(1024)}, f32[1024]{0:T(1024)S(1)}, u32[]{:S(2)}) copy-start(f32[1024]{0:T(1024)S(1)} %add_rsqrt_fusion.2) | copy-start | bytes 12292
  24.6 12.9 %copy-start.7 = (f32[1024,384]{0,1:T(8,128)}, f32[1024,384]{0,1:T(8,128)S(1)}, u32[]{:S(2)}) copy-start(f32[1024,384]{0,1:T(8,128)S(1)} %copy.146) | copy-start | bytes 4718596
  24.6 12.9 %copy-start.72 = (f32[64]{0:T(128)}, f32[64]{0:T(128)S(1)}, u32[]{:S(2)}) copy-start(f32[64]{0:T(128)S(1)} %convert_element_type.235) | copy-start | bytes 772
  24.6 12.9 %copy-start.66 = (f32[64]{0:T(128)}, f32[64]{0:T(128)S(1)}, u32[]{:S(2)}) copy-start(f32[64]{0:T(128)S(1)} %convert_element_type.237) | copy-start | bytes 772
  24.9 6.0 copy-start.58
  24.9 8.0 %copy-start.63 = (s32[6]{0:T(128)}, s32[6]{0:T(128)S(1)}, u32[]{:S(2)}) copy-start(s32[6]{0:T(128)S(1)} %fusion.79) | copy-start | bytes 76
  32.5 15.7 %copy-start.26 = (bf16[1024,6,64]{0,1,2:T(8,128)(2,1)}, bf16[1024,6,64]{0,1,2:T(8,128)(2,1)S(1)}, u32[]{:S(2)}) copy-start(bf16[1024,6,64]{0,1,2:T(8,128)(2,1)S(1)} %fusion.29) | copy-start | bytes 2359300
  32.6 14.4 %copy-start.37 = (bf16[512,6,64]{0,1,2:T(8,128)(2,1)}, bf16[512,6,64]{0,1,2:T(8,128)(2,1)S(1)}, u32[]{:S(2)}) copy-start(bf16[512,6,64]{0,1,2:T(8,128)(2,1)S(1)} %slice.504) | copy-start | bytes 1179652
  35.4 197.4 %copy-start.46 = (f32[1024,6]{0,1:T(8,128)}, f32[1024,6]{0,1:T(8,128)S(1)}, u32[]{:S(2)}) copy-start(f32[1024,6]{0,1:T(8,128)S(1)} %add_rsqrt_fusion.1) | copy-start | bytes 73732
  40.7 6.2 copy-start.3
  52.4 34.0 %copy-start.32 = (bf16[1024,6,64]{0,2,1:T(8,128)(2,1)}, bf16[1024,6,64]{0,2,1:T(8,128)(2,1)S(1)}, u32[]{:S(2)}) copy-start(bf16[1024,6,64]{0,2,1:T(8,128)(2,1)S(1)} %maximum_convert_fusion) | copy-start | bytes 2359300
  52.4 32.7 %copy-start.69 = (bf16[2048]{0:T(1024)(128)(2,1)S(1)}, bf16[2048]{0:T(1024)(128)(2,1)}, u32[]{:S(2)}) copy-start(bf16[2048]{0:T(1024)(128)(2,1)} %param.35) | copy-start | bytes 12292
  102.4 260.3 %copy-start.56 = (f32[256]{0:T(256)}, f32[256]{0:T(256)S(1)}, u32[]{:S(2)}) copy-start(f32[256]{0:T(256)S(1)} %add_rsqrt_fusion.4) | copy-start | bytes 3076
  105.0 254.4 %reduce-scatter.5.cloned.1.call-start = ((), (), s32[]{:S(2)}) async-start(), calls=%async_computation.5 | async-start | bytes 5242880 | tf_op jit(solution)/shard_map/reduce_scatter | solution.py:481
  186.2 10.3 %copy-start.76 = (bf16[1024,2048]{1,0:T(8,128)(2,1)S(1)}, bf16[1024,2048]{1,0:T(8,128)(2,1)}, u32[]{:S(2)}) copy-start(bf16[1024,2048]{1,0:T(8,128)(2,1)} %all-gather.7.cloned.1.call-done) | copy-start | bytes 12582916
  196.5 9.7 %copy-start.42 = (bf16[1024,2048]{1,0:T(8,128)(2,1)S(1)}, bf16[1024,2048]{1,0:T(8,128)(2,1)}, u32[]{:S(2)}) copy-start(bf16[1024,2048]{1,0:T(8,128)(2,1)} %param.39) | copy-start | bytes 12582916
  196.5 22.4 %slice-start.6 = ((s8[4718592]{0:T(1024)(128)(4,1)}), s8[4194304]{0:T(1024)(128)(4,1)S(1)}, s32[]{:S(2)}) async-start(s8[4718592]{0:T(1024)(128)(4,1)} %bitcast.223), calls=%async_computation.14 | async-start | bytes 8388608
  196.5 28.1 %slice-start.8 = ((s8[4718592]{0:T(1024)(128)(4,1)}), s8[4194304]{0:T(1024)(128)(4,1)S(1)}, s32[]{:S(2)}) async-start(s8[4718592]{0:T(1024)(128)(4,1)} %bitcast.225), calls=%async_computation.16 | async-start | bytes 8388608
  206.2 12.7 %slice-start.7 = ((s8[4718592]{0:T(1024)(128)(4,1)}), s8[524288]{0:T(1024)(128)(4,1)S(1)}, s32[]{:S(2)}) async-start(s8[4718592]{0:T(1024)(128)(4,1)} %bitcast.223), calls=%async_computation.15 | async-start | bytes 1048576
  206.2 18.4 %slice-start.9 = ((s8[4718592]{0:T(1024)(128)(4,1)}), s8[524288]{0:T(1024)(128)(4,1)S(1)}, s32[]{:S(2)}) async-start(s8[4718592]{0:T(1024)(128)(4,1)} %bitcast.225), calls=%async_computation.17 | async-start | bytes 1048576
  218.9 5.6 copy-start.80
  219.0 5.7 copy-start.81
  232.0 266.3 %all-gather.9.cloned.1.call-start = ((), (), s32[]{:S(2)}) async-start(), calls=%async_computation.6 | async-start | bytes 6488064 | tf_op jit(solution)/shard_map/all_gather | solution.py:383
  232.7 306.7 %reduce-scatter.3.cloned.1.call-start = ((), (), s32[]{:S(2)}) async-start(), calls=%async_computation.4 | async-start | bytes 5242880 | tf_op jit(solution)/shard_map/reduce_scatter | solution.py:453
  238.0 172.1 %copy-start.52 = (f32[6,512]{1,0:T(8,128)}, f32[6,512]{1,0:T(8,128)S(1)}, u32[]{:S(2)}) copy-start(f32[6,512]{1,0:T(8,128)S(1)} %log_add_fusion.1) | copy-start | bytes 36868
  253.9 9.7 %copy-start.77 = (bf16[1024,2048]{1,0:T(8,128)(2,1)S(1)}, bf16[1024,2048]{1,0:T(8,128)(2,1)}, u32[]{:S(2)}) copy-start(bf16[1024,2048]{1,0:T(8,128)(2,1)} %all-gather.7.cloned.1.call-done) | copy-start | bytes 12582916
  253.9 9.7 %copy-start.82 = (bf16[1024,1152]{1,0:T(8,128)(2,1)S(1)}, bf16[1024,1152]{1,0:T(8,128)(2,1)}, u32[]{:S(2)}) copy-start(bf16[1024,1152]{1,0:T(8,128)(2,1)} %get-tuple-element.144) | copy-start | bytes 7077892
  359.1 209.1 %all-gather.11.cloned.1.call-start = ((), (), s32[]{:S(2)}) async-start(), calls=%async_computation.7 | async-start | bytes 5242880 | tf_op jit(solution)/shard_map/all_gather | solution.py:487
  401.5 6.0 copy-start.64
  409.3 8.0 %slice-start.3 = ((s8[6291456]{0:T(1024)(128)(4,1)}), s8[4194304]{0:T(1024)(128)(4,1)S(1)}, s32[]{:S(2)}) async-start(s8[6291456]{0:T(1024)(128)(4,1)} %bitcast.193), calls=%async_computation.11 | async-start | bytes 8388608
  410.1 7.3 %slice-start.4 = ((s8[6291456]{0:T(1024)(128)(4,1)}), s8[2097152]{0:T(1024)(128)(4,1)S(1)}, s32[]{:S(2)}) async-start(s8[6291456]{0:T(1024)(128)(4,1)} %bitcast.193), calls=%async_computation.12 | async-start | bytes 4194304
  417.4 5.6 copy-start.16
  417.4 7.0 %slice-start = ((s8[12582912]{0:T(1024)(128)(4,1)}), s8[4194304]{0:T(1024)(128)(4,1)S(1)}, s32[]{:S(2)}) async-start(s8[12582912]{0:T(1024)(128)(4,1)} %bitcast.191), calls=%async_computation.8 | async-start | bytes 8388608
  417.4 7.0 %slice-start.1 = ((s8[12582912]{0:T(1024)(128)(4,1)}), s8[4194304]{0:T(1024)(128)(4,1)S(1)}, s32[]{:S(2)}) async-start(s8[12582912]{0:T(1024)(128)(4,1)} %bitcast.191), calls=%async_computation.9 | async-start | bytes 8388608
  431.4 6.8 %copy-start.17 = (bf16[1024,6,32]{0,2,1:T(8,128)(2,1)S(1)}, bf16[1024,6,32]{0,2,1:T(8,128)(2,1)}, u32[]{:S(2)}) copy-start(bf16[1024,6,32]{0,2,1:T(8,128)(2,1)} %copy-done.15) | copy-start | bytes 1179652
  457.2 33.8 %copy-start.34 = (bf16[1024,384]{1,0:T(8,128)(2,1)}, bf16[1024,384]{1,0:T(8,128)(2,1)S(1)}, u32[]{:S(2)}) copy-start(bf16[1024,384]{1,0:T(8,128)(2,1)S(1)} %get-tuple-element.148) | copy-start | bytes 2359300
  498.2 5.2 copy-start.25
  504.2 26.3 %copy-start.50 = (bf16[1024,2,64]{0,2,1:T(8,128)(2,1)S(1)}, bf16[1024,2,64]{0,2,1:T(8,128)(2,1)}, u32[]{:S(2)}) copy-start(bf16[1024,2,64]{0,2,1:T(8,128)(2,1)} %copy.167) | copy-start | bytes 786436
  504.2 26.3 %copy-start.51 = (bf16[1024,2,64]{0,2,1:T(8,128)(2,1)S(1)}, bf16[1024,2,64]{0,2,1:T(8,128)(2,1)}, u32[]{:S(2)}) copy-start(bf16[1024,2,64]{0,2,1:T(8,128)(2,1)} %copy.164) | copy-start | bytes 786436
  504.2 26.3 %copy-start.71 = (f32[1024]{0:T(1024)S(1)}, f32[1024]{0:T(1024)}, u32[]{:S(2)}) copy-start(f32[1024]{0:T(1024)} %copy-done.70) | copy-start | bytes 12292
  539.5 28.8 %copy-start.33 = (bf16[1024,6,64]{0,2,1:T(8,128)(2,1)S(1)}, bf16[1024,6,64]{0,2,1:T(8,128)(2,1)}, u32[]{:S(2)}) copy-start(bf16[1024,6,64]{0,2,1:T(8,128)(2,1)} %copy-done.32) | copy-start | bytes 2359300
  600.7 13.6 %copy-start.49 = (f32[256,384]{1,0:T(8,128)S(1)}, f32[256,384]{1,0:T(8,128)}, u32[]{:S(2)}) copy-start(f32[256,384]{1,0:T(8,128)} %get-tuple-element.232) | copy-start | bytes 1179652
  610.9 6.5 %copy-start.41 = (f32[256,1152]{1,0:T(8,128)S(1)}, f32[256,1152]{1,0:T(8,128)}, u32[]{:S(2)}) copy-start(f32[256,1152]{1,0:T(8,128)} %get-tuple-element.239) | copy-start | bytes 3538948
  (51 other events, 142.7 us)
Sparse Core Ops, SparseCore 0:
  11.4 85.5 all-gather.4
  105.1 81.0 all-gather.6
  232.1 75.2 reduce-scatter.4
  310.7 81.7 all-gather.8
  394.6 77.7 reduce-scatter.2
  474.4 93.7 all-gather.10

commit v3 on v2

--- a/solution.py
+++ b/solution.py
@@ -380,13 +380,10 @@
         w_query, dp_index * (model_width // dp_size), model_width // dp_size, 0
     )
     w_out_full = lax.all_gather(out_piece, ("mp", "dp"), axis=0, tiled=True)
-    w_query_full = lax.all_gather(query_piece, ("mp", "dp"), axis=0, tiled=True).reshape(
-        mp_size, model_width, head_span
-    )
     doc_id, doc_pos, token_index = doc_layout(doc_lengths[0], row_count)
     cosine_tab, sine_tab = rope_table(doc_pos, head_size)
     x_float = tokens.astype(jnp.float32)
-    x_rows = lax.dynamic_slice_in_dim(x_float, row_first, shard_rows, 0)
+    x_rows = lax.dynamic_slice_in_dim(tokens, row_first, shard_rows, 0).astype(jnp.float32)
     gain_one = attn_gain.astype(jnp.float32)
     gain_two = ffn_gain.astype(jnp.float32)
     q_gain_f = q_gain.astype(jnp.float32)
@@ -440,61 +437,80 @@
     att_rows_all = exchange(attended.reshape(mp_size, shard_rows, head_span), 1)
     att_rows_cat = jnp.concatenate([att_rows_all[i] for i in range(mp_size)], axis=1)
     hidden_rows = x_rows + jnp.dot(att_rows_cat, w_out_full, preferred_element_type=jnp.float32)
-    xn_two = lax.all_gather(
-        (normalize(hidden_rows) * gain_two).astype(jnp.bfloat16), "mp", axis=0, tiled=True
-    )
+    chunks = 2
+    chunk_rows = shard_rows // chunks
+    xn_two_rows = (normalize(hidden_rows) * gain_two).astype(jnp.bfloat16)
+    grad_chunks = out_grad.reshape(mp_size, chunks, chunk_rows, model_width)
     live_cols = jnp.repeat(slot_live.astype(jnp.float32), tile_cols)
-    gate_act = jnp.dot(xn_two, w_gate, preferred_element_type=jnp.float32)
-    up_act = jnp.dot(xn_two, w_up, preferred_element_type=jnp.float32)
-    gate_sigmoid = jax.nn.sigmoid(gate_act)
-    gate_silu = gate_act * gate_sigmoid
-    ffn_hidden = (gate_silu * up_act * live_cols).astype(jnp.bfloat16)
-    ffn_part = jnp.dot(ffn_hidden, w_down, preferred_element_type=jnp.float32)
-    out_rows = hidden_rows + lax.psum_scatter(
-        ffn_part.astype(jnp.bfloat16), "mp", scatter_dimension=0, tiled=True
-    ).astype(jnp.float32)
-    block_out = out_rows.astype(jnp.bfloat16)
-    d_hidden = (
-        lax.dot_general(out_grad, w_down, CONTRACT_LAST, preferred_element_type=jnp.float32)
-        * live_cols
-    )
-    grad_down = lax.dot_general(
-        out_grad, ffn_hidden, CONTRACT_FIRST, preferred_element_type=jnp.float32
-    ).astype(jnp.bfloat16)
-    d_gate = (d_hidden * up_act * gate_sigmoid * (1.0 + gate_act * (1.0 - gate_sigmoid))).astype(
-        jnp.bfloat16
-    )
-    d_up = (d_hidden * gate_silu).astype(jnp.bfloat16)
-    grad_gate = lax.dot_general(
-        xn_two, d_gate, CONTRACT_FIRST, preferred_element_type=jnp.float32
-    ).astype(jnp.bfloat16)
-    grad_up = lax.dot_general(
-        xn_two, d_up, CONTRACT_FIRST, preferred_element_type=jnp.float32
-    ).astype(jnp.bfloat16)
-    grad_gate, grad_up, grad_down = reduce_rows(
-        (grad_gate, grad_up, grad_down), dp_size, 2
-    )
-    grad_down = grad_down.T
-    dn_two_part = lax.dot_general(
-        d_gate, w_gate, CONTRACT_LAST, preferred_element_type=jnp.float32
-    ) + lax.dot_general(d_up, w_up, CONTRACT_LAST, preferred_element_type=jnp.float32)
-    dn_two_rows = lax.psum_scatter(
-        dn_two_part.astype(jnp.bfloat16), "mp", scatter_dimension=0, tiled=True
-    ).astype(jnp.float32)
+    pieces = []
+    for chunk in range(chunks):
+        xn_two = lax.all_gather(
+            xn_two_rows[chunk * chunk_rows : (chunk + 1) * chunk_rows], "mp", axis=0, tiled=True
+        )
+        grad_chunk = grad_chunks[:, chunk].reshape(mp_size * chunk_rows, model_width)
+        gate_act = jnp.dot(xn_two, w_gate, preferred_element_type=jnp.float32)
+        up_act = jnp.dot(xn_two, w_up, preferred_element_type=jnp.float32)
+        gate_sigmoid = jax.nn.sigmoid(gate_act)
+        gate_silu = gate_act * gate_sigmoid
+        ffn_hidden = (gate_silu * up_act * live_cols).astype(jnp.bfloat16)
+        d_hidden = (
+            lax.dot_general(grad_chunk, w_down, CONTRACT_LAST, preferred_element_type=jnp.float32)
+            * live_cols
+        )
+        d_gate = (
+            d_hidden * up_act * gate_sigmoid * (1.0 + gate_act * (1.0 - gate_sigmoid))
+        ).astype(jnp.bfloat16)
+        d_up = (d_hidden * gate_silu).astype(jnp.bfloat16)
+        dn_two_part = lax.dot_general(
+            d_gate, w_gate, CONTRACT_LAST, preferred_element_type=jnp.float32
+        ) + lax.dot_general(d_up, w_up, CONTRACT_LAST, preferred_element_type=jnp.float32)
+        dn_two_chunk = lax.psum_scatter(
+            dn_two_part.astype(jnp.bfloat16), "mp", scatter_dimension=0, tiled=True
+        )
+        pieces.append((xn_two, grad_chunk, ffn_hidden, d_gate, d_up, dn_two_chunk))
+    xn_two, grad_cat, ffn_hidden, d_gate, d_up, dn_two_rows = (
+        jnp.concatenate(parts, axis=0) for parts in zip(*pieces)
+    )
+    dn_two_rows = dn_two_rows.astype(jnp.float32)
     back_two, grad_gain_two = norm_back(dn_two_rows, hidden_rows, gain_two)
     g_rows = lax.dynamic_slice_in_dim(out_grad, row_first, shard_rows, 0)
     dh_rows = g_rows.astype(jnp.float32) + back_two
-    dh_low = lax.all_gather(dh_rows.astype(jnp.bfloat16), "mp", axis=0, tiled=True)
-    grad_out_proj = lax.dot_general(
-        dh_low, attended, CONTRACT_FIRST, preferred_element_type=jnp.float32
-    ).astype(jnp.bfloat16)
+    dh_rows_low = dh_rows.astype(jnp.bfloat16)
+    dh_low = lax.all_gather(dh_rows_low, "mp", axis=0, tiled=True)
+    query_piece, _ = lax.optimization_barrier((query_piece, dh_rows_low))
+    w_query_full = lax.all_gather(query_piece, ("mp", "dp"), axis=0, tiled=True).reshape(
+        mp_size, model_width, head_span
+    )
     d_att_rows = lax.dot_general(
-        dh_rows.astype(jnp.bfloat16), w_out_full, CONTRACT_LAST, preferred_element_type=jnp.float32
+        dh_rows_low, w_out_full, CONTRACT_LAST, preferred_element_type=jnp.float32
     ).astype(jnp.bfloat16)
     d_att_blocks = jnp.stack(
         [d_att_rows[:, i * head_span : (i + 1) * head_span] for i in range(mp_size)]
     )
-    d_att = exchange(d_att_blocks, 3).reshape(row_count, heads_dev, head_size)
+    d_att = exchange(d_att_blocks, 3)
+    xn_two, grad_cat, _ = lax.optimization_barrier((xn_two, grad_cat, d_att))
+    d_att = d_att.reshape(row_count, heads_dev, head_size)
+    grad_down = lax.dot_general(
+        grad_cat, ffn_hidden, CONTRACT_FIRST, preferred_element_type=jnp.float32
+    ).astype(jnp.bfloat16)
+    grad_gate = lax.dot_general(
+        xn_two, d_gate, CONTRACT_FIRST, preferred_element_type=jnp.float32
+    ).astype(jnp.bfloat16)
+    grad_up = lax.dot_general(
+        xn_two, d_up, CONTRACT_FIRST, preferred_element_type=jnp.float32
+    ).astype(jnp.bfloat16)
+    grad_gate, grad_up, grad_down = reduce_rows(
+        (grad_gate, grad_up, grad_down), dp_size, 2
+    )
+    grad_down = grad_down.T
+    ffn_part = jnp.dot(
+        ffn_hidden, w_down, preferred_element_type=jnp.float32
+    ).astype(jnp.bfloat16)
+    ffn_part = ffn_part.reshape(chunks, mp_size, chunk_rows, model_width).swapaxes(0, 1)
+    out_rows = hidden_rows + lax.psum_scatter(
+        ffn_part.reshape(row_count, model_width), "mp", scatter_dimension=0, tiled=True
+    ).astype(jnp.float32)
+    block_out = out_rows.astype(jnp.bfloat16)
     dq_blocks = []
     d_keys = jnp.zeros((row_count, heads_dev, head_size), jnp.float32)
     d_values = jnp.zeros((row_count, heads_dev, head_size), jnp.float32)
@@ -557,6 +573,9 @@
         )
     back_one, grad_gain_one = norm_back(dn_one_rows, x_rows, gain_one)
     grad_tokens = dh_rows + back_one
+    grad_out_proj = lax.dot_general(
+        dh_low, attended, CONTRACT_FIRST, preferred_element_type=jnp.float32
+    ).astype(jnp.bfloat16)
     grad_query = lax.dot_general(
         xn_one, dq_low, CONTRACT_FIRST, preferred_element_type=jnp.float32
     ).astype(jnp.bfloat16)

time: 635 us -> 673 us (1.060)
  waiting for transfers between devices: 114 us -> 141 us
  Pallas kernels: 215 us -> 240 us
  matrix products: 170 us -> 157 us
    reduce_scatter x1 -> x2, waiting for transfers between devices: 0.02 us -> 65.7 us  [shards(): lax.psum_scatter(dn_two_part.astype(jnp.bfloat16), 'mp', scatter_dimensio...]
    all_gather x2 -> x3, waiting for transfers between devices: 103 us -> 64.9 us  [the longest x2 64.9 us: shards(): lax.all_gather(xn_two_rows[chunk * chunk_rows:(chunk + 1) * chunk_rows],...]
    pallas_call x4, Pallas kernels: 92.9 us -> 125 us  [exchange(): pl.pallas_call(functools.partial(exchange_kernel, size), out_shape=jax.Sh...]
    concatenate x0 -> x2, other arithmetic: none -> 10.4 us  [shards(): jnp.concatenate(parts, axis=0)]
    dot_general x4 -> x5, matrix products: 36.5 us -> 28.3 us  [the longest x2 9.66 us: shards(): lax.dot_general(grad_chunk, w_down, CONTRACT_LAST, preferred_element_type...]
    pallas_call x1, Pallas kernels: 19 us -> 11.3 us  [sum_everywhere(): pl.pallas_call(functools.partial(sum_kernel, mp_size, dp_size), out_shape...]
    convert_element_type x3 -> x2, other arithmetic: 10.3 us -> 3.14 us  [the longest x1 2.9 us: shards(): dh_rows_low = dh_rows.astype(jnp.bfloat16)]
  transfers between devices with their start and end apart: 6 -> 8, of which waited for: 3 -> 5; matrix products, arithmetic and copies ran while one was open for 33% -> 36% of each run, Pallas kernels for 29% -> 36%
where the time goes in v3:
time: 673 us; the launch traced here: 663 us
  Pallas kernels  240 us (36%)
  matrix products  157 us (23%)
  waiting for transfers between devices  141 us (21%)
  other arithmetic  59.5 us (9%)
  local copies, waits for them, and re-layouts  48.4 us (7%)
  between operations  16.5 us (2%)
    pallas_call x4, Pallas kernels, exchange(): pl.pallas_call(functools.partial(exchange_kernel, size), out_shape=jax.Sh...  125 us
    pallas_call x2, Pallas kernels, reduce_rows(): pl.pallas_call(functools.partial(reduce_kernel, size, splits, count), out...  103 us
    reduce_scatter x2, waiting for transfers between devices, shards(): lax.psum_scatter(dn_two_part.astype(jnp.bfloat16), 'mp', scatter_dimensio...  65.7 us
    all_gather x2, waiting for transfers between devices, shards(): lax.all_gather(xn_two_rows[chunk * chunk_rows:(chunk + 1) * chunk_rows],...  64.9 us
  transfers between devices with their start and end apart: 8, of which 5 were waited for; matrix products, arithmetic and copies ran while one was open for 36% of the time, Pallas kernels for 36%

profile of v3, /device:TPU:0, one launch (start us, length us, event | category | flops | bytes accessed | tf_op | source)
XLA Modules:
  0.0 663.0 jit_solution(3377411605987759736)
XLA Ops:
  9.9 3.3 fusion.2
  13.2 3.5 fusion.117
  21.2 3.9 fusion.59
  38.4 2.9 fusion
  43.0 3.6 fusion.55
  48.8 30.0 %exchange_1.1 = bf16[4,256,384]{2,1,0:T(8,128)(2,1)} custom-call(bf16[4,256,384]{2,1,0:T(8,128)(2,1)} %copy.152.data_ref), custom_call_target="tpu_custom_call" | custom-call | bytes 12582912 | tf_op jit(solution)/shard_map/exchange_1/pallas_call | solution.py:51
  80.1 9.9 %all-gather.6.cloned.1.call-done = bf16[1536,2048]{1,0:T(8,128)(2,1)} async-done(((bf16[48,2048]{1,0:T(8,128)(2,1)}), bf16[1536,2048]{1,0:T(8,128)(2,1)}) %all-gather.6.cloned.1.call-update) | async-done | bytes 6291472 | tf_op jit(solution)/shard_map/all_gather | solution.py:382
  90.0 5.0 multiply_reduce_fusion.2
  96.8 4.7 fusion.120
  102.0 42.2 %all-gather.8.cloned.1.call-done = bf16[512,2048]{1,0:T(8,128)(2,1)} async-done(((bf16[128,2048]{1,0:T(8,128)(2,1)}), bf16[512,2048]{1,0:T(8,128)(2,1)}) %all-gather.8.cloned.1.call-update) | async-done | bytes 2097168 | tf_op jit(solution)/shard_map/all_gather | solution.py:447
  144.3 6.0 fusion.128
  150.3 5.6 fusion.129
  156.0 4.8 multiply_convert_fusion.4
  160.8 2.9 fusion.132
  163.8 4.1 add_convert_fusion.1
  168.2 22.7 %all-gather.10.cloned.1.call-done = bf16[512,2048]{1,0:T(8,128)(2,1)} async-done(((bf16[128,2048]{1,0:T(8,128)(2,1)}), bf16[512,2048]{1,0:T(8,128)(2,1)}) %all-gather.10.cloned.1.call-update) | async-done | bytes 2097168 | tf_op jit(solution)/shard_map/all_gather | solution.py:447
  190.9 6.0 fusion.130
  196.9 5.7 fusion.131
  202.7 4.8 multiply_convert_fusion.2
  207.6 2.9 fusion.133
  210.5 4.2 add_convert_fusion
  214.8 20.7 %reduce-scatter.6.cloned.1.call-done = bf16[128,2048]{1,0:T(8,128)(2,1)} async-done(((bf16[512,2048]{1,0:T(8,128)(2,1)}), bf16[128,2048]{1,0:T(8,128)(2,1)}) %reduce-scatter.6.cloned.1.call-update) | async-done | bytes 524304 | tf_op jit(solution)/shard_map/reduce_scatter | solution.py:467
  235.5 45.0 %reduce-scatter.8.cloned.1.call-done = bf16[128,2048]{1,0:T(8,128)(2,1)} async-done(((bf16[512,2048]{1,0:T(8,128)(2,1)}), bf16[128,2048]{1,0:T(8,128)(2,1)}) %reduce-scatter.8.cloned.1.call-update) | async-done | bytes 524304 | tf_op jit(solution)/shard_map/reduce_scatter | solution.py:467
  283.3 2.9 fusion.114
  290.8 5.5 pad_maximum_fusion.1
  297.1 6.5 convolution_convert_fusion.3
  305.9 4.9 pad_maximum_fusion
  310.8 4.7 convolution_convert_fusion.7
  316.6 29.4 %exchange_3.1 = bf16[4,256,384]{2,1,0:T(8,128)(2,1)} custom-call(bf16[4,256,384]{2,1,0:T(8,128)(2,1)} %pad_maximum_fusion.11.data_ref), custom_call_target="tpu_custom_call" | custom-call | bytes 12582912 | tf_op jit(solution)/shard_map/exchange_3/pallas_call | solution.py:51
  346.1 9.7 %convolution_convert_fusion.1 = bf16[2048,1152]{1,0:T(8,128)(2,1)} fusion(bf16[1024,2048]{1,0:T(8,128)(2,1)} %pad_maximum_fusion, bf16[512,1152]{1,0:T(8,128)(2,1)} %copy-done.77, bf16[512,1152]{1,0:T(8,128)(2,1)} %copy-done.76), kind=kOutput, calls=%fused_computation.14 | convolution fusion | flops 4838916096 | bytes 11272192 | tf_op jit(solution)/shard_map/dot_general | solution.py:499
  355.8 7.5 %convolution_convert_fusion.2 = bf16[2048,1152]{1,0:T(8,128)(2,1)} fusion(bf16[1024,2048]{1,0:T(8,128)(2,1)S(1)} %copy-done.33, bf16[512,1152]{1,0:T(8,128)(2,1)S(1)} %copy-done.75, bf16[512,1152]{1,0:T(8,128)(2,1)S(1)} %copy-done.73), kind=kOutput, calls=%fused_computation.15 | convolution fusion | flops 4838916096 | bytes 11272192 | tf_op jit(solution)/shard_map/dot_general | solution.py:496
  365.4 4.6 multiply_reduce_fusion.1
  370.0 4.7 multiply_convert_fusion.1
  381.5 7.4 %convolution_convert_fusion = bf16[2048,1152]{1,0:T(8,128)(2,1)} fusion(bf16[1024,2048]{1,0:T(8,128)(2,1)S(1)} %copy-done.32, bf16[512,1152]{1,0:T(8,128)(2,1)S(1)} %copy-done.81, bf16[512,1152]{1,0:T(8,128)(2,1)S(1)} %copy-done.79), kind=kOutput, calls=%fused_computation.13 | convolution fusion | flops 4838916096 | bytes 11272192 | tf_op jit(solution)/shard_map/dot_general | solution.py:493
  389.8 6.7 %multiply_reduce_fusion = (f32[6,512]{1,0:T(8,128)S(1)}, f32[6,512,1024]{2,1,0:T(8,128)S(1)}) fusion(f32[6,512,1024]{2,1,0:T(8,128)} %copy-done.2, f32[6,512]{1,0:T(8,128)S(1)} %log_add_fusion, bf16[512,6,64]{0,2,1:T(8,128)(2,1)S(1)} %slice.452, bf16[1024,6,64]{0,1,2:T(8,128)(2,1)S(1)} %copy-done.25), kind=kOutput, calls=%fused_computation.1 | convolution fusion | flops 412087296 | bytes 26370048 | tf_op jit(solution)/shard_map/qhe,khe->hqk/dot_general | solution.py:523
  396.5 6.4 multiply_convert_fusion
  426.0 76.8 %reduce_rows_2.1 = (f32[256,1152]{1,0:T(8,128)}, f32[256,1152]{1,0:T(8,128)}, f32[256,1152]{1,0:T(8,128)}) custom-call(bf16[8,256,1152]{2,1,0:T(8,128)(2,1)} %bitcast.219, bf16[8,256,1152]{2,1,0:T(8,128)(2,1)} %bitcast.218, bf16[8,256,1152]{2,1,0:T(8,128)(2,1)} %bitcast.220), custom_call_target="tpu_custom_call" | custom-call | bytes 84934656 | tf_op jit(solution)/shard_map/reduce_rows_2/pallas_call | solution.py:249
  505.5 51.5 %exchange_4.1 = bf16[4,256,640]{2,1,0:T(8,128)(2,1)} custom-call(bf16[4,256,640]{2,1,0:T(8,128)(2,1)} %pad_maximum_fusion.7.data_ref), custom_call_target="tpu_custom_call" | custom-call | bytes 20971520 | tf_op jit(solution)/shard_map/exchange_4/pallas_call | solution.py:51
  559.4 4.4 fusion.134
  563.8 2.8 convolution_convert_fusion.6
  566.6 3.8 convolution_convert_fusion.4
  570.4 5.7 convolution_convert_fusion.5
  576.2 26.7 %reduce_rows_5.1 = (f32[256,384]{1,0:T(8,128)}, f32[256,384]{1,0:T(8,128)}, f32[256,256]{1,0:T(8,128)}) custom-call(bf16[8,256,384]{2,1,0:T(8,128)(2,1)} %bitcast.225, bf16[8,256,384]{2,1,0:T(8,128)(2,1)} %bitcast.224, bf16[8,256,256]{2,1,0:T(8,128)(2,1)} %bitcast.228), custom_call_target="tpu_custom_call" | custom-call | bytes 25165824 | tf_op jit(solution)/shard_map/reduce_rows_5/pallas_call | solution.py:249
  604.6 13.9 %exchange_6.1 = bf16[4,64,256]{2,1,0:T(8,128)(2,1)} custom-call(bf16[4,64,256]{2,1,0:T(8,128)(2,1)} %bitcast.233), custom_call_target="tpu_custom_call" | custom-call | bytes 2097152 | tf_op jit(solution)/shard_map/exchange_6/pallas_call | solution.py:51
  622.7 3.0 convolution_add_fusion.3
  628.6 3.6 fusion.36
  632.9 11.3 %sum_everywhere_7.1 = f32[40,128]{1,0:T(8,128)} custom-call(f32[40,128]{1,0:T(8,128)} %pad_bitcast_fusion.data_ref), custom_call_target="tpu_custom_call" | custom-call | tf_op jit(solution)/shard_map/sum_everywhere_7/pallas_call | solution.py:121
  646.9 6.0 fusion.35
  (358 shorter events, 91.8 us)
Async XLA Ops:
  7.2 6.0 copy-start
  7.2 82.8 %all-gather.6.cloned.1.call-start = ((), (), s32[]{:S(2)}) async-start(), calls=%async_computation.3 | async-start | bytes 6488064 | tf_op jit(solution)/shard_map/all_gather | solution.py:382
  9.0 135.3 %all-gather.8.cloned.1.call-start = ((), (), s32[]{:S(2)}) async-start(), calls=%async_computation.4 | async-start | bytes 2621440 | tf_op jit(solution)/shard_map/all_gather | solution.py:447
  9.9 11.3 %copy-start.56 = (f32[2048]{0:T(1024)}, f32[2048]{0:T(1024)S(1)}, u32[]{:S(2)}) copy-start(f32[2048]{0:T(1024)S(1)} %convert_element_type.242) | copy-start | bytes 24580
  13.2 8.0 %copy-start.64 = (f32[1024]{0:T(1024)}, f32[1024]{0:T(1024)S(1)}, u32[]{:S(2)}) copy-start(f32[1024]{0:T(1024)S(1)} %add_rsqrt_fusion.2) | copy-start | bytes 12292
  18.7 13.0 %copy-start.8 = (f32[1024,384]{0,1:T(8,128)}, f32[1024,384]{0,1:T(8,128)S(1)}, u32[]{:S(2)}) copy-start(f32[1024,384]{0,1:T(8,128)S(1)} %copy.146) | copy-start | bytes 4718596
  18.7 13.0 %copy-start.61 = (f32[64]{0:T(128)}, f32[64]{0:T(128)S(1)}, u32[]{:S(2)}) copy-start(f32[64]{0:T(128)S(1)} %convert_element_type.249) | copy-start | bytes 772
  18.8 13.0 %copy-start.66 = (f32[64]{0:T(128)}, f32[64]{0:T(128)S(1)}, u32[]{:S(2)}) copy-start(f32[64]{0:T(128)S(1)} %convert_element_type.247) | copy-start | bytes 772
  19.0 6.2 copy-start.58
  19.0 8.2 %copy-start.59 = (s32[6]{0:T(128)}, s32[6]{0:T(128)S(1)}, u32[]{:S(2)}) copy-start(s32[6]{0:T(128)S(1)} %fusion.97) | copy-start | bytes 76
  26.8 15.7 %copy-start.24 = (bf16[1024,6,64]{0,1,2:T(8,128)(2,1)}, bf16[1024,6,64]{0,1,2:T(8,128)(2,1)S(1)}, u32[]{:S(2)}) copy-start(bf16[1024,6,64]{0,1,2:T(8,128)(2,1)S(1)} %fusion.47) | copy-start | bytes 2359300
  26.8 14.4 %copy-start.45 = (bf16[512,6,64]{0,1,2:T(8,128)(2,1)}, bf16[512,6,64]{0,1,2:T(8,128)(2,1)S(1)}, u32[]{:S(2)}) copy-start(bf16[512,6,64]{0,1,2:T(8,128)(2,1)S(1)} %slice.520) | copy-start | bytes 1179652
  35.0 6.2 copy-start.3
  46.7 32.1 %copy-start.39 = (bf16[1024,6,64]{0,2,1:T(8,128)(2,1)}, bf16[1024,6,64]{0,2,1:T(8,128)(2,1)S(1)}, u32[]{:S(2)}) copy-start(bf16[1024,6,64]{0,2,1:T(8,128)(2,1)S(1)} %maximum_convert_fusion) | copy-start | bytes 2359300
  46.7 32.1 %copy-start.63 = (bf16[2048]{0:T(1024)(128)(2,1)S(1)}, bf16[2048]{0:T(1024)(128)(2,1)}, u32[]{:S(2)}) copy-start(bf16[2048]{0:T(1024)(128)(2,1)} %param.35) | copy-start | bytes 12292
  96.7 94.2 %all-gather.10.cloned.1.call-start = ((), (), s32[]{:S(2)}) async-start(), calls=%async_computation.5 | async-start | bytes 2621440 | tf_op jit(solution)/shard_map/all_gather | solution.py:447
  101.6 133.9 %reduce-scatter.6.cloned.1.call-start = ((), (), s32[]{:S(2)}) async-start(), calls=%async_computation.7 | async-start | bytes 2621440 | tf_op jit(solution)/shard_map/reduce_scatter | solution.py:467
  144.3 11.7 %slice-start.14 = ((s8[4718592]{0:T(1024)(128)(4,1)}), s8[4194304]{0:T(1024)(128)(4,1)S(1)}, s32[]{:S(2)}) async-start(s8[4718592]{0:T(1024)(128)(4,1)} %bitcast.249), calls=%async_computation.25 | async-start | bytes 8388608
  150.3 10.6 %slice-start.6 = ((s8[4718592]{0:T(1024)(128)(4,1)}), s8[4194304]{0:T(1024)(128)(4,1)S(1)}, s32[]{:S(2)}) async-start(s8[4718592]{0:T(1024)(128)(4,1)} %bitcast.241), calls=%async_computation.17 | async-start | bytes 8388608
  150.3 13.5 %slice-start.10 = ((s8[4718592]{0:T(1024)(128)(4,1)}), s8[4194304]{0:T(1024)(128)(4,1)S(1)}, s32[]{:S(2)}) async-start(s8[4718592]{0:T(1024)(128)(4,1)} %bitcast.245), calls=%async_computation.21 | async-start | bytes 8388608
  156.0 7.8 %slice-start.11 = ((s8[4718592]{0:T(1024)(128)(4,1)}), s8[524288]{0:T(1024)(128)(4,1)S(1)}, s32[]{:S(2)}) async-start(s8[4718592]{0:T(1024)(128)(4,1)} %bitcast.245), calls=%async_computation.22 | async-start | bytes 1048576
  168.0 112.5 %reduce-scatter.8.cloned.1.call-start = ((), (), s32[]{:S(2)}) async-start(), calls=%async_computation.8 | async-start | bytes 2621440 | tf_op jit(solution)/shard_map/reduce_scatter | solution.py:467
  190.9 11.7 %slice-start.16 = ((s8[4718592]{0:T(1024)(128)(4,1)}), s8[4194304]{0:T(1024)(128)(4,1)S(1)}, s32[]{:S(2)}) async-start(s8[4718592]{0:T(1024)(128)(4,1)} %bitcast.251), calls=%async_computation.27 | async-start | bytes 8388608
  196.9 10.6 %slice-start.8 = ((s8[4718592]{0:T(1024)(128)(4,1)}), s8[4194304]{0:T(1024)(128)(4,1)S(1)}, s32[]{:S(2)}) async-start(s8[4718592]{0:T(1024)(128)(4,1)} %bitcast.243), calls=%async_computation.19 | async-start | bytes 8388608
  196.9 13.6 %slice-start.12 = ((s8[4718592]{0:T(1024)(128)(4,1)}), s8[4194304]{0:T(1024)(128)(4,1)S(1)}, s32[]{:S(2)}) async-start(s8[4718592]{0:T(1024)(128)(4,1)} %bitcast.247), calls=%async_computation.23 | async-start | bytes 8388608
  202.7 7.8 %slice-start.13 = ((s8[4718592]{0:T(1024)(128)(4,1)}), s8[524288]{0:T(1024)(128)(4,1)S(1)}, s32[]{:S(2)}) async-start(s8[4718592]{0:T(1024)(128)(4,1)} %bitcast.247), calls=%async_computation.24 | async-start | bytes 1048576
  214.7 355.7 %all-gather.14.cloned.1.call-start = ((), (), s32[]{:S(2)}) async-start(), calls=%async_computation.10 | async-start | bytes 5242880 | tf_op jit(solution)/shard_map/all_gather | solution.py:479
  235.5 47.8 %copy-start.27 = (bf16[128,2048]{1,0:T(8,128)(2,1)S(1)}, bf16[128,2048]{1,0:T(8,128)(2,1)}, u32[]{:S(2)}) copy-start(bf16[128,2048]{1,0:T(8,128)(2,1)} %reduce-scatter.6.cloned.1.call-done) | copy-start | bytes 1572868
  286.2 336.4 %all-gather.12.cloned.1.call-start = ((), (), s32[]{:S(2)}) async-start(), calls=%async_computation.9 | async-start | bytes 6488064 | tf_op jit(solution)/shard_map/all_gather | solution.py:481
  287.0 359.9 %reduce-scatter.4.cloned.1.call-start = ((), (), s32[]{:S(2)}) async-start(), calls=%async_computation.6 | async-start | bytes 5242880 | tf_op jit(solution)/shard_map/reduce_scatter | solution.py:510
  287.3 9.0 %slice-start.18 = ((s8[4718592]{0:T(1024)(128)(4,1)}), s8[524288]{0:T(1024)(128)(4,1)S(1)}, s32[]{:S(2)}) async-start(s8[4718592]{0:T(1024)(128)(4,1)} %bitcast.253), calls=%async_computation.29 | async-start | bytes 1048576
  290.8 6.3 copy-start.80
  346.0 9.7 %copy-start.33 = (bf16[1024,2048]{1,0:T(8,128)(2,1)S(1)}, bf16[1024,2048]{1,0:T(8,128)(2,1)}, u32[]{:S(2)}) copy-start(bf16[1024,2048]{1,0:T(8,128)(2,1)} %pad_maximum_fusion) | copy-start | bytes 12582916
  346.0 9.7 %copy-start.73 = (bf16[512,1152]{1,0:T(8,128)(2,1)S(1)}, bf16[512,1152]{1,0:T(8,128)(2,1)}, u32[]{:S(2)}) copy-start(bf16[512,1152]{1,0:T(8,128)(2,1)} %copy-done.72) | copy-start | bytes 3538948
  346.1 9.7 %copy-start.75 = (bf16[512,1152]{1,0:T(8,128)(2,1)S(1)}, bf16[512,1152]{1,0:T(8,128)(2,1)}, u32[]{:S(2)}) copy-start(bf16[512,1152]{1,0:T(8,128)(2,1)} %copy-done.74) | copy-start | bytes 3538948
  355.8 7.5 %copy-start.41 = (bf16[4,256,384]{2,1,0:T(8,128)(2,1)S(1)}, bf16[4,256,384]{2,1,0:T(8,128)(2,1)}, u32[]{:S(2)}) copy-start(bf16[4,256,384]{2,1,0:T(8,128)(2,1)} %exchange_3.1) | copy-start | bytes 2359300
  365.4 12.9 %slice-start.3 = ((s8[6291456]{0:T(1024)(128)(4,1)}), s8[4194304]{0:T(1024)(128)(4,1)S(1)}, s32[]{:S(2)}) async-start(s8[6291456]{0:T(1024)(128)(4,1)} %bitcast.204), calls=%async_computation.14 | async-start | bytes 8388608
  370.0 8.3 %slice-start.4 = ((s8[6291456]{0:T(1024)(128)(4,1)}), s8[2097152]{0:T(1024)(128)(4,1)S(1)}, s32[]{:S(2)}) async-start(s8[6291456]{0:T(1024)(128)(4,1)} %bitcast.204), calls=%async_computation.15 | async-start | bytes 4194304
  381.5 7.5 %copy-start.47 = (bf16[2,256,384]{2,1,0:T(8,128)(2,1)S(1)}, bf16[2,256,384]{2,1,0:T(8,128)(2,1)}, u32[]{:S(2)}) copy-start(bf16[2,256,384]{2,1,0:T(8,128)(2,1)} %get-tuple-element.186) | copy-start | bytes 1179652
  381.5 8.3 %copy-start.25 = (bf16[1024,6,64]{0,1,2:T(8,128)(2,1)S(1)}, bf16[1024,6,64]{0,1,2:T(8,128)(2,1)}, u32[]{:S(2)}) copy-start(bf16[1024,6,64]{0,1,2:T(8,128)(2,1)} %copy-done.24) | copy-start | bytes 2359300
  389.8 6.7 %copy-start.34 = (bf16[512,6,64]{0,2,1:T(8,128)(2,1)}, bf16[512,6,64]{0,2,1:T(8,128)(2,1)S(1)}, u32[]{:S(2)}) copy-start(bf16[512,6,64]{0,2,1:T(8,128)(2,1)S(1)} %slice.452) | copy-start | bytes 1179652
  405.0 6.7 %slice-start = ((s8[12582912]{0:T(1024)(128)(4,1)}), s8[4194304]{0:T(1024)(128)(4,1)S(1)}, s32[]{:S(2)}) async-start(s8[12582912]{0:T(1024)(128)(4,1)} %bitcast.202), calls=%async_computation.11 | async-start | bytes 8388608
  405.0 6.7 %slice-start.1 = ((s8[12582912]{0:T(1024)(128)(4,1)}), s8[4194304]{0:T(1024)(128)(4,1)S(1)}, s32[]{:S(2)}) async-start(s8[12582912]{0:T(1024)(128)(4,1)} %bitcast.202), calls=%async_computation.12 | async-start | bytes 8388608
  602.8 19.8 %copy-start.26 = (bf16[4,256,640]{2,1,0:T(8,128)(2,1)S(1)}, bf16[4,256,640]{2,1,0:T(8,128)(2,1)}, u32[]{:S(2)}) copy-start(bf16[4,256,640]{2,1,0:T(8,128)(2,1)} %exchange_4.1) | copy-start | bytes 3932164
  628.6 18.3 %copy-start.28 = (bf16[128,2048]{1,0:T(8,128)(2,1)S(1)}, bf16[128,2048]{1,0:T(8,128)(2,1)}, u32[]{:S(2)}) copy-start(bf16[128,2048]{1,0:T(8,128)(2,1)} %reduce-scatter.6.cloned.1.call-done) | copy-start | bytes 1572868
  628.6 18.3 %copy-start.30 = (bf16[128,2048]{1,0:T(8,128)(2,1)S(1)}, bf16[128,2048]{1,0:T(8,128)(2,1)}, u32[]{:S(2)}) copy-start(bf16[128,2048]{1,0:T(8,128)(2,1)} %reduce-scatter.8.cloned.1.call-done) | copy-start | bytes 1572868
  646.9 6.1 copy-start.55
  646.9 6.8 %copy-start.51 = (f32[256,1152]{1,0:T(8,128)S(1)}, f32[256,1152]{1,0:T(8,128)}, u32[]{:S(2)}) copy-start(f32[256,1152]{1,0:T(8,128)} %get-tuple-element.251) | copy-start | bytes 3538948
  (62 other events, 199.8 us)
Sparse Core Ops, SparseCore 0:
  11.4 78.5 all-gather.5
  96.8 47.4 all-gather.7
  146.4 44.4 all-gather.9
  193.0 42.4 reduce-scatter.5
  237.6 42.8 reduce-scatter.7
  286.3 96.4 all-gather.13
  385.7 67.6 all-gather.11
  455.7 96.2 reduce-scatter.3

commit v4 on v3

--- a/solution.py
+++ b/solution.py
@@ -134,10 +134,12 @@
     )(data)
 
 
-def reduce_kernel(size, splits, count, *refs):
-    data_refs, out_refs = refs[:count], refs[count : 2 * count]
-    recv_refs, sums_refs = refs[2 * count : 3 * count], refs[3 * count : 4 * count]
-    send_sem, recv_sem = refs[4 * count :]
+def reduce_kernel(size, splits, count, lefts, lhs_count, *refs):
+    lhs_refs, refs = refs[:lhs_count], refs[lhs_count:]
+    rhs_refs, out_refs = refs[:count], refs[count : 2 * count]
+    data_refs, refs = refs[2 * count : 3 * count], refs[3 * count :]
+    recv_refs, sums_refs = refs[:count], refs[count : 2 * count]
+    send_sem, recv_sem = refs[2 * count :]
     here = lax.axis_index("dp")
     masks = [1 << index for index in range(size.bit_length() - 1)]
     bit_of = {mask: (here // mask) % 2 for mask in masks}
@@ -165,10 +167,12 @@
             items.append((index, split * rows, rows, order))
     copies = {}
 
-    def start(item, stage, source_of):
+    def start(item, stage, source_of, only=None):
         index, first_row, rows, order = items[item]
         mask = order[stage]
         for offset in range(size):
+            if only is not None and offset != only:
+                continue
             if offset & mask and not any(offset & done for done in order[:stage]):
                 source = source_of(offset)
                 copy = pltpu.make_async_remote_copy(
@@ -205,13 +209,44 @@
 
         lax.fori_loop(0, rows // step, body, 0)
 
-    for item in range(len(items)):
-        index, first_row, rows, order = items[item]
-        start(
-            item,
-            0,
-            lambda offset: data_refs[index].at[relative(offset), pl.ds(first_row, rows)],
-        )
+    block_rows = data_refs[0].shape[1]
+
+    def multiply(offset, index):
+        place = here
+        for mask in masks:
+            place = place + ((offset // mask) % 2) * (mask - 2 * mask * bit_of[mask])
+        columns = pl.ds(pl.multiple_of(place * block_rows, block_rows), block_rows)
+        data_refs[index][place] = lax.dot_general(
+            lhs_refs[lefts[index]][:, columns],
+            rhs_refs[index][...],
+            CONTRACT_FIRST,
+            preferred_element_type=jnp.float32,
+        ).astype(jnp.bfloat16)
+
+    def start_first(offset):
+        for item in range(len(items)):
+            index, first_row, rows, order = items[item]
+            start(
+                item,
+                0,
+                lambda offset: data_refs[index].at[relative(offset), pl.ds(first_row, rows)],
+                offset,
+            )
+
+    for offset in range(1, size, 2):
+        for index in range(count):
+            multiply(offset, index)
+        if offset > 1:
+            start_first(offset - 2)
+
+    def own_block(turn, carry):
+        for index in range(count):
+            multiply(2 * turn, index)
+        return carry
+
+    own_block(0, 0)
+    start_first(size - 1)
+    lax.fori_loop(1, size // 2, own_block, 0)
     for stage in range(1, len(masks)):
         for item in range(len(items)):
             index, first_row, rows, order = items[item]
@@ -240,26 +275,31 @@
         copy.wait_send()
 
 
-def reduce_rows(arrays, size, collective_id, splits=2):
-    rows = arrays[0].shape[0] // size
-    widths = [array.shape[1] for array in arrays]
-    count = len(arrays)
+def reduce_products(lhs, rhs, lefts, size, collective_id, splits=2):
+    depth, model_width = lhs[0].shape
+    rows = model_width // size
+    widths = [array.shape[1] for array in rhs]
+    count = len(rhs)
     items = count * splits
-    total = sum(array.size for array in arrays)
     return pl.pallas_call(
-        functools.partial(reduce_kernel, size, splits, count),
+        functools.partial(reduce_kernel, size, splits, count, lefts, len(lhs)),
         out_shape=[jax.ShapeDtypeStruct((rows, width), jnp.float32) for width in widths],
-        in_specs=[pl.BlockSpec(memory_space=pltpu.VMEM)] * count,
+        in_specs=[pl.BlockSpec(memory_space=pltpu.VMEM)] * (len(lhs) + count),
         out_specs=[pl.BlockSpec(memory_space=pltpu.VMEM)] * count,
-        scratch_shapes=[pltpu.VMEM((size - 1, rows, width), jnp.bfloat16) for width in widths]
+        scratch_shapes=[pltpu.VMEM((size, rows, width), jnp.bfloat16) for width in widths]
+        + [pltpu.VMEM((size - 1, rows, width), jnp.bfloat16) for width in widths]
         + [pltpu.VMEM((size // 2 - 1, rows, width), jnp.bfloat16) for width in widths]
         + [pltpu.SemaphoreType.DMA((items, size)), pltpu.SemaphoreType.DMA((items, size))],
         compiler_params=pltpu.CompilerParams(
             collective_id=collective_id, has_side_effects=True, vmem_limit_bytes=KERNEL_VMEM
         ),
-        cost_estimate=pl.CostEstimate(flops=0, bytes_accessed=total * 12, transcendentals=0),
-        name=f"reduce_rows_{collective_id}",
-    )(*[array.reshape(size, rows, array.shape[1]) for array in arrays])
+        cost_estimate=pl.CostEstimate(
+            flops=2 * depth * model_width * sum(widths),
+            bytes_accessed=24 * model_width * sum(widths),
+            transcendentals=0,
+        ),
+        name=f"reduce_products_{collective_id}",
+    )(*lhs, *rhs)
 
 
 def normalize(raw_in):
@@ -471,13 +511,18 @@
     xn_two, grad_cat, ffn_hidden, d_gate, d_up, dn_two_rows = (
         jnp.concatenate(parts, axis=0) for parts in zip(*pieces)
     )
+    grad_gate, grad_up, grad_down = reduce_products(
+        (xn_two, grad_cat), (d_gate, d_up, ffn_hidden), (0, 0, 1), dp_size, 2
+    )
+    grad_down = grad_down.T
+    dn_two_rows, grad_up = lax.optimization_barrier((dn_two_rows, grad_up))
     dn_two_rows = dn_two_rows.astype(jnp.float32)
     back_two, grad_gain_two = norm_back(dn_two_rows, hidden_rows, gain_two)
     g_rows = lax.dynamic_slice_in_dim(out_grad, row_first, shard_rows, 0)
     dh_rows = g_rows.astype(jnp.float32) + back_two
     dh_rows_low = dh_rows.astype(jnp.bfloat16)
     dh_low = lax.all_gather(dh_rows_low, "mp", axis=0, tiled=True)
-    query_piece, _ = lax.optimization_barrier((query_piece, dh_rows_low))
+    query_piece, _ = lax.optimization_barrier((query_piece, pieces[-1][-1]))
     w_query_full = lax.all_gather(query_piece, ("mp", "dp"), axis=0, tiled=True).reshape(
         mp_size, model_width, head_span
     )
@@ -488,21 +533,7 @@
         [d_att_rows[:, i * head_span : (i + 1) * head_span] for i in range(mp_size)]
     )
     d_att = exchange(d_att_blocks, 3)
-    xn_two, grad_cat, _ = lax.optimization_barrier((xn_two, grad_cat, d_att))
     d_att = d_att.reshape(row_count, heads_dev, head_size)
-    grad_down = lax.dot_general(
-        grad_cat, ffn_hidden, CONTRACT_FIRST, preferred_element_type=jnp.float32
-    ).astype(jnp.bfloat16)
-    grad_gate = lax.dot_general(
-        xn_two, d_gate, CONTRACT_FIRST, preferred_element_type=jnp.float32
-    ).astype(jnp.bfloat16)
-    grad_up = lax.dot_general(
-        xn_two, d_up, CONTRACT_FIRST, preferred_element_type=jnp.float32
-    ).astype(jnp.bfloat16)
-    grad_gate, grad_up, grad_down = reduce_rows(
-        (grad_gate, grad_up, grad_down), dp_size, 2
-    )
-    grad_down = grad_down.T
     ffn_part = jnp.dot(
         ffn_hidden, w_down, preferred_element_type=jnp.float32
     ).astype(jnp.bfloat16)
@@ -573,17 +604,8 @@
         )
     back_one, grad_gain_one = norm_back(dn_one_rows, x_rows, gain_one)
     grad_tokens = dh_rows + back_one
-    grad_out_proj = lax.dot_general(
-        dh_low, attended, CONTRACT_FIRST, preferred_element_type=jnp.float32
-    ).astype(jnp.bfloat16)
-    grad_query = lax.dot_general(
-        xn_one, dq_low, CONTRACT_FIRST, preferred_element_type=jnp.float32
-    ).astype(jnp.bfloat16)
-    grad_window = lax.dot_general(
-        xn_one, d_window, CONTRACT_FIRST, preferred_element_type=jnp.float32
-    ).astype(jnp.bfloat16)
-    grad_out_proj, grad_query, grad_window = reduce_rows(
-        (grad_out_proj, grad_query, grad_window), dp_size, 5
+    grad_out_proj, grad_query, grad_window = reduce_products(
+        (dh_low, xn_one), (attended, dq_low, d_window), (0, 1, 1), dp_size, 5
     )
     grad_out_proj = grad_out_proj.T
     window_rows = exchange(

time: 673 us -> 629 us (0.935)
  waiting for transfers between devices: 141 us -> 73.5 us
  matrix products: 157 us -> 132 us
  local copies, waits for them, and re-layouts: 48.4 us -> 70.1 us
  Pallas kernels: 240 us -> 258 us
  other arithmetic: 59.5 us -> 66.9 us
    reduce_scatter x2, waiting for transfers between devices: 65.7 us -> 0.04 us  [shards(): lax.psum_scatter(dn_two_part.astype(jnp.bfloat16), 'mp', scatter_dimensio...]
    dot_general x6 -> x0, matrix products: 37 us -> none  [the longest x1 9.71 us: shards(): lax.dot_general(xn_two, d_up, CONTRACT_FIRST, preferred_element_type=jnp....]
    pallas_call x2, Pallas kernels: 103 us -> 121 us  [reduce_products(): pl.pallas_call(functools.partial(reduce_kernel, size, splits, count, left...]
    concatenate x2 -> x6, other arithmetic: 10.4 us -> 13.8 us  [shards(): jnp.concatenate(parts, axis=0)]
    unnamed x207 -> x221, local copies, waits for them, and re-layouts: 12.2 us -> 14.1 us
  transfers between devices with their start and end apart: 8 -> 8, of which waited for: 5 -> 3; matrix products, arithmetic and copies ran while one was open for 36% -> 39% of each run, Pallas kernels for 36% -> 42%
where the time goes in v4:
time: 629 us; the launch traced here: 618 us
  Pallas kernels  258 us (41%)
  matrix products  132 us (21%)
  waiting for transfers between devices  73.5 us (12%)
  local copies, waits for them, and re-layouts  70.1 us (11%)
  other arithmetic  66.9 us (11%)
  between operations  16.5 us (3%)
    pallas_call x4, Pallas kernels, exchange(): pl.pallas_call(functools.partial(exchange_kernel, size), out_shape=jax.Sh...  124 us
    pallas_call x2, Pallas kernels, reduce_products(): pl.pallas_call(functools.partial(reduce_kernel, size, splits, count, left...  121 us
    all_gather x2, waiting for transfers between devices, shards(): lax.all_gather(xn_two_rows[chunk * chunk_rows:(chunk + 1) * chunk_rows],...  63.3 us
    dot_general x2, matrix products, shards(): jnp.einsum('qhe,khe->hqk', att_rows, v_low[:key_stop], preferred_element_...  15.3 us
    unnamed x221, local copies, waits for them, and re-layouts  14.1 us
    concatenate x6, other arithmetic, shards(): jnp.concatenate(parts, axis=0)  13.8 us
    pallas_call x1, Pallas kernels, sum_everywhere(): pl.pallas_call(functools.partial(sum_kernel, mp_size, dp_size), out_shape...  13.3 us
  transfers between devices with their start and end apart: 8, of which 3 were waited for; matrix products, arithmetic and copies ran while one was open for 39% of the time, Pallas kernels for 42%

profile of v4, /device:TPU:0, one launch (start us, length us, event | category | flops | bytes accessed | tf_op | source)
XLA Modules:
  0.0 618.3 jit_solution(10413540813024281727)
XLA Ops:
  9.8 3.2 fusion.2
  16.2 3.5 fusion.109
  24.2 3.5 fusion.53
  38.6 2.4 fusion.107
  41.1 2.9 fusion
  45.7 3.6 fusion.49
  51.4 31.4 %exchange_1.1 = bf16[4,256,384]{2,1,0:T(8,128)(2,1)} custom-call(bf16[4,256,384]{2,1,0:T(8,128)(2,1)} %copy.167.data_ref), custom_call_target="tpu_custom_call" | custom-call | bytes 12582912 | tf_op jit(solution)/shard_map/exchange_1/pallas_call | solution.py:51
  84.2 9.9 %all-gather.6.cloned.1.call-done = bf16[1536,2048]{1,0:T(8,128)(2,1)} async-done(((bf16[48,2048]{1,0:T(8,128)(2,1)}), bf16[1536,2048]{1,0:T(8,128)(2,1)}) %all-gather.6.cloned.1.call-update) | async-done | bytes 6291472 | tf_op jit(solution)/shard_map/all_gather | solution.py:422
  94.1 5.0 multiply_reduce_fusion.2
  101.9 4.8 fusion.101
  106.8 39.7 %all-gather.10.cloned.1.call-done = bf16[512,2048]{1,0:T(8,128)(2,1)} async-done(((bf16[128,2048]{1,0:T(8,128)(2,1)}), bf16[512,2048]{1,0:T(8,128)(2,1)}) %all-gather.10.cloned.1.call-update) | async-done | bytes 2097168 | tf_op jit(solution)/shard_map/all_gather | solution.py:487
  146.6 6.0 fusion.112
  152.6 5.6 fusion.113
  158.3 3.8 multiply_convert_fusion.2
  162.2 2.9 fusion.115
  165.2 4.2 add_convert_fusion
  169.6 23.6 %all-gather.8.cloned.1.call-done = bf16[512,2048]{1,0:T(8,128)(2,1)} async-done(((bf16[128,2048]{1,0:T(8,128)(2,1)}), bf16[512,2048]{1,0:T(8,128)(2,1)}) %all-gather.8.cloned.1.call-update) | async-done | bytes 2097168 | tf_op jit(solution)/shard_map/all_gather | solution.py:487
  193.2 6.0 fusion.110
  199.3 5.7 fusion.111
  205.0 4.9 multiply_convert_fusion.4
  209.9 2.9 fusion.114
  212.9 4.3 add_convert_fusion.1
  217.5 5.1 pad_maximum_fusion.1.refs_1_
  229.8 2.5 pad_maximum_fusion.refs_0_
  232.3 87.3 %reduce_products_2.1 = (f32[256,1152]{1,0:T(8,128)}, f32[256,1152]{1,0:T(8,128)}, f32[256,1152]{1,0:T(8,128)}) custom-call(bf16[1024,2048]{1,0:T(8,128)(2,1)} %pad_maximum_fusion.refs_0_, bf16[1024,2048]{1,0:T(8,128)(2,1)} %pad_maximum_fusion.1.refs_1_, bf16[1024,1152]{1,0:T(8,128)(2,1)} %pad_maximum_fusion.3.refs_2_, ...), custom_call_target="tpu_custom_call" | custom-call | flops 14495514624 | bytes 169869312 | tf_op jit(solution)/shard_map/reduce_products_2/pallas_call | solution.py:284
  323.5 2.9 fusion.100
  329.3 3.1 copy.179
  340.4 8.2 %convolution_convert_fusion = bf16[1024,2048]{1,0:T(8,128)(2,1)S(1)} fusion(bf16[1152,2048]{1,0:T(8,128)(2,1)} %param.38, bf16[512,1152]{1,0:T(8,128)(2,1)S(1)} %get-tuple-element.157, bf16[512,1152]{1,0:T(8,128)(2,1)} %get-tuple-element.154), kind=kOutput, calls=%fused_computation.28 | convolution fusion | flops 4838653952 | bytes 11272192 | tf_op jit(solution)/shard_map/dot_general | solution.py:537
  353.5 4.6 convolution_convert_fusion.1
  359.2 29.1 %exchange_3.1 = bf16[4,256,384]{2,1,0:T(8,128)(2,1)} custom-call(bf16[4,256,384]{2,1,0:T(8,128)(2,1)} %pad_maximum_fusion.11.data_ref), custom_call_target="tpu_custom_call" | custom-call | bytes 12582912 | tf_op jit(solution)/shard_map/exchange_3/pallas_call | solution.py:51
  390.5 4.9 fusion.43
  395.4 4.5 multiply_reduce_fusion.1
  407.7 10.8 %multiply_reduce_fusion = (f32[6,512]{1,0:T(8,128)S(1)}, f32[6,512,1024]{2,1,0:T(8,128)}) fusion(f32[6,512,1024]{2,1,0:T(8,128)} %copy-done.1, f32[6,512]{1,0:T(8,128)S(1)} %log_add_fusion, bf16[512,6,64]{0,2,1:T(8,128)(2,1)S(1)} %slice.452, bf16[1024,6,64]{0,1,2:T(8,128)(2,1)} %copy-done.23), kind=kOutput, calls=%fused_computation.1 | convolution fusion | flops 412087296 | bytes 26370048 | tf_op jit(solution)/shard_map/qhe,khe->hqk/dot_general | solution.py:554
  418.5 6.1 fusion.37
  425.2 6.2 %multiply_convert_fusion = bf16[6,512,1024]{2,1,0:T(8,128)(2,1)S(1)} fusion(f32[6,512,1024]{2,1,0:T(8,128)} %get-tuple-element.224, f32[6,512,1024]{2,1,0:T(8,128)S(1)} %bitcast.197, f32[6,512]{1,0:T(8,128)S(1)} %get-tuple-element.223, f32[6,512]{1,0:T(8,128)S(1)} %log_add_fusion), kind=kLoop, calls=%fused_computation | loop fusion | flops 12582912 | bytes 31481856 | tf_op jit(solution)/shard_map/convert_element_type | solution.py:559
  442.4 2.3 copy.200
  449.8 2.9 pad_maximum_fusion.5
  452.7 3.0 copy.176
  457.5 3.3 multiply_reduce_fusion.4
  462.1 48.9 %exchange_4.1 = bf16[4,256,640]{2,1,0:T(8,128)(2,1)} custom-call(bf16[4,256,640]{2,1,0:T(8,128)(2,1)} %pad_maximum_fusion.7.data_ref), custom_call_target="tpu_custom_call" | custom-call | bytes 20971520 | tf_op jit(solution)/shard_map/exchange_4/pallas_call | solution.py:51
  516.6 4.2 fusion.116
  520.8 33.4 %reduce_products_5.1 = (f32[256,384]{1,0:T(8,128)}, f32[256,384]{1,0:T(8,128)}, f32[256,256]{1,0:T(8,128)}) custom-call(bf16[1024,2048]{1,0:T(8,128)(2,1)} %all-gather.14.cloned.1.call-done.refs_0_, bf16[1024,2048]{1,0:T(8,128)(2,1)} %copy-done.25, bf16[1024,384]{1,0:T(8,128)(2,1)} %copy.193.refs_2_, bf16[1024,384]{1,0:T(8,128)(2,1)} %copy-done.29, ...), custom_call_target="tpu_custom_call" | custom-call | flops 4294967296 | bytes 50331648 | tf_op jit(solution)/shard_map/reduce_products_5/pallas_call | solution.py:284
  555.9 14.6 %exchange_6.1 = bf16[4,64,256]{2,1,0:T(8,128)(2,1)} custom-call(bf16[4,64,256]{2,1,0:T(8,128)(2,1)} %bitcast.223), custom_call_target="tpu_custom_call" | custom-call | bytes 2097152 | tf_op jit(solution)/shard_map/exchange_6/pallas_call | solution.py:51
  574.6 3.0 convolution_add_fusion.3
  577.7 2.3 convolution_add_fusion.2
  581.8 3.7 fusion.30
  586.2 13.3 %sum_everywhere_7.1 = f32[40,128]{1,0:T(8,128)} custom-call(f32[40,128]{1,0:T(8,128)} %pad_bitcast_fusion.data_ref), custom_call_target="tpu_custom_call" | custom-call | tf_op jit(solution)/shard_map/sum_everywhere_7/pallas_call | solution.py:121
  602.2 6.1 fusion.29
  (374 shorter events, 105.9 us)
Async XLA Ops:
  7.2 9.1 %copy-start = (bf16[2048,384]{1,0:T(8,128)(2,1)S(1)}, bf16[2048,384]{1,0:T(8,128)(2,1)}, u32[]{:S(2)}) copy-start(bf16[2048,384]{1,0:T(8,128)(2,1)} %param.30) | copy-start | bytes 4718596
  7.2 86.9 %all-gather.6.cloned.1.call-start = ((), (), s32[]{:S(2)}) async-start(), calls=%async_computation.3 | async-start | bytes 6488064 | tf_op jit(solution)/shard_map/all_gather | solution.py:422
  9.0 137.6 %all-gather.10.cloned.1.call-start = ((), (), s32[]{:S(2)}) async-start(), calls=%async_computation.5 | async-start | bytes 2621440 | tf_op jit(solution)/shard_map/all_gather | solution.py:487
  21.7 12.7 %copy-start.8 = (f32[1024,384]{0,1:T(8,128)}, f32[1024,384]{0,1:T(8,128)S(1)}, u32[]{:S(2)}) copy-start(f32[1024,384]{0,1:T(8,128)S(1)} %copy.161) | copy-start | bytes 4718596
  21.7 12.7 %copy-start.85 = (f32[64]{0:T(128)}, f32[64]{0:T(128)S(1)}, u32[]{:S(2)}) copy-start(f32[64]{0:T(128)S(1)} %convert_element_type.225) | copy-start | bytes 772
  21.7 12.7 %copy-start.82 = (f32[64]{0:T(128)}, f32[64]{0:T(128)S(1)}, u32[]{:S(2)}) copy-start(f32[64]{0:T(128)S(1)} %convert_element_type.227) | copy-start | bytes 772
  22.0 7.8 %copy-start.80 = (s32[6]{0:T(128)}, s32[6]{0:T(128)S(1)}, u32[]{:S(2)}) copy-start(s32[6]{0:T(128)S(1)} %fusion.88) | copy-start | bytes 76
  29.4 15.8 %copy-start.23 = (bf16[1024,6,64]{0,1,2:T(8,128)(2,1)}, bf16[1024,6,64]{0,1,2:T(8,128)(2,1)S(1)}, u32[]{:S(2)}) copy-start(bf16[1024,6,64]{0,1,2:T(8,128)(2,1)S(1)} %fusion.41) | copy-start | bytes 2359300
  29.4 14.5 %copy-start.34 = (bf16[512,6,64]{0,1,2:T(8,128)(2,1)}, bf16[512,6,64]{0,1,2:T(8,128)(2,1)S(1)}, u32[]{:S(2)}) copy-start(bf16[512,6,64]{0,1,2:T(8,128)(2,1)S(1)} %slice.520) | copy-start | bytes 1179652
  37.6 6.3 %copy-start.2 = (f32[6,512,512]{1,2,0:T(8,128)}, f32[6,512,512]{1,2,0:T(8,128)S(1)}, u32[]{:S(2)}) copy-start(f32[6,512,512]{1,2,0:T(8,128)S(1)} %get-tuple-element.220) | copy-start | bytes 18874372
  37.6 6.3 %copy-start.63 = (f32[6,512]{1,0:T(8,128)}, f32[6,512]{1,0:T(8,128)S(1)}, u32[]{:S(2)}) copy-start(f32[6,512]{1,0:T(8,128)S(1)} %get-tuple-element.219) | copy-start | bytes 36868
  49.4 33.5 %copy-start.84 = (bf16[2048]{0:T(1024)(128)(2,1)S(1)}, bf16[2048]{0:T(1024)(128)(2,1)}, u32[]{:S(2)}) copy-start(bf16[2048]{0:T(1024)(128)(2,1)} %param.35) | copy-start | bytes 12292
  82.8 240.0 %copy-start.61 = (f32[2048]{0:T(1024)}, f32[2048]{0:T(1024)S(1)}, u32[]{:S(2)}) copy-start(f32[2048]{0:T(1024)S(1)} %convert_element_type.232) | copy-start | bytes 24580
  99.1 223.8 %copy-start.71 = (f32[256]{0:T(256)}, f32[256]{0:T(256)S(1)}, u32[]{:S(2)}) copy-start(f32[256]{0:T(256)S(1)} %add_rsqrt_fusion.4) | copy-start | bytes 3076
  100.8 92.4 %all-gather.8.cloned.1.call-start = ((), (), s32[]{:S(2)}) async-start(), calls=%async_computation.4 | async-start | bytes 2621440 | tf_op jit(solution)/shard_map/all_gather | solution.py:487
  106.8 212.8 %reduce-scatter.8.cloned.1.call-start = ((), (), s32[]{:S(2)}) async-start(), calls=%async_computation.8 | async-start | bytes 2621440 | tf_op jit(solution)/shard_map/reduce_scatter | solution.py:507
  146.6 11.7 %slice-start.14 = ((s8[4718592]{0:T(1024)(128)(4,1)}), s8[4194304]{0:T(1024)(128)(4,1)S(1)}, s32[]{:S(2)}) async-start(s8[4718592]{0:T(1024)(128)(4,1)} %bitcast.237), calls=%async_computation.25 | async-start | bytes 8388608
  152.6 9.6 %slice-start.6 = ((s8[4718592]{0:T(1024)(128)(4,1)}), s8[4194304]{0:T(1024)(128)(4,1)S(1)}, s32[]{:S(2)}) async-start(s8[4718592]{0:T(1024)(128)(4,1)} %bitcast.229), calls=%async_computation.17 | async-start | bytes 8388608
  152.6 12.5 %slice-start.10 = ((s8[4718592]{0:T(1024)(128)(4,1)}), s8[4194304]{0:T(1024)(128)(4,1)S(1)}, s32[]{:S(2)}) async-start(s8[4718592]{0:T(1024)(128)(4,1)} %bitcast.233), calls=%async_computation.21 | async-start | bytes 8388608
  158.3 6.8 %slice-start.11 = ((s8[4718592]{0:T(1024)(128)(4,1)}), s8[524288]{0:T(1024)(128)(4,1)S(1)}, s32[]{:S(2)}) async-start(s8[4718592]{0:T(1024)(128)(4,1)} %bitcast.233), calls=%async_computation.22 | async-start | bytes 1048576
  169.4 150.3 %reduce-scatter.6.cloned.1.call-start = ((), (), s32[]{:S(2)}) async-start(), calls=%async_computation.7 | async-start | bytes 2621440 | tf_op jit(solution)/shard_map/reduce_scatter | solution.py:507
  193.2 6.0 copy-start.32
  193.2 11.8 %slice-start.16 = ((s8[4718592]{0:T(1024)(128)(4,1)}), s8[4194304]{0:T(1024)(128)(4,1)S(1)}, s32[]{:S(2)}) async-start(s8[4718592]{0:T(1024)(128)(4,1)} %bitcast.239), calls=%async_computation.27 | async-start | bytes 8388608
  199.3 10.7 %slice-start.8 = ((s8[4718592]{0:T(1024)(128)(4,1)}), s8[4194304]{0:T(1024)(128)(4,1)S(1)}, s32[]{:S(2)}) async-start(s8[4718592]{0:T(1024)(128)(4,1)} %bitcast.231), calls=%async_computation.19 | async-start | bytes 8388608
  199.3 13.6 %slice-start.12 = ((s8[4718592]{0:T(1024)(128)(4,1)}), s8[4194304]{0:T(1024)(128)(4,1)S(1)}, s32[]{:S(2)}) async-start(s8[4718592]{0:T(1024)(128)(4,1)} %bitcast.235), calls=%async_computation.23 | async-start | bytes 8388608
  205.0 7.8 %slice-start.13 = ((s8[4718592]{0:T(1024)(128)(4,1)}), s8[524288]{0:T(1024)(128)(4,1)S(1)}, s32[]{:S(2)}) async-start(s8[4718592]{0:T(1024)(128)(4,1)} %bitcast.235), calls=%async_computation.24 | async-start | bytes 1048576
  217.2 303.7 %all-gather.14.cloned.1.call-start = ((), (), s32[]{:S(2)}) async-start(), calls=%async_computation.10 | async-start | bytes 5242880 | tf_op jit(solution)/shard_map/all_gather | solution.py:524
  326.4 248.2 %all-gather.12.cloned.1.call-start = ((), (), s32[]{:S(2)}) async-start(), calls=%async_computation.9 | async-start | bytes 6488064 | tf_op jit(solution)/shard_map/all_gather | solution.py:526
  327.2 274.9 %reduce-scatter.4.cloned.1.call-start = ((), (), s32[]{:S(2)}) async-start(), calls=%async_computation.6 | async-start | bytes 5242880 | tf_op jit(solution)/shard_map/reduce_scatter | solution.py:541
  359.2 31.2 %copy-start.59 = (f32[6,512]{1,0:T(8,128)S(1)}, f32[6,512]{1,0:T(8,128)}, u32[]{:S(2)}) copy-start(f32[6,512]{1,0:T(8,128)} %log_add_fusion.1) | copy-start | bytes 36868
  390.4 9.4 %slice-start.3 = ((s8[6291456]{0:T(1024)(128)(4,1)}), s8[4194304]{0:T(1024)(128)(4,1)S(1)}, s32[]{:S(2)}) async-start(s8[6291456]{0:T(1024)(128)(4,1)} %bitcast.198), calls=%async_computation.14 | async-start | bytes 8388608
  407.7 10.8 %copy-start.28 = (f32[512,6,64]{0,2,1:T(8,128)S(1)}, f32[512,6,64]{0,2,1:T(8,128)}, u32[]{:S(2)}) copy-start(f32[512,6,64]{0,2,1:T(8,128)} %fusion.43) | copy-start | bytes 2359300
  407.7 17.5 %slice-start = ((s8[12582912]{0:T(1024)(128)(4,1)}), s8[4194304]{0:T(1024)(128)(4,1)S(1)}, s32[]{:S(2)}) async-start(s8[12582912]{0:T(1024)(128)(4,1)} %bitcast.196), calls=%async_computation.11 | async-start | bytes 8388608
  407.7 17.5 %slice-start.1 = ((s8[12582912]{0:T(1024)(128)(4,1)}), s8[4194304]{0:T(1024)(128)(4,1)S(1)}, s32[]{:S(2)}) async-start(s8[12582912]{0:T(1024)(128)(4,1)} %bitcast.196), calls=%async_computation.12 | async-start | bytes 8388608
  418.5 6.1 copy-start.81
  418.5 6.8 %slice-start.2 = ((s8[12582912]{0:T(1024)(128)(4,1)}), s8[4194304]{0:T(1024)(128)(4,1)S(1)}, s32[]{:S(2)}) async-start(s8[12582912]{0:T(1024)(128)(4,1)} %bitcast.196), calls=%async_computation.13 | async-start | bytes 8388608
  440.5 9.3 %copy-start.9 = (f32[1024,384]{0,1:T(8,128)S(1)}, f32[1024,384]{0,1:T(8,128)}, u32[]{:S(2)}) copy-start(f32[1024,384]{0,1:T(8,128)} %copy-done.8) | copy-start | bytes 4718596
  440.5 9.3 %copy-start.56 = (f32[1024,6]{0,1:T(8,128)S(1)}, f32[1024,6]{0,1:T(8,128)}, u32[]{:S(2)}) copy-start(f32[1024,6]{0,1:T(8,128)} %copy-done.55) | copy-start | bytes 73732
  440.5 9.3 %copy-start.86 = (f32[64]{0:T(128)S(1)}, f32[64]{0:T(128)}, u32[]{:S(2)}) copy-start(f32[64]{0:T(128)} %copy-done.85) | copy-start | bytes 772
  460.8 50.2 %copy-start.29 = (bf16[1024,384]{1,0:T(8,128)(2,1)}, bf16[1024,384]{1,0:T(8,128)(2,1)S(1)}, u32[]{:S(2)}) copy-start(bf16[1024,384]{1,0:T(8,128)(2,1)S(1)} %get-tuple-element.151.refs_3_) | copy-start | bytes 2359300
  462.1 51.7 %copy-start.51 = (bf16[1024,2,64]{0,2,1:T(8,128)(2,1)S(1)}, bf16[1024,2,64]{0,2,1:T(8,128)(2,1)}, u32[]{:S(2)}) copy-start(bf16[1024,2,64]{0,2,1:T(8,128)(2,1)} %copy.185) | copy-start | bytes 786436
  462.1 51.9 %copy-start.52 = (bf16[1024,2,64]{0,2,1:T(8,128)(2,1)S(1)}, bf16[1024,2,64]{0,2,1:T(8,128)(2,1)}, u32[]{:S(2)}) copy-start(bf16[1024,2,64]{0,2,1:T(8,128)(2,1)} %copy.182) | copy-start | bytes 786436
  581.8 20.4 %copy-start.11 = (bf16[256,2048]{1,0:T(8,128)(2,1)S(1)}, bf16[256,2048]{1,0:T(8,128)(2,1)}, u32[]{:S(2)}) copy-start(bf16[256,2048]{1,0:T(8,128)(2,1)} %copy-done.10) | copy-start | bytes 3145732
  581.8 20.4 %copy-start.62 = (f32[2048]{0:T(1024)S(1)}, f32[2048]{0:T(1024)}, u32[]{:S(2)}) copy-start(f32[2048]{0:T(1024)} %copy-done.61) | copy-start | bytes 24580
  581.8 20.4 %copy-start.72 = (f32[256]{0:T(256)S(1)}, f32[256]{0:T(256)}, u32[]{:S(2)}) copy-start(f32[256]{0:T(256)} %copy-done.71) | copy-start | bytes 3076
  581.8 20.4 %copy-start.75 = (f32[256]{0:T(256)S(1)}, f32[256]{0:T(256)}, u32[]{:S(2)}) copy-start(f32[256]{0:T(256)} %copy-done.74) | copy-start | bytes 3076
  602.1 6.1 copy-start.58
  602.2 6.8 %copy-start.39 = (f32[256,1152]{1,0:T(8,128)S(1)}, f32[256,1152]{1,0:T(8,128)}, u32[]{:S(2)}) copy-start(f32[256,1152]{1,0:T(8,128)} %get-tuple-element.251) | copy-start | bytes 3538948
  (69 other events, 212.7 us)
Sparse Core Ops, SparseCore 0:
  11.4 82.6 all-gather.5
  100.9 45.6 all-gather.9
  148.7 44.4 all-gather.7
  195.4 42.4 reduce-scatter.7
  240.0 42.8 reduce-scatter.5
  326.5 95.0 all-gather.13
  424.5 83.7 all-gather.11
  510.6 77.0 reduce-scatter.3

commit v5 on v4

--- a/solution.py
+++ b/solution.py
@@ -416,9 +416,6 @@
     out_piece = lax.dynamic_slice_in_dim(
         w_out, dp_index * (head_span // dp_size), head_span // dp_size, 0
     )
-    query_piece = lax.dynamic_slice_in_dim(
-        w_query, dp_index * (model_width // dp_size), model_width // dp_size, 0
-    )
     w_out_full = lax.all_gather(out_piece, ("mp", "dp"), axis=0, tiled=True)
     doc_id, doc_pos, token_index = doc_layout(doc_lengths[0], row_count)
     cosine_tab, sine_tab = rope_table(doc_pos, head_size)
@@ -487,6 +484,8 @@
         xn_two = lax.all_gather(
             xn_two_rows[chunk * chunk_rows : (chunk + 1) * chunk_rows], "mp", axis=0, tiled=True
         )
+        if chunk:
+            xn_two, _ = lax.optimization_barrier((xn_two, dn_two_low))
         grad_chunk = grad_chunks[:, chunk].reshape(mp_size * chunk_rows, model_width)
         gate_act = jnp.dot(xn_two, w_gate, preferred_element_type=jnp.float32)
         up_act = jnp.dot(xn_two, w_up, preferred_element_type=jnp.float32)
@@ -504,13 +503,19 @@
         dn_two_part = lax.dot_general(
             d_gate, w_gate, CONTRACT_LAST, preferred_element_type=jnp.float32
         ) + lax.dot_general(d_up, w_up, CONTRACT_LAST, preferred_element_type=jnp.float32)
-        dn_two_chunk = lax.psum_scatter(
-            dn_two_part.astype(jnp.bfloat16), "mp", scatter_dimension=0, tiled=True
-        )
+        dn_two_low = dn_two_part.astype(jnp.bfloat16)
+        dn_two_chunk = lax.psum_scatter(dn_two_low, "mp", scatter_dimension=0, tiled=True)
         pieces.append((xn_two, grad_chunk, ffn_hidden, d_gate, d_up, dn_two_chunk))
     xn_two, grad_cat, ffn_hidden, d_gate, d_up, dn_two_rows = (
         jnp.concatenate(parts, axis=0) for parts in zip(*pieces)
     )
+    ffn_hidden, _ = lax.optimization_barrier((ffn_hidden, dn_two_low))
+    ffn_part = jnp.dot(ffn_hidden, w_down, preferred_element_type=jnp.float32).astype(jnp.bfloat16)
+    out_chunks = [
+        lax.psum_scatter(part, "mp", scatter_dimension=0, tiled=True)
+        for part in jnp.split(ffn_part, chunks, axis=0)
+    ]
+    xn_two, _ = lax.optimization_barrier((xn_two, ffn_part))
     grad_gate, grad_up, grad_down = reduce_products(
         (xn_two, grad_cat), (d_gate, d_up, ffn_hidden), (0, 0, 1), dp_size, 2
     )
@@ -521,11 +526,6 @@
     g_rows = lax.dynamic_slice_in_dim(out_grad, row_first, shard_rows, 0)
     dh_rows = g_rows.astype(jnp.float32) + back_two
     dh_rows_low = dh_rows.astype(jnp.bfloat16)
-    dh_low = lax.all_gather(dh_rows_low, "mp", axis=0, tiled=True)
-    query_piece, _ = lax.optimization_barrier((query_piece, pieces[-1][-1]))
-    w_query_full = lax.all_gather(query_piece, ("mp", "dp"), axis=0, tiled=True).reshape(
-        mp_size, model_width, head_span
-    )
     d_att_rows = lax.dot_general(
         dh_rows_low, w_out_full, CONTRACT_LAST, preferred_element_type=jnp.float32
     ).astype(jnp.bfloat16)
@@ -533,15 +533,9 @@
         [d_att_rows[:, i * head_span : (i + 1) * head_span] for i in range(mp_size)]
     )
     d_att = exchange(d_att_blocks, 3)
+    dh_low, d_att, out_chunks = lax.optimization_barrier((dh_rows_low, d_att, out_chunks))
+    dh_low = lax.all_gather(dh_low, "mp", axis=0, tiled=True)
     d_att = d_att.reshape(row_count, heads_dev, head_size)
-    ffn_part = jnp.dot(
-        ffn_hidden, w_down, preferred_element_type=jnp.float32
-    ).astype(jnp.bfloat16)
-    ffn_part = ffn_part.reshape(chunks, mp_size, chunk_rows, model_width).swapaxes(0, 1)
-    out_rows = hidden_rows + lax.psum_scatter(
-        ffn_part.reshape(row_count, model_width), "mp", scatter_dimension=0, tiled=True
-    ).astype(jnp.float32)
-    block_out = out_rows.astype(jnp.bfloat16)
     dq_blocks = []
     d_keys = jnp.zeros((row_count, heads_dev, head_size), jnp.float32)
     d_values = jnp.zeros((row_count, heads_dev, head_size), jnp.float32)
@@ -583,27 +577,21 @@
         jnp.bfloat16
     )
     window_span = kv_window * head_size
-    d_proj = jnp.concatenate([dq_low, d_window], axis=1)
-    d_proj_all = exchange(d_proj.reshape(mp_size, shard_rows, head_span + 2 * window_span), 4)
-    d_keyval_rows = jnp.concatenate(
-        [
-            unfold_windows(d_proj_all[:, :, head_span : head_span + window_span]),
-            unfold_windows(d_proj_all[:, :, head_span + window_span :]),
-        ],
-        axis=1,
-    ).astype(jnp.bfloat16)
-    dn_one_rows = lax.dot_general(
-        d_keyval_rows, w_keyval, CONTRACT_LAST, preferred_element_type=jnp.float32
-    )
-    for index in range(mp_size):
-        dn_one_rows = dn_one_rows + lax.dot_general(
-            d_proj_all[index, :, :head_span],
-            w_query_full[index],
+    dn_one_part = (
+        lax.dot_general(dq_low, w_query, CONTRACT_LAST, preferred_element_type=jnp.float32)
+        + lax.dot_general(
+            d_window,
+            jnp.concatenate([key_cols, value_cols], axis=1),
             CONTRACT_LAST,
             preferred_element_type=jnp.float32,
         )
+    ).astype(jnp.bfloat16)
+    dn_one_rows = lax.psum_scatter(dn_one_part, "mp", scatter_dimension=0, tiled=True).astype(
+        jnp.float32
+    )
     back_one, grad_gain_one = norm_back(dn_one_rows, x_rows, gain_one)
     grad_tokens = dh_rows + back_one
+    xn_one, _ = lax.optimization_barrier((xn_one, dn_one_part))
     grad_out_proj, grad_query, grad_window = reduce_products(
         (dh_low, xn_one), (attended, dq_low, d_window), (0, 1, 1), dp_size, 5
     )
@@ -618,6 +606,8 @@
         ],
         axis=1,
     )
+    out_rows = hidden_rows + jnp.concatenate(out_chunks, axis=0).astype(jnp.float32)
+    block_out = out_rows.astype(jnp.bfloat16)
     gain_sizes = (model_width, model_width, head_size, head_size)
     gains = jnp.concatenate([grad_gain_one, grad_gain_two, grad_q_gain, grad_k_gain])
     gain_rows = 8 * pl.cdiv(gains.shape[0], 1024)

time: 629 us -> 625 us (level)
  waiting for transfers between devices: 73.5 us -> 139 us
  Pallas kernels: 258 us -> 201 us
  matrix products: 132 us -> 123 us
  local copies, waits for them, and re-layouts: 70.1 us -> 61.1 us
  other arithmetic: 66.9 us -> 74.7 us
    pallas_call x4 -> x3, Pallas kernels: 124 us -> 66.8 us  [exchange(): pl.pallas_call(functools.partial(exchange_kernel, size), out_shape=jax.Sh...]
    reduce_scatter x3 -> x5, waiting for transfers between devices: 0.04 us -> 54.5 us  [the longest x1 30 us: shards(): lax.psum_scatter(dn_one_part, 'mp', scatter_dimension=0, tiled=True)]
    all_gather x2 -> x1, waiting for transfers between devices: 0.01 us -> 16.8 us  [shards(): dh_low = lax.all_gather(dh_low, 'mp', axis=0, tiled=True)]
    dot_general x5 -> x2, matrix products: 14.9 us -> 5.71 us  [the longest x1 3.33 us: shards(): lax.dot_general(d_window, jnp.concatenate([key_cols, value_cols], axis=1)...]
    concatenate x5 -> x0, local copies, waits for them, and re-layouts: 8 us -> none  [the longest x4 6.85 us: shards(): jnp.concatenate([fold_heads(dk_raw), fold_heads(d_values)], axis=1)]
    unnamed x221 -> x193, local copies, waits for them, and re-layouts: 14.1 us -> 12.4 us
  transfers between devices with their start and end apart: 8 -> 9, of which waited for: 3 -> 6; matrix products, arithmetic and copies ran while one was open for 39% -> 31% of each run, Pallas kernels for 42% -> 31%
where the time goes in v5:
time: 625 us; the launch traced here: 615 us
  Pallas kernels  201 us (32%)
  waiting for transfers between devices  139 us (22%)
  matrix products  123 us (20%)
  other arithmetic  74.7 us (12%)
  local copies, waits for them, and re-layouts  61.1 us (10%)
  between operations  15.9 us (3%)
    pallas_call x2, Pallas kernels, reduce_products(): pl.pallas_call(functools.partial(reduce_kernel, size, splits, count, left...  122 us
    pallas_call x3, Pallas kernels, exchange(): pl.pallas_call(functools.partial(exchange_kernel, size), out_shape=jax.Sh...  66.8 us
    all_gather x2, waiting for transfers between devices, shards(): lax.all_gather(xn_two_rows[chunk * chunk_rows:(chunk + 1) * chunk_rows],...  57.5 us
    reduce_scatter x1, waiting for transfers between devices, shards(): lax.psum_scatter(dn_one_part, 'mp', scatter_dimension=0, tiled=True)  30 us
    reduce_scatter x2, waiting for transfers between devices, shards(): lax.psum_scatter(part, 'mp', scatter_dimension=0, tiled=True)  24.4 us
    all_gather x1, waiting for transfers between devices, shards(): dh_low = lax.all_gather(dh_low, 'mp', axis=0, tiled=True)  16.8 us
    concatenate x6, other arithmetic, shards(): jnp.concatenate(parts, axis=0)  15.7 us
    dot_general x2, matrix products, shards(): up_act = jnp.dot(xn_two, w_up, preferred_element_type=jnp.float32)  14.4 us
  transfers between devices with their start and end apart: 9, of which 6 were waited for; matrix products, arithmetic and copies ran while one was open for 31% of the time, Pallas kernels for 31%

profile of v5, /device:TPU:0, one launch (start us, length us, event | category | flops | bytes accessed | tf_op | source)
XLA Modules:
  0.0 615.1 jit_solution(11349286041508482264)
XLA Ops:
  12.0 3.2 fusion.2
  34.8 2.9 fusion
  39.4 3.6 fusion.45
  44.0 2.7 convert_element_type.204
  48.8 29.3 %exchange_1.1 = bf16[4,256,384]{2,1,0:T(8,128)(2,1)} custom-call(bf16[4,256,384]{2,1,0:T(8,128)(2,1)} %copy.154.data_ref), custom_call_target="tpu_custom_call" | custom-call | bytes 12582912 | tf_op jit(solution)/shard_map/exchange_1/pallas_call | solution.py:51
  80.2 9.9 %all-gather.5.cloned.1.call-done = bf16[1536,2048]{1,0:T(8,128)(2,1)} async-done(((bf16[48,2048]{1,0:T(8,128)(2,1)}), bf16[1536,2048]{1,0:T(8,128)(2,1)}) %all-gather.5.cloned.1.call-update) | async-done | bytes 6291472 | tf_op jit(solution)/shard_map/all_gather | solution.py:419
  90.1 5.2 multiply_reduce_fusion.2
  97.7 2.9 fusion.88
  100.6 8.1 %convolution_multiply_fusion.1 = f32[512,1152]{1,0:T(8,128)} fusion(bf16[512,2048]{1,0:T(8,128)(2,1)S(1)} %bitcast.164, bf16[1152,2048]{1,0:T(8,128)(2,1)} %param.38, f32[1152]{0:T(1024)S(1)} %broadcast_bitcast_fusion), kind=kOutput, calls=%fused_computation.31 | convolution fusion | flops 2416508928 | bytes 9179648 | tf_op jit(solution)/shard_map/dot_general | solution.py:496
  108.8 4.3 convolution_multiply_fusion
  113.2 31.6 %all-gather.7.cloned.1.call-done = bf16[512,2048]{1,0:T(8,128)(2,1)} async-done(((bf16[128,2048]{1,0:T(8,128)(2,1)}), bf16[512,2048]{1,0:T(8,128)(2,1)}) %all-gather.7.cloned.1.call-update) | async-done | bytes 2097168 | tf_op jit(solution)/shard_map/all_gather | solution.py:484
  144.7 6.0 fusion.97
  150.8 7.3 %multiply_convert_fusion.3 = (bf16[512,1152]{1,0:T(8,128)(2,1)}, bf16[512,1152]{1,0:T(8,128)(2,1)S(1)}, bf16[512,1152]{1,0:T(8,128)(2,1)S(1)}) fusion(f32[1152]{0:T(1024)S(1)} %broadcast_bitcast_fusion, f32[512,1152]{1,0:T(8,128)S(1)} %fusion.97, f32[512,1152]{1,0:T(8,128)S(1)} %copy-done.83, bf16[512,2048]{1,0:T(8,128)(2,1)S(1)} %copy-done.41, ...), kind=kOutput, calls=%fused_computation.52 | convolution fusion | flops 2425356288 | bytes 15077888 | tf_op jit(solution)/shard_map/dot_general | solution.py:491
  158.1 2.9 fusion.98
  161.1 4.3 add_convert_fusion.2
  165.4 25.9 %all-gather.9.cloned.1.call-done = bf16[512,2048]{1,0:T(8,128)(2,1)} async-done(((bf16[128,2048]{1,0:T(8,128)(2,1)}), bf16[512,2048]{1,0:T(8,128)(2,1)}) %all-gather.9.cloned.1.call-update) | async-done | bytes 2097168 | tf_op jit(solution)/shard_map/all_gather | solution.py:484
  191.4 6.0 fusion.99
  197.4 7.1 %multiply_convert_fusion.2 = (bf16[512,1152]{1,0:T(8,128)(2,1)}, bf16[512,1152]{1,0:T(8,128)(2,1)S(1)}, bf16[512,1152]{1,0:T(8,128)(2,1)S(1)}) fusion(f32[1152]{0:T(1024)S(1)} %broadcast_bitcast_fusion, f32[512,1152]{1,0:T(8,128)S(1)} %fusion.99, f32[512,1152]{1,0:T(8,128)S(1)} %copy-done.82, bf16[512,2048]{1,0:T(8,128)(2,1)S(1)} %copy-done.43, ...), kind=kOutput, calls=%fused_computation.51 | convolution fusion | flops 2425356288 | bytes 15077888 | tf_op jit(solution)/shard_map/dot_general | solution.py:491
  204.5 2.9 fusion.100
  207.5 4.1 add_convert_fusion.1
  215.5 8.5 %convolution_convert_fusion = bf16[1024,2048]{1,0:T(8,128)(2,1)S(1)} fusion(bf16[1024,1152]{1,0:T(8,128)(2,1)S(1)} %pad_maximum_fusion.2.refs_4_, bf16[1152,2048]{1,0:T(8,128)(2,1)} %param.38), kind=kOutput, calls=%fused_computation.29 | convolution fusion | flops 4833935360 | bytes 11272192 | tf_op jit(solution)/shard_map/dot_general | solution.py:513
  224.0 2.5 fusion.87
  229.7 3.0 copy.166
  234.1 4.9 pad_maximum_fusion.1.refs_1_
  239.0 2.7 pad_maximum_fusion.refs_0_
  241.8 3.4 pad_maximum_fusion.3.refs_2_
  246.7 87.5 %reduce_products_2.1 = (f32[256,1152]{1,0:T(8,128)}, f32[256,1152]{1,0:T(8,128)}, f32[256,1152]{1,0:T(8,128)}) custom-call(bf16[1024,2048]{1,0:T(8,128)(2,1)} %pad_maximum_fusion.refs_0_, bf16[1024,2048]{1,0:T(8,128)(2,1)} %pad_maximum_fusion.1.refs_1_, bf16[1024,1152]{1,0:T(8,128)(2,1)} %pad_maximum_fusion.3.refs_2_, ...), custom_call_target="tpu_custom_call" | custom-call | flops 14495514624 | bytes 169869312 | tf_op jit(solution)/shard_map/reduce_products_2/pallas_call | solution.py:284
  337.6 2.9 fusion.86
  340.5 5.0 convolution_convert_fusion.1
  346.6 27.9 %exchange_3.1 = bf16[4,256,384]{2,1,0:T(8,128)(2,1)} custom-call(bf16[4,256,384]{2,1,0:T(8,128)(2,1)} %pad_maximum_fusion.11.data_ref), custom_call_target="tpu_custom_call" | custom-call | bytes 12582912 | tf_op jit(solution)/shard_map/exchange_3/pallas_call | solution.py:51
  374.5 24.4 %reduce-scatter.12.cloned.1.call-done = bf16[128,2048]{1,0:T(8,128)(2,1)} async-done(((bf16[512,2048]{1,0:T(8,128)(2,1)}), bf16[128,2048]{1,0:T(8,128)(2,1)}) %reduce-scatter.12.cloned.1.call-update) | async-done | bytes 524304 | tf_op jit(solution)/shard_map/reduce_scatter | solution.py:515
  403.2 4.6 multiply_reduce_fusion.1
  407.8 4.7 multiply_convert_fusion.1
  420.0 7.6 %multiply_reduce_fusion = (f32[6,512]{1,0:T(8,128)S(1)}, f32[6,512,1024]{2,1,0:T(8,128)S(1)}) fusion(f32[6,512,1024]{2,1,0:T(8,128)} %copy-done.1, f32[6,512]{1,0:T(8,128)S(1)} %log_add_fusion, bf16[512,6,64]{0,2,1:T(8,128)(2,1)} %slice.334, bf16[1024,6,64]{0,1,2:T(8,128)(2,1)} %copy-done.27), kind=kOutput, calls=%fused_computation.1 | convolution fusion | flops 412087296 | bytes 26370048 | tf_op jit(solution)/shard_map/qhe,khe->hqk/dot_general | solution.py:548
  427.6 6.7 %multiply_convert_fusion = bf16[6,512,1024]{2,1,0:T(8,128)(2,1)S(1)} fusion(f32[6,512,1024]{2,1,0:T(8,128)S(1)} %get-tuple-element.234, f32[6,512,1024]{2,1,0:T(8,128)} %copy-done.1, f32[6,512]{1,0:T(8,128)S(1)} %get-tuple-element.233, f32[6,512]{1,0:T(8,128)S(1)} %log_add_fusion), kind=kLoop, calls=%fused_computation | loop fusion | flops 12582912 | bytes 31481856 | tf_op jit(solution)/shard_map/convert_element_type | solution.py:553
  441.0 3.1 copy.162
  446.0 4.0 fusion.39
  450.0 6.3 %fusion.33 = bf16[1024,6,64]{0,2,1:T(8,128)(2,1)S(1)} fusion(f32[512,6,64]{0,2,1:T(8,128)S(1)} %fusion.39, bf16[512,6,64]{0,2,1:T(8,128)(2,1)S(1)} %copy-done.32, f32[6,512,1024]{2,1,0:T(8,128)} %copy-done.1, f32[6,512]{1,0:T(8,128)S(1)} %log_add_fusion), kind=kOutput, calls=%fused_computation.81 | convolution fusion | flops 409731072 | bytes 14561280 | tf_op jit(solution)/shard_map/hqk,qhe->khe/dot_general | solution.py:570
  458.9 3.5 multiply_reduce_fusion.3
  466.7 2.8 multiply_reduce_fusion.4
  472.8 3.3 add_convert_fusion
  480.5 2.7 copy.178
  484.6 16.8 %all-gather.11.cloned.1.call-done.refs_0_ = bf16[1024,2048]{1,0:T(8,128)(2,1)} async-done(((bf16[256,2048]{1,0:T(8,128)(2,1)}), bf16[1024,2048]{1,0:T(8,128)(2,1)}) %all-gather.11.cloned.1.call-update) | async-done | bytes 4194320 | tf_op jit(solution)/shard_map/all_gather | solution.py:537
  501.4 34.1 %reduce_products_5.1 = (f32[256,384]{1,0:T(8,128)}, f32[256,384]{1,0:T(8,128)}, f32[256,256]{1,0:T(8,128)}) custom-call(bf16[1024,2048]{1,0:T(8,128)(2,1)} %all-gather.11.cloned.1.call-done.refs_0_, bf16[1024,2048]{1,0:T(8,128)(2,1)} %copy-done.28, bf16[1024,384]{1,0:T(8,128)(2,1)} %copy.176.refs_2_, bf16[1024,384]{1,0:T(8,128)(2,1)} %copy-done.29, ...), custom_call_target="tpu_custom_call" | custom-call | flops 4294967296 | bytes 50331648 | tf_op jit(solution)/shard_map/reduce_products_5/pallas_call | solution.py:284
  537.2 9.6 %exchange_6.1 = bf16[4,64,256]{2,1,0:T(8,128)(2,1)} custom-call(bf16[4,64,256]{2,1,0:T(8,128)(2,1)} %bitcast.174), custom_call_target="tpu_custom_call" | custom-call | bytes 2097152 | tf_op jit(solution)/shard_map/exchange_6/pallas_call | solution.py:51
  551.1 30.0 %reduce-scatter.14.cloned.1.call-done = bf16[256,2048]{1,0:T(8,128)(2,1)} async-done(((bf16[1024,2048]{1,0:T(8,128)(2,1)}), bf16[256,2048]{1,0:T(8,128)(2,1)}) %reduce-scatter.14.cloned.1.call-update) | async-done | bytes 1048592 | tf_op jit(solution)/shard_map/reduce_scatter | solution.py:589
  584.9 12.1 %sum_everywhere_7.1 = f32[40,128]{1,0:T(8,128)} custom-call(f32[40,128]{1,0:T(8,128)} %pad_bitcast_fusion.data_ref), custom_call_target="tpu_custom_call" | custom-call | tf_op jit(solution)/shard_map/sum_everywhere_7/pallas_call | solution.py:121
  599.7 5.6 fusion.24
  (327 shorter events, 98.8 us)
Async XLA Ops:
  7.2 14.3 %copy-start = (bf16[2048,384]{1,0:T(8,128)(2,1)S(1)}, bf16[2048,384]{1,0:T(8,128)(2,1)}, u32[]{:S(2)}) copy-start(bf16[2048,384]{1,0:T(8,128)(2,1)} %param.30) | copy-start | bytes 4718596
  7.2 82.9 %all-gather.5.cloned.1.call-start = ((), (), s32[]{:S(2)}) async-start(), calls=%async_computation.5 | async-start | bytes 6488064 | tf_op jit(solution)/shard_map/all_gather | solution.py:419
  9.0 135.7 %all-gather.7.cloned.1.call-start = ((), (), s32[]{:S(2)}) async-start(), calls=%async_computation.6 | async-start | bytes 2621440 | tf_op jit(solution)/shard_map/all_gather | solution.py:484
  9.8 7.4 %copy-start.66 = (f32[2048]{0:T(1024)}, f32[2048]{0:T(1024)S(1)}, u32[]{:S(2)}) copy-start(f32[2048]{0:T(1024)S(1)} %convert_element_type.193) | copy-start | bytes 24580
  10.4 17.7 %copy-start.77 = (f32[64]{0:T(128)}, f32[64]{0:T(128)S(1)}, u32[]{:S(2)}) copy-start(f32[64]{0:T(128)S(1)} %convert_element_type.198) | copy-start | bytes 772
  11.1 17.1 %copy-start.74 = (f32[64]{0:T(128)}, f32[64]{0:T(128)S(1)}, u32[]{:S(2)}) copy-start(f32[64]{0:T(128)S(1)} %convert_element_type.200) | copy-start | bytes 772
  11.9 5.3 copy-start.69
  12.0 11.6 %copy-start.72 = (s32[6]{0:T(128)}, s32[6]{0:T(128)S(1)}, u32[]{:S(2)}) copy-start(s32[6]{0:T(128)S(1)} %fusion.73) | copy-start | bytes 76
  12.0 5.2 copy-start.7
  21.3 17.6 %copy-start.27 = (bf16[1024,6,64]{0,1,2:T(8,128)(2,1)}, bf16[1024,6,64]{0,1,2:T(8,128)(2,1)S(1)}, u32[]{:S(2)}) copy-start(bf16[1024,6,64]{0,1,2:T(8,128)(2,1)S(1)} %fusion.37) | copy-start | bytes 2359300
  21.3 16.4 %copy-start.45 = (bf16[512,6,64]{0,1,2:T(8,128)(2,1)}, bf16[512,6,64]{0,1,2:T(8,128)(2,1)S(1)}, u32[]{:S(2)}) copy-start(bf16[512,6,64]{0,1,2:T(8,128)(2,1)S(1)} %slice.370) | copy-start | bytes 1179652
  26.0 202.4 %copy-start.58 = (f32[1024,6]{0,1:T(8,128)}, f32[1024,6]{0,1:T(8,128)S(1)}, u32[]{:S(2)}) copy-start(f32[1024,6]{0,1:T(8,128)S(1)} %add_rsqrt_fusion.1) | copy-start | bytes 73732
  31.4 6.3 %copy-start.2 = (f32[6,512,512]{1,2,0:T(8,128)}, f32[6,512,512]{1,2,0:T(8,128)S(1)}, u32[]{:S(2)}) copy-start(f32[6,512,512]{1,2,0:T(8,128)S(1)} %get-tuple-element.228) | copy-start | bytes 18874372
  44.0 34.1 %copy-start.76 = (bf16[2048]{0:T(1024)(128)(2,1)S(1)}, bf16[2048]{0:T(1024)(128)(2,1)}, u32[]{:S(2)}) copy-start(bf16[2048]{0:T(1024)(128)(2,1)} %param.35) | copy-start | bytes 12292
  78.2 259.4 %copy-start.64 = (f32[2048]{0:T(1024)}, f32[2048]{0:T(1024)S(1)}, u32[]{:S(2)}) copy-start(f32[2048]{0:T(1024)S(1)} %convert_element_type.207) | copy-start | bytes 24580
  95.4 242.2 %copy-start.68 = (f32[256]{0:T(256)}, f32[256]{0:T(256)S(1)}, u32[]{:S(2)}) copy-start(f32[256]{0:T(256)S(1)} %add_rsqrt_fusion.4) | copy-start | bytes 3076
  97.1 94.2 %all-gather.9.cloned.1.call-start = ((), (), s32[]{:S(2)}) async-start(), calls=%async_computation.8 | async-start | bytes 2621440 | tf_op jit(solution)/shard_map/all_gather | solution.py:484
  97.7 11.1 %slice-start.9 = ((s8[4718592]{0:T(1024)(128)(4,1)}), s8[4194304]{0:T(1024)(128)(4,1)S(1)}, s32[]{:S(2)}) async-start(s8[4718592]{0:T(1024)(128)(4,1)} %bitcast.188), calls=%async_computation.23 | async-start | bytes 8388608
  100.6 8.2 %copy-start.11 = (bf16[4,1,128,2048]{3,2,1,0:T(8,128)(2,1)}, bf16[4,1,128,2048]{3,2,1,0:T(8,128)(2,1)S(1)}, u32[]{:S(2)}) copy-start(bf16[4,1,128,2048]{3,2,1,0:T(8,128)(2,1)S(1)} %get-tuple-element.175) | copy-start | bytes 6291460
  100.6 8.2 %copy-start.10 = (bf16[4,1,128,2048]{3,2,1,0:T(8,128)(2,1)}, bf16[4,1,128,2048]{3,2,1,0:T(8,128)(2,1)S(1)}, u32[]{:S(2)}) copy-start(bf16[4,1,128,2048]{3,2,1,0:T(8,128)(2,1)S(1)} %get-tuple-element.174) | copy-start | bytes 6291460
  100.6 8.2 %slice-start.10 = ((s8[4718592]{0:T(1024)(128)(4,1)}), s8[524288]{0:T(1024)(128)(4,1)S(1)}, s32[]{:S(2)}) async-start(s8[4718592]{0:T(1024)(128)(4,1)} %bitcast.188), calls=%async_computation.24 | async-start | bytes 1048576
  113.1 221.1 %reduce-scatter.8.cloned.1.call-start = ((), (), s32[]{:S(2)}) async-start(), calls=%async_computation.9 | async-start | bytes 2621440 | tf_op jit(solution)/shard_map/reduce_scatter | solution.py:507
  144.7 6.0 copy-start.41
  144.7 6.0 copy-start.83
  144.7 13.4 %slice-start.1 = ((s8[4718592]{0:T(1024)(128)(4,1)}), s8[4194304]{0:T(1024)(128)(4,1)S(1)}, s32[]{:S(2)}) async-start(s8[4718592]{0:T(1024)(128)(4,1)} %bitcast.180), calls=%async_computation.15 | async-start | bytes 8388608
  144.7 16.3 %slice-start.5 = ((s8[4718592]{0:T(1024)(128)(4,1)}), s8[4194304]{0:T(1024)(128)(4,1)S(1)}, s32[]{:S(2)}) async-start(s8[4718592]{0:T(1024)(128)(4,1)} %bitcast.184), calls=%async_computation.19 | async-start | bytes 8388608
  150.7 7.4 %slice-start.2 = ((s8[4718592]{0:T(1024)(128)(4,1)}), s8[524288]{0:T(1024)(128)(4,1)S(1)}, s32[]{:S(2)}) async-start(s8[4718592]{0:T(1024)(128)(4,1)} %bitcast.180), calls=%async_computation.16 | async-start | bytes 1048576
  150.7 10.3 %slice-start.6 = ((s8[4718592]{0:T(1024)(128)(4,1)}), s8[524288]{0:T(1024)(128)(4,1)S(1)}, s32[]{:S(2)}) async-start(s8[4718592]{0:T(1024)(128)(4,1)} %bitcast.184), calls=%async_computation.20 | async-start | bytes 1048576
  191.4 6.0 copy-start.43
  191.4 6.0 copy-start.82
  191.4 13.1 %slice-start.3 = ((s8[4718592]{0:T(1024)(128)(4,1)}), s8[4194304]{0:T(1024)(128)(4,1)S(1)}, s32[]{:S(2)}) async-start(s8[4718592]{0:T(1024)(128)(4,1)} %bitcast.182), calls=%async_computation.17 | async-start | bytes 8388608
  191.4 16.1 %slice-start.7 = ((s8[4718592]{0:T(1024)(128)(4,1)}), s8[4194304]{0:T(1024)(128)(4,1)S(1)}, s32[]{:S(2)}) async-start(s8[4718592]{0:T(1024)(128)(4,1)} %bitcast.186), calls=%async_computation.21 | async-start | bytes 8388608
  197.4 7.1 %slice-start.4 = ((s8[4718592]{0:T(1024)(128)(4,1)}), s8[524288]{0:T(1024)(128)(4,1)S(1)}, s32[]{:S(2)}) async-start(s8[4718592]{0:T(1024)(128)(4,1)} %bitcast.182), calls=%async_computation.18 | async-start | bytes 1048576
  197.4 10.1 %slice-start.8 = ((s8[4718592]{0:T(1024)(128)(4,1)}), s8[524288]{0:T(1024)(128)(4,1)S(1)}, s32[]{:S(2)}) async-start(s8[4718592]{0:T(1024)(128)(4,1)} %bitcast.186), calls=%async_computation.22 | async-start | bytes 1048576
  211.6 122.7 %reduce-scatter.6.cloned.1.call-start = ((), (), s32[]{:S(2)}) async-start(), calls=%async_computation.7 | async-start | bytes 2621440 | tf_op jit(solution)/shard_map/reduce_scatter | solution.py:507
  212.2 162.3 %reduce-scatter.10.cloned.1.call-start = ((), (), s32[]{:S(2)}) async-start(), calls=%async_computation.10 | async-start | bytes 2621440 | tf_op jit(solution)/shard_map/reduce_scatter | solution.py:515
  226.5 172.4 %reduce-scatter.12.cloned.1.call-start = ((), (), s32[]{:S(2)}) async-start(), calls=%async_computation.11 | async-start | bytes 2621440 | tf_op jit(solution)/shard_map/reduce_scatter | solution.py:515
  241.7 259.7 %all-gather.11.cloned.1.call-start = ((), (), s32[]{:S(2)}) async-start(), calls=%async_computation.13 | async-start | bytes 5242880 | tf_op jit(solution)/shard_map/all_gather | solution.py:537
  419.9 161.2 %reduce-scatter.14.cloned.1.call-start = ((), (), s32[]{:S(2)}) async-start(), calls=%async_computation.12 | async-start | bytes 5242880 | tf_op jit(solution)/shard_map/reduce_scatter | solution.py:589
  427.6 6.7 %copy-start.19 = (bf16[1024,6,32]{0,2,1:T(8,128)(2,1)S(1)}, bf16[1024,6,32]{0,2,1:T(8,128)(2,1)}, u32[]{:S(2)}) copy-start(bf16[1024,6,32]{0,2,1:T(8,128)(2,1)} %copy-done.17) | copy-start | bytes 1179652
  427.6 6.7 %copy-start.34 = (f32[512,6,64]{0,2,1:T(8,128)S(1)}, f32[512,6,64]{0,2,1:T(8,128)}, u32[]{:S(2)}) copy-start(f32[512,6,64]{0,2,1:T(8,128)} %fusion.42) | copy-start | bytes 2359300
  450.0 6.3 %copy-start.73 = (s32[6]{0:T(128)S(1)}, s32[6]{0:T(128)}, u32[]{:S(2)}) copy-start(s32[6]{0:T(128)} %copy-done.72) | copy-start | bytes 76
  535.5 45.6 %copy-start.67 = (f32[2048]{0:T(1024)S(1)}, f32[2048]{0:T(1024)}, u32[]{:S(2)}) copy-start(f32[2048]{0:T(1024)} %copy-done.66) | copy-start | bytes 24580
  546.8 52.9 %copy-start.9 = (bf16[256,2048]{1,0:T(8,128)(2,1)S(1)}, bf16[256,2048]{1,0:T(8,128)(2,1)}, u32[]{:S(2)}) copy-start(bf16[256,2048]{1,0:T(8,128)(2,1)} %copy-done.8) | copy-start | bytes 3145732
  546.8 52.9 %copy-start.60 = (bf16[128,2048]{1,0:T(8,128)(2,1)S(1)}, bf16[128,2048]{1,0:T(8,128)(2,1)}, u32[]{:S(2)}) copy-start(bf16[128,2048]{1,0:T(8,128)(2,1)} %reduce-scatter.10.cloned.1.call-done) | copy-start | bytes 1572868
  546.8 52.9 %copy-start.65 = (f32[2048]{0:T(1024)S(1)}, f32[2048]{0:T(1024)}, u32[]{:S(2)}) copy-start(f32[2048]{0:T(1024)} %copy-done.64) | copy-start | bytes 24580
  599.7 5.7 copy-start.62
  599.7 6.4 %copy-start.49 = (f32[256,1152]{1,0:T(8,128)S(1)}, f32[256,1152]{1,0:T(8,128)}, u32[]{:S(2)}) copy-start(f32[256,1152]{1,0:T(8,128)} %get-tuple-element.258) | copy-start | bytes 3538948
  (56 other events, 150.6 us)
Sparse Core Ops, SparseCore 0:
  11.4 78.6 all-gather.4
  97.2 47.4 all-gather.6
  146.9 44.4 all-gather.8
  211.7 42.4 reduce-scatter.7
  256.3 42.8 reduce-scatter.5
  301.3 42.8 reduce-scatter.9
  346.5 52.3 reduce-scatter.11
  420.1 81.2 all-gather.10
  503.7 77.3 reduce-scatter.13

commit v6 on v5

--- a/solution.py
+++ b/solution.py
@@ -295,7 +295,7 @@
         ),
         cost_estimate=pl.CostEstimate(
             flops=2 * depth * model_width * sum(widths),
-            bytes_accessed=24 * model_width * sum(widths),
+            bytes_accessed=2 * model_width * sum(widths),
             transcendentals=0,
         ),
         name=f"reduce_products_{collective_id}",
@@ -533,7 +533,7 @@
         [d_att_rows[:, i * head_span : (i + 1) * head_span] for i in range(mp_size)]
     )
     d_att = exchange(d_att_blocks, 3)
-    dh_low, d_att, out_chunks = lax.optimization_barrier((dh_rows_low, d_att, out_chunks))
+    dh_low, _, out_chunks = lax.optimization_barrier((dh_rows_low, d_att, out_chunks))
     dh_low = lax.all_gather(dh_low, "mp", axis=0, tiled=True)
     d_att = d_att.reshape(row_count, heads_dev, head_size)
     dq_blocks = []

time: 625 us -> 611 us (0.978)
  waiting for transfers between devices: 139 us -> 127 us
    reduce_scatter x2, waiting for transfers between devices: 24.4 us -> 3.26 us  [shards(): lax.psum_scatter(part, 'mp', scatter_dimension=0, tiled=True)]
    all_gather x1, waiting for transfers between devices: 16.8 us -> 25.6 us  [shards(): dh_low = lax.all_gather(dh_low, 'mp', axis=0, tiled=True)]
    unnamed x193 -> x197, local copies, waits for them, and re-layouts: 12.4 us -> 13.2 us
  transfers between devices with their start and end apart: 9 -> 9, of which waited for: 6 -> 6; matrix products, arithmetic and copies ran while one was open for 31% -> 35% of each run, Pallas kernels for 31% -> 31%
where the time goes in v6:
time: 611 us; the launch traced here: 601 us
  Pallas kernels  200 us (33%)
  waiting for transfers between devices  127 us (21%)
  matrix products  122 us (20%)
  other arithmetic  72.6 us (12%)
  local copies, waits for them, and re-layouts  62.1 us (10%)
  between operations  15.9 us (3%)
    pallas_call x2, Pallas kernels, reduce_products(): pl.pallas_call(functools.partial(reduce_kernel, size, splits, count, left...  122 us
    pallas_call x3, Pallas kernels, exchange(): pl.pallas_call(functools.partial(exchange_kernel, size), out_shape=jax.Sh...  66.8 us
    all_gather x2, waiting for transfers between devices, shards(): lax.all_gather(xn_two_rows[chunk * chunk_rows:(chunk + 1) * chunk_rows],...  57.5 us
    reduce_scatter x1, waiting for transfers between devices, shards(): lax.psum_scatter(dn_one_part, 'mp', scatter_dimension=0, tiled=True)  30 us
    all_gather x1, waiting for transfers between devices, shards(): dh_low = lax.all_gather(dh_low, 'mp', axis=0, tiled=True)  25.6 us
    dot_general x2, matrix products, shards(): up_act = jnp.dot(xn_two, w_up, preferred_element_type=jnp.float32)  14.4 us
    concatenate x6, other arithmetic, shards(): jnp.concatenate(parts, axis=0)  14 us
    unnamed x197, local copies, waits for them, and re-layouts  13.2 us
  transfers between devices with their start and end apart: 9, of which 6 were waited for; matrix products, arithmetic and copies ran while one was open for 35% of the time, Pallas kernels for 31%

profile of v6, /device:TPU:0, one launch (start us, length us, event | category | flops | bytes accessed | tf_op | source)
XLA Modules:
  0.0 601.4 jit_solution(12530670445959562556)
XLA Ops:
  12.0 3.2 fusion.2
  32.3 2.4 fusion.94
  34.8 2.9 fusion
  39.4 3.6 fusion.45
  44.0 2.7 convert_element_type.204
  48.8 29.3 %exchange_1.1 = bf16[4,256,384]{2,1,0:T(8,128)(2,1)} custom-call(bf16[4,256,384]{2,1,0:T(8,128)(2,1)} %copy.154.data_ref), custom_call_target="tpu_custom_call" | custom-call | bytes 12582912 | tf_op jit(solution)/shard_map/exchange_1/pallas_call | solution.py:51
  80.2 9.9 %all-gather.5.cloned.1.call-done = bf16[1536,2048]{1,0:T(8,128)(2,1)} async-done(((bf16[48,2048]{1,0:T(8,128)(2,1)}), bf16[1536,2048]{1,0:T(8,128)(2,1)}) %all-gather.5.cloned.1.call-update) | async-done | bytes 6291472 | tf_op jit(solution)/shard_map/all_gather | solution.py:419
  90.1 5.2 multiply_reduce_fusion.2
  97.7 2.9 fusion.88
  100.6 8.1 %convolution_multiply_fusion.1 = f32[512,1152]{1,0:T(8,128)} fusion(bf16[512,2048]{1,0:T(8,128)(2,1)S(1)} %bitcast.164, bf16[1152,2048]{1,0:T(8,128)(2,1)} %param.38, f32[1152]{0:T(1024)S(1)} %broadcast_bitcast_fusion), kind=kOutput, calls=%fused_computation.31 | convolution fusion | flops 2416508928 | bytes 9179648 | tf_op jit(solution)/shard_map/dot_general | solution.py:496
  108.8 4.3 convolution_multiply_fusion
  113.1 31.6 %all-gather.7.cloned.1.call-done = bf16[512,2048]{1,0:T(8,128)(2,1)} async-done(((bf16[128,2048]{1,0:T(8,128)(2,1)}), bf16[512,2048]{1,0:T(8,128)(2,1)}) %all-gather.7.cloned.1.call-update) | async-done | bytes 2097168 | tf_op jit(solution)/shard_map/all_gather | solution.py:484
  144.7 6.0 fusion.97
  150.7 7.3 %multiply_convert_fusion.3 = (bf16[512,1152]{1,0:T(8,128)(2,1)}, bf16[512,1152]{1,0:T(8,128)(2,1)S(1)}, bf16[512,1152]{1,0:T(8,128)(2,1)S(1)}) fusion(f32[1152]{0:T(1024)S(1)} %broadcast_bitcast_fusion, f32[512,1152]{1,0:T(8,128)S(1)} %fusion.97, f32[512,1152]{1,0:T(8,128)S(1)} %copy-done.85, bf16[512,2048]{1,0:T(8,128)(2,1)S(1)} %copy-done.41, ...), kind=kOutput, calls=%fused_computation.52 | convolution fusion | flops 2425356288 | bytes 15077888 | tf_op jit(solution)/shard_map/dot_general | solution.py:491
  158.1 2.9 fusion.98
  161.1 4.3 add_convert_fusion.2
  165.4 26.0 %all-gather.9.cloned.1.call-done = bf16[512,2048]{1,0:T(8,128)(2,1)} async-done(((bf16[128,2048]{1,0:T(8,128)(2,1)}), bf16[512,2048]{1,0:T(8,128)(2,1)}) %all-gather.9.cloned.1.call-update) | async-done | bytes 2097168 | tf_op jit(solution)/shard_map/all_gather | solution.py:484
  191.4 6.0 fusion.99
  197.4 7.1 %multiply_convert_fusion.2 = (bf16[512,1152]{1,0:T(8,128)(2,1)}, bf16[512,1152]{1,0:T(8,128)(2,1)S(1)}, bf16[512,1152]{1,0:T(8,128)(2,1)S(1)}) fusion(f32[1152]{0:T(1024)S(1)} %broadcast_bitcast_fusion, f32[512,1152]{1,0:T(8,128)S(1)} %fusion.99, f32[512,1152]{1,0:T(8,128)S(1)} %copy-done.84, bf16[512,2048]{1,0:T(8,128)(2,1)S(1)} %copy-done.43, ...), kind=kOutput, calls=%fused_computation.51 | convolution fusion | flops 2425356288 | bytes 15077888 | tf_op jit(solution)/shard_map/dot_general | solution.py:491
  204.5 2.9 fusion.100
  207.5 4.1 add_convert_fusion.1
  215.4 8.5 %convolution_convert_fusion = bf16[1024,2048]{1,0:T(8,128)(2,1)S(1)} fusion(bf16[1024,1152]{1,0:T(8,128)(2,1)S(1)} %pad_maximum_fusion.2.refs_4_, bf16[1152,2048]{1,0:T(8,128)(2,1)} %param.38), kind=kOutput, calls=%fused_computation.29 | convolution fusion | flops 4833935360 | bytes 11272192 | tf_op jit(solution)/shard_map/dot_general | solution.py:513
  224.0 2.6 fusion.87
  229.8 3.0 copy.166
  234.1 4.9 pad_maximum_fusion.1.refs_1_
  239.1 2.6 pad_maximum_fusion.refs_0_
  245.8 87.5 %reduce_products_2.1 = (f32[256,1152]{1,0:T(8,128)}, f32[256,1152]{1,0:T(8,128)}, f32[256,1152]{1,0:T(8,128)}) custom-call(bf16[1024,2048]{1,0:T(8,128)(2,1)} %pad_maximum_fusion.refs_0_, bf16[1024,2048]{1,0:T(8,128)(2,1)} %pad_maximum_fusion.1.refs_1_, bf16[1024,1152]{1,0:T(8,128)(2,1)} %pad_maximum_fusion.3.refs_2_, ...), custom_call_target="tpu_custom_call" | custom-call | flops 14495514624 | bytes 14155776 | tf_op jit(solution)/shard_map/reduce_products_2/pallas_call | solution.py:284
  336.6 2.9 fusion.86
  339.5 5.0 convolution_convert_fusion.1
  345.6 27.9 %exchange_3.1 = bf16[4,256,384]{2,1,0:T(8,128)(2,1)} custom-call(bf16[4,256,384]{2,1,0:T(8,128)(2,1)} %pad_maximum_fusion.11.data_ref), custom_call_target="tpu_custom_call" | custom-call | bytes 12582912 | tf_op jit(solution)/shard_map/exchange_3/pallas_call | solution.py:51
  381.9 4.5 multiply_reduce_fusion.1
  386.4 4.7 multiply_convert_fusion.1
  394.6 3.3 reduce-scatter.12.cloned.1.call-done
  398.0 7.6 %multiply_reduce_fusion = (f32[6,512]{1,0:T(8,128)S(1)}, f32[6,512,1024]{2,1,0:T(8,128)S(1)}) fusion(f32[6,512,1024]{2,1,0:T(8,128)} %copy-done.1, f32[6,512]{1,0:T(8,128)S(1)} %log_add_fusion, bf16[512,6,64]{0,2,1:T(8,128)(2,1)} %slice.334, bf16[1024,6,64]{0,1,2:T(8,128)(2,1)} %copy-done.27), kind=kOutput, calls=%fused_computation.1 | convolution fusion | flops 412087296 | bytes 26370048 | tf_op jit(solution)/shard_map/qhe,khe->hqk/dot_general | solution.py:548
  405.6 6.3 %multiply_convert_fusion = bf16[6,512,1024]{2,1,0:T(8,128)(2,1)S(1)} fusion(f32[6,512,1024]{2,1,0:T(8,128)S(1)} %get-tuple-element.232, f32[6,512,1024]{2,1,0:T(8,128)} %copy-done.1, f32[6,512]{1,0:T(8,128)S(1)} %get-tuple-element.231, f32[6,512]{1,0:T(8,128)S(1)} %log_add_fusion), kind=kLoop, calls=%fused_computation | loop fusion | flops 12582912 | bytes 31481856 | tf_op jit(solution)/shard_map/convert_element_type | solution.py:553
  418.6 3.1 copy.162
  423.5 3.9 fusion.39
  427.4 6.2 %fusion.33 = bf16[1024,6,64]{0,2,1:T(8,128)(2,1)S(1)} fusion(f32[512,6,64]{0,2,1:T(8,128)S(1)} %fusion.39, bf16[512,6,64]{0,2,1:T(8,128)(2,1)S(1)} %copy-done.32, f32[6,512,1024]{2,1,0:T(8,128)} %copy-done.1, f32[6,512]{1,0:T(8,128)S(1)} %log_add_fusion), kind=kOutput, calls=%fused_computation.81 | convolution fusion | flops 409731072 | bytes 14561280 | tf_op jit(solution)/shard_map/hqk,qhe->khe/dot_general | solution.py:570
  436.3 3.5 multiply_reduce_fusion.3
  444.1 2.8 multiply_reduce_fusion.4
  450.2 3.3 add_convert_fusion
  457.9 2.7 copy.178
  462.1 25.6 %all-gather.11.cloned.1.call-done.refs_0_ = bf16[1024,2048]{1,0:T(8,128)(2,1)} async-done(((bf16[256,2048]{1,0:T(8,128)(2,1)}), bf16[1024,2048]{1,0:T(8,128)(2,1)}) %all-gather.11.cloned.1.call-update) | async-done | bytes 4194320 | tf_op jit(solution)/shard_map/all_gather | solution.py:537
  487.7 34.1 %reduce_products_5.1 = (f32[256,384]{1,0:T(8,128)}, f32[256,384]{1,0:T(8,128)}, f32[256,256]{1,0:T(8,128)}) custom-call(bf16[1024,2048]{1,0:T(8,128)(2,1)} %all-gather.11.cloned.1.call-done.refs_0_, bf16[1024,2048]{1,0:T(8,128)(2,1)} %copy-done.28, bf16[1024,384]{1,0:T(8,128)(2,1)} %copy.176.refs_2_, bf16[1024,384]{1,0:T(8,128)(2,1)} %copy-done.29, ...), custom_call_target="tpu_custom_call" | custom-call | flops 4294967296 | bytes 4194304 | tf_op jit(solution)/shard_map/reduce_products_5/pallas_call | solution.py:284
  523.4 9.6 %exchange_6.1 = bf16[4,64,256]{2,1,0:T(8,128)(2,1)} custom-call(bf16[4,64,256]{2,1,0:T(8,128)(2,1)} %bitcast.174), custom_call_target="tpu_custom_call" | custom-call | bytes 2097152 | tf_op jit(solution)/shard_map/exchange_6/pallas_call | solution.py:51
  537.4 30.0 %reduce-scatter.14.cloned.1.call-done = bf16[256,2048]{1,0:T(8,128)(2,1)} async-done(((bf16[1024,2048]{1,0:T(8,128)(2,1)}), bf16[256,2048]{1,0:T(8,128)(2,1)}) %reduce-scatter.14.cloned.1.call-update) | async-done | bytes 1048592 | tf_op jit(solution)/shard_map/reduce_scatter | solution.py:589
  571.2 12.1 %sum_everywhere_7.1 = f32[40,128]{1,0:T(8,128)} custom-call(f32[40,128]{1,0:T(8,128)} %pad_bitcast_fusion.data_ref), custom_call_target="tpu_custom_call" | custom-call | tf_op jit(solution)/shard_map/sum_everywhere_7/pallas_call | solution.py:121
  586.0 5.6 fusion.24
  (331 shorter events, 99.0 us)
Async XLA Ops:
  7.2 14.3 %copy-start = (bf16[2048,384]{1,0:T(8,128)(2,1)S(1)}, bf16[2048,384]{1,0:T(8,128)(2,1)}, u32[]{:S(2)}) copy-start(bf16[2048,384]{1,0:T(8,128)(2,1)} %param.30) | copy-start | bytes 4718596
  7.2 82.9 %all-gather.5.cloned.1.call-start = ((), (), s32[]{:S(2)}) async-start(), calls=%async_computation.5 | async-start | bytes 6488064 | tf_op jit(solution)/shard_map/all_gather | solution.py:419
  9.0 135.7 %all-gather.7.cloned.1.call-start = ((), (), s32[]{:S(2)}) async-start(), calls=%async_computation.6 | async-start | bytes 2621440 | tf_op jit(solution)/shard_map/all_gather | solution.py:484
  9.8 7.4 %copy-start.68 = (f32[2048]{0:T(1024)}, f32[2048]{0:T(1024)S(1)}, u32[]{:S(2)}) copy-start(f32[2048]{0:T(1024)S(1)} %convert_element_type.193) | copy-start | bytes 24580
  10.4 17.7 %copy-start.79 = (f32[64]{0:T(128)}, f32[64]{0:T(128)S(1)}, u32[]{:S(2)}) copy-start(f32[64]{0:T(128)S(1)} %convert_element_type.198) | copy-start | bytes 772
  11.1 17.0 %copy-start.76 = (f32[64]{0:T(128)}, f32[64]{0:T(128)S(1)}, u32[]{:S(2)}) copy-start(f32[64]{0:T(128)S(1)} %convert_element_type.200) | copy-start | bytes 772
  11.9 5.3 copy-start.71
  12.0 11.6 %copy-start.74 = (s32[6]{0:T(128)}, s32[6]{0:T(128)S(1)}, u32[]{:S(2)}) copy-start(s32[6]{0:T(128)S(1)} %fusion.73) | copy-start | bytes 76
  21.3 17.6 %copy-start.27 = (bf16[1024,6,64]{0,1,2:T(8,128)(2,1)}, bf16[1024,6,64]{0,1,2:T(8,128)(2,1)S(1)}, u32[]{:S(2)}) copy-start(bf16[1024,6,64]{0,1,2:T(8,128)(2,1)S(1)} %fusion.37) | copy-start | bytes 2359300
  21.3 16.3 %copy-start.45 = (bf16[512,6,64]{0,1,2:T(8,128)(2,1)}, bf16[512,6,64]{0,1,2:T(8,128)(2,1)S(1)}, u32[]{:S(2)}) copy-start(bf16[512,6,64]{0,1,2:T(8,128)(2,1)S(1)} %slice.370) | copy-start | bytes 1179652
  26.0 202.4 %copy-start.60 = (f32[1024,6]{0,1:T(8,128)}, f32[1024,6]{0,1:T(8,128)S(1)}, u32[]{:S(2)}) copy-start(f32[1024,6]{0,1:T(8,128)S(1)} %add_rsqrt_fusion.1) | copy-start | bytes 73732
  31.4 6.3 %copy-start.2 = (f32[6,512,512]{1,2,0:T(8,128)}, f32[6,512,512]{1,2,0:T(8,128)S(1)}, u32[]{:S(2)}) copy-start(f32[6,512,512]{1,2,0:T(8,128)S(1)} %get-tuple-element.226) | copy-start | bytes 18874372
  44.0 34.1 %copy-start.78 = (bf16[2048]{0:T(1024)(128)(2,1)S(1)}, bf16[2048]{0:T(1024)(128)(2,1)}, u32[]{:S(2)}) copy-start(bf16[2048]{0:T(1024)(128)(2,1)} %param.35) | copy-start | bytes 12292
  78.2 258.4 %copy-start.66 = (f32[2048]{0:T(1024)}, f32[2048]{0:T(1024)S(1)}, u32[]{:S(2)}) copy-start(f32[2048]{0:T(1024)S(1)} %convert_element_type.207) | copy-start | bytes 24580
  95.4 241.2 %copy-start.70 = (f32[256]{0:T(256)}, f32[256]{0:T(256)S(1)}, u32[]{:S(2)}) copy-start(f32[256]{0:T(256)S(1)} %add_rsqrt_fusion.4) | copy-start | bytes 3076
  97.1 94.2 %all-gather.9.cloned.1.call-start = ((), (), s32[]{:S(2)}) async-start(), calls=%async_computation.8 | async-start | bytes 2621440 | tf_op jit(solution)/shard_map/all_gather | solution.py:484
  97.7 11.1 %slice-start.9 = ((s8[4718592]{0:T(1024)(128)(4,1)}), s8[4194304]{0:T(1024)(128)(4,1)S(1)}, s32[]{:S(2)}) async-start(s8[4718592]{0:T(1024)(128)(4,1)} %bitcast.188), calls=%async_computation.23 | async-start | bytes 8388608
  100.5 8.2 %copy-start.11 = (bf16[4,1,128,2048]{3,2,1,0:T(8,128)(2,1)}, bf16[4,1,128,2048]{3,2,1,0:T(8,128)(2,1)S(1)}, u32[]{:S(2)}) copy-start(bf16[4,1,128,2048]{3,2,1,0:T(8,128)(2,1)S(1)} %get-tuple-element.173) | copy-start | bytes 6291460
  100.6 8.2 %copy-start.10 = (bf16[4,1,128,2048]{3,2,1,0:T(8,128)(2,1)}, bf16[4,1,128,2048]{3,2,1,0:T(8,128)(2,1)S(1)}, u32[]{:S(2)}) copy-start(bf16[4,1,128,2048]{3,2,1,0:T(8,128)(2,1)S(1)} %get-tuple-element.172) | copy-start | bytes 6291460
  100.6 8.2 %slice-start.10 = ((s8[4718592]{0:T(1024)(128)(4,1)}), s8[524288]{0:T(1024)(128)(4,1)S(1)}, s32[]{:S(2)}) async-start(s8[4718592]{0:T(1024)(128)(4,1)} %bitcast.188), calls=%async_computation.24 | async-start | bytes 1048576
  113.1 220.2 %reduce-scatter.8.cloned.1.call-start = ((), (), s32[]{:S(2)}) async-start(), calls=%async_computation.9 | async-start | bytes 2621440 | tf_op jit(solution)/shard_map/reduce_scatter | solution.py:507
  144.7 6.0 copy-start.41
  144.7 6.0 copy-start.85
  144.7 13.4 %slice-start.1 = ((s8[4718592]{0:T(1024)(128)(4,1)}), s8[4194304]{0:T(1024)(128)(4,1)S(1)}, s32[]{:S(2)}) async-start(s8[4718592]{0:T(1024)(128)(4,1)} %bitcast.180), calls=%async_computation.15 | async-start | bytes 8388608
  144.7 16.3 %slice-start.5 = ((s8[4718592]{0:T(1024)(128)(4,1)}), s8[4194304]{0:T(1024)(128)(4,1)S(1)}, s32[]{:S(2)}) async-start(s8[4718592]{0:T(1024)(128)(4,1)} %bitcast.184), calls=%async_computation.19 | async-start | bytes 8388608
  150.7 7.4 %slice-start.2 = ((s8[4718592]{0:T(1024)(128)(4,1)}), s8[524288]{0:T(1024)(128)(4,1)S(1)}, s32[]{:S(2)}) async-start(s8[4718592]{0:T(1024)(128)(4,1)} %bitcast.180), calls=%async_computation.16 | async-start | bytes 1048576
  150.7 10.3 %slice-start.6 = ((s8[4718592]{0:T(1024)(128)(4,1)}), s8[524288]{0:T(1024)(128)(4,1)S(1)}, s32[]{:S(2)}) async-start(s8[4718592]{0:T(1024)(128)(4,1)} %bitcast.184), calls=%async_computation.20 | async-start | bytes 1048576
  191.3 6.0 copy-start.43
  191.3 6.0 copy-start.84
  191.3 13.1 %slice-start.3 = ((s8[4718592]{0:T(1024)(128)(4,1)}), s8[4194304]{0:T(1024)(128)(4,1)S(1)}, s32[]{:S(2)}) async-start(s8[4718592]{0:T(1024)(128)(4,1)} %bitcast.182), calls=%async_computation.17 | async-start | bytes 8388608
  191.4 16.1 %slice-start.7 = ((s8[4718592]{0:T(1024)(128)(4,1)}), s8[4194304]{0:T(1024)(128)(4,1)S(1)}, s32[]{:S(2)}) async-start(s8[4718592]{0:T(1024)(128)(4,1)} %bitcast.186), calls=%async_computation.21 | async-start | bytes 8388608
  197.4 7.1 %slice-start.4 = ((s8[4718592]{0:T(1024)(128)(4,1)}), s8[524288]{0:T(1024)(128)(4,1)S(1)}, s32[]{:S(2)}) async-start(s8[4718592]{0:T(1024)(128)(4,1)} %bitcast.182), calls=%async_computation.18 | async-start | bytes 1048576
  197.4 10.1 %slice-start.8 = ((s8[4718592]{0:T(1024)(128)(4,1)}), s8[524288]{0:T(1024)(128)(4,1)S(1)}, s32[]{:S(2)}) async-start(s8[4718592]{0:T(1024)(128)(4,1)} %bitcast.186), calls=%async_computation.22 | async-start | bytes 1048576
  211.6 121.7 %reduce-scatter.6.cloned.1.call-start = ((), (), s32[]{:S(2)}) async-start(), calls=%async_computation.7 | async-start | bytes 2621440 | tf_op jit(solution)/shard_map/reduce_scatter | solution.py:507
  212.2 182.4 %reduce-scatter.10.cloned.1.call-start = ((), (), s32[]{:S(2)}) async-start(), calls=%async_computation.10 | async-start | bytes 2621440 | tf_op jit(solution)/shard_map/reduce_scatter | solution.py:515
  226.6 171.3 %reduce-scatter.12.cloned.1.call-start = ((), (), s32[]{:S(2)}) async-start(), calls=%async_computation.11 | async-start | bytes 2621440 | tf_op jit(solution)/shard_map/reduce_scatter | solution.py:515
  245.8 241.9 %all-gather.11.cloned.1.call-start = ((), (), s32[]{:S(2)}) async-start(), calls=%async_computation.13 | async-start | bytes 5242880 | tf_op jit(solution)/shard_map/all_gather | solution.py:537
  377.8 8.6 %copy-start.30 = (bf16[512,6,64]{0,2,1:T(8,128)(2,1)}, bf16[512,6,64]{0,2,1:T(8,128)(2,1)S(1)}, u32[]{:S(2)}) copy-start(bf16[512,6,64]{0,2,1:T(8,128)(2,1)S(1)} %slice.332) | copy-start | bytes 1179652
  397.9 169.5 %reduce-scatter.14.cloned.1.call-start = ((), (), s32[]{:S(2)}) async-start(), calls=%async_computation.12 | async-start | bytes 5242880 | tf_op jit(solution)/shard_map/reduce_scatter | solution.py:589
  405.6 6.3 %copy-start.19 = (bf16[1024,6,32]{0,2,1:T(8,128)(2,1)S(1)}, bf16[1024,6,32]{0,2,1:T(8,128)(2,1)}, u32[]{:S(2)}) copy-start(bf16[1024,6,32]{0,2,1:T(8,128)(2,1)} %copy-done.17) | copy-start | bytes 1179652
  405.6 6.3 %copy-start.34 = (f32[512,6,64]{0,2,1:T(8,128)S(1)}, f32[512,6,64]{0,2,1:T(8,128)}, u32[]{:S(2)}) copy-start(f32[512,6,64]{0,2,1:T(8,128)} %fusion.42) | copy-start | bytes 2359300
  427.4 6.2 %copy-start.75 = (s32[6]{0:T(128)S(1)}, s32[6]{0:T(128)}, u32[]{:S(2)}) copy-start(s32[6]{0:T(128)} %copy-done.74) | copy-start | bytes 76
  521.8 45.6 %copy-start.69 = (f32[2048]{0:T(1024)S(1)}, f32[2048]{0:T(1024)}, u32[]{:S(2)}) copy-start(f32[2048]{0:T(1024)} %copy-done.68) | copy-start | bytes 24580
  533.1 52.9 %copy-start.9 = (bf16[256,2048]{1,0:T(8,128)(2,1)S(1)}, bf16[256,2048]{1,0:T(8,128)(2,1)}, u32[]{:S(2)}) copy-start(bf16[256,2048]{1,0:T(8,128)(2,1)} %copy-done.8) | copy-start | bytes 3145732
  533.1 52.9 %copy-start.62 = (bf16[128,2048]{1,0:T(8,128)(2,1)S(1)}, bf16[128,2048]{1,0:T(8,128)(2,1)}, u32[]{:S(2)}) copy-start(bf16[128,2048]{1,0:T(8,128)(2,1)} %reduce-scatter.10.cloned.1.call-done) | copy-start | bytes 1572868
  533.1 52.9 %copy-start.67 = (f32[2048]{0:T(1024)S(1)}, f32[2048]{0:T(1024)}, u32[]{:S(2)}) copy-start(f32[2048]{0:T(1024)} %copy-done.66) | copy-start | bytes 24580
  586.0 5.7 copy-start.64
  586.0 6.4 %copy-start.49 = (f32[256,1152]{1,0:T(8,128)S(1)}, f32[256,1152]{1,0:T(8,128)}, u32[]{:S(2)}) copy-start(f32[256,1152]{1,0:T(8,128)} %get-tuple-element.256) | copy-start | bytes 3538948
  (58 other events, 153.6 us)
Sparse Core Ops, SparseCore 0:
  11.4 78.6 all-gather.4
  97.2 47.4 all-gather.6
  146.8 44.4 all-gather.8
  211.7 42.4 reduce-scatter.7
  256.3 42.8 reduce-scatter.5
  301.3 42.8 reduce-scatter.9
  346.5 51.3 reduce-scatter.11
  400.0 87.6 all-gather.10
  490.0 77.3 reduce-scatter.13
